TPU v7x, 256 devices: a whole 4x4x8 slice. The times are simulated.
256 devices in a mesh: dp: 16 (over z_lo, y, core), mp: 16 (over z_hi, x).
Axes of the slice: x: 4, y: 4, z: 8 (z_hi: 4, z_lo: 2; z = z_hi * 2 + z_lo), core: 2. Of those that a mesh axis runs over, the one named last changes fastest.
Arguments:
- tokens: bfloat16 [4096, 1024], P('dp'), may hold values from -6 to 6
- lengths: int32 [16], P('dp'), may hold values from 64 to 256
- cotangent: bfloat16 [4096, 1024], P('dp'), may hold values from -6 to 6
- triple_weight: bfloat16 [2, 1024, 3, 1024], P(None, None, None, 'mp'), may hold values from -0.1875 to 0.1875
- output_weight: bfloat16 [2, 1024, 1024], P(None, None, 'mp'), may hold values from -0.1875 to 0.1875
- upward_weight: bfloat16 [2, 1024, 4096], P(None, None, 'mp'), may hold values from -0.1875 to 0.1875
- downward_weight: bfloat16 [2, 1024, 4096], P(None, None, 'mp'), may hold values from -0.09375 to 0.09375
Outputs:
- final_stream: bfloat16 [4096, 1024], P('dp')
- triple_grad: float32 [2, 1024, 3, 1024], P(None, 'dp', None, 'mp')
- output_grad: float32 [2, 1024, 1024], P(None, 'dp', 'mp')
- upward_grad: float32 [2, 1024, 4096], P(None, 'dp', 'mp')
- downward_grad: float32 [2, 1024, 4096], P(None, 'dp', 'mp')
Inputs may be any that keep to these rules, and one draw needn't show every extreme that they name: lengths[s] counts the live candidates of slate s; its other positions are padding.
All inputs are finite; a program needn't handle non-finite values.
Results may differ from a plain program's by a relative error of at most 0.04.
Values may be sent and summed in bfloat16 or wider, within the bound.
No kernel may reach another device: no remote copies, remote signals or barrier semaphores. Data moves between devices by JAX's collectives and lax.ppermute only.
A program may use at most 64 MiB of HBM per device.

v0:
```python
import math

import jax
import jax.numpy as jnp
from jax import lax
from jax.sharding import Mesh
from jax.sharding import PartitionSpec as P

HD = 64
SLATE = 256
LAYERS = 2
DP = ("dp_0", "dp_1", "dp_2")


epsilon = 1e-06


def sent_together(arrays, axis, dim, along):
    both = jnp.concatenate(arrays, axis=along)
    result, at, done = (lax.all_gather(both, axis, axis=dim, tiled=True), 0, [])
    for a in arrays:
        done.append(lax.slice_in_dim(result, at, at + a.shape[along], axis=along))
        at += a.shape[along]
    return tuple(done)


def in_blocks(x, dim, devices):
    lengths = x.shape
    blocks = x.reshape(*lengths[:dim], devices, lengths[dim] // devices, *lengths[dim + 1 :])
    return jnp.moveaxis(blocks, dim, 0)


def sent_and_summed(x, axis, dim):
    devices = lax.axis_size(axis)
    blocks = lax.all_to_all(in_blocks(x, dim, devices), axis, 0, 0, tiled=True)
    return jnp.sum(blocks.astype(jnp.float32), axis=0)


def from_everyone(x, axis):
    copies = jnp.broadcast_to(x, (lax.axis_size(axis), *x.shape))
    return lax.all_to_all(copies, axis, split_axis=0, concat_axis=0, tiled=True)


def in_order(blocks, dim):
    blocks = jnp.moveaxis(blocks, 0, dim)
    lengths = blocks.shape
    return blocks.reshape(*lengths[:dim], lengths[dim] * lengths[dim + 1], *lengths[dim + 2 :])


def gathered_copies(x, axis, dim):
    blocks = from_everyone(x, axis)
    return in_order(blocks, dim)


def rows_for(lines, devices):
    spare = -len(lines) % devices
    return jnp.pad(lines, [(0, spare)] + [(0, 0)] * (lines.ndim - 1))


def sum_by_parts(x, axes):
    lines = x.reshape(-1, x.shape[-1])
    own = sent_and_summed(rows_for(lines, lax.axis_size(axes)), axes, 0)
    whole = gathered_copies(own.astype(jnp.bfloat16), axes, 0)
    return whole[: len(lines)].reshape(x.shape).astype(jnp.float32)


def sum_by_axis(x, axes, dim):
    far, near = axes
    blocks = in_blocks(x, dim, lax.axis_size(far))
    nearer = sent_and_summed(blocks, near, dim + 1)
    arrived = lax.all_to_all(
        nearer.astype(jnp.bfloat16), far, split_axis=0, concat_axis=0, tiled=True
    )
    return arrived.astype(jnp.float32).sum(axis=0)


def side_by_side(arrays, axis, dim, along):
    widths = [math.prod(a.shape[along:]) for a in arrays]
    both = jnp.concatenate(
        [a.reshape(*a.shape[:along], w) for a, w in zip(arrays, widths)], axis=along
    )
    result = sum_by_axis(both, axis, dim)
    blocks = jnp.split(result, [sum(widths[:k]) for k in range(1, len(widths))], axis=along)
    return tuple(
        (b.reshape(*result.shape[:along], *a.shape[along:]) for a, b in zip(arrays, blocks))
    )


def normalize(stream):
    widened = stream.astype(jnp.float32)
    rscale = lax.rsqrt(jnp.mean(widened * widened, axis=-1, keepdims=True) + epsilon)
    scaled = widened * rscale
    return (scaled.astype(jnp.bfloat16), scaled, rscale)


def norm_backward(scaled, rscale, upward):
    inner = jnp.mean(upward * scaled, axis=-1, keepdims=True)
    return rscale * (upward - scaled * inner)


def smooth_gate(preact):
    return jax.nn.gelu(preact, approximate=True)


def attend(queries, key_rows, values, lengths):
    live_keys = (jnp.arange(SLATE)[None, :] < lengths[:, None]).astype(jnp.float32)
    scores = jnp.einsum(
        "bqhe,bkhe->bhqk", queries, key_rows, preferred_element_type=jnp.float32
    ) * HD ** (-0.5)
    weights = jnp.exp(scores) * live_keys[:, None, None, :]
    probs = weights / jnp.sum(weights, axis=-1, keepdims=True)
    probs_low = probs.astype(jnp.bfloat16)
    context = jnp.einsum(
        "bhqk,bkhe->bqhe", probs_low, values, preferred_element_type=jnp.float32
    ).astype(jnp.bfloat16)
    return (probs, probs_low, context)


def attend_backward(probs, probs_low, queries, key_rows, values, grad_context):
    grad_prob = jnp.einsum(
        "bqhe,bkhe->bhqk", grad_context, values, preferred_element_type=jnp.float32
    )
    grad_value = jnp.einsum(
        "bhqk,bqhe->bkhe", probs_low, grad_context, preferred_element_type=jnp.float32
    ).astype(jnp.bfloat16)
    inner = jnp.sum(grad_prob * probs, axis=-1, keepdims=True)
    grad_score = (probs * (grad_prob - inner) * HD ** (-0.5)).astype(jnp.bfloat16)
    grad_query = jnp.einsum(
        "bhqk,bkhe->bqhe", grad_score, key_rows, preferred_element_type=jnp.float32
    ).astype(jnp.bfloat16)
    grad_key = jnp.einsum(
        "bhqk,bqhe->bkhe", grad_score, queries, preferred_element_type=jnp.float32
    ).astype(jnp.bfloat16)
    return (grad_query, grad_key, grad_value)


def contract_rows(left, right):
    return lax.dot_general(
        left, right, (((0,), (0,)), ((), ())), preferred_element_type=jnp.float32
    )


def contract_cols(left, right):
    return lax.dot_general(
        left, right, (((1,), (1,)), ((), ())), preferred_element_type=jnp.float32
    )


def spread(stream_part):
    normed_part = normalize(stream_part)[0]
    return sent_together((stream_part, normed_part), "mp", 0, 1)


def body(tokens, lengths, cotangent, triple_weight, output_weight, upward_weight, downward_weight):
    row_count = tokens.shape[0]
    slates = row_count // SLATE
    model_width = tokens.shape[1]
    heads_here = triple_weight.shape[-1] // HD
    row_share = row_count // lax.axis_size("mp")
    row_start = lax.axis_index("mp") * row_share
    stream = tokens
    stream_part = lax.dynamic_slice_in_dim(tokens, row_start, row_share, 0)
    normed, scaled, rscale = normalize(tokens)
    final_stream = tokens
    saved = []
    for layer_index in range(LAYERS):
        flat_triple = triple_weight[layer_index].reshape(model_width, -1)
        qkv = jnp.dot(normed, flat_triple, preferred_element_type=jnp.float32).astype(jnp.bfloat16)
        shaped = qkv.reshape(slates, SLATE, 3, heads_here, HD)
        queries = shaped[:, :, 0]
        key_rows = shaped[:, :, 1]
        values = shaped[:, :, 2]
        probs, probs_low, context = attend(queries, key_rows, values, lengths)
        context_flat = context.reshape(row_count, -1)
        partial_att = contract_cols(context_flat, output_weight[layer_index])
        attn_part = sent_and_summed(partial_att.astype(jnp.bfloat16), "mp", 0)
        mid_part = (stream_part.astype(jnp.float32) + attn_part).astype(jnp.bfloat16)
        mid_stream, normed_mid = spread(mid_part)
        _, scaled_mid, rscale_mid = normalize(mid_stream)
        preact = jnp.dot(normed_mid, upward_weight[layer_index], preferred_element_type=jnp.float32)
        activated = smooth_gate(preact).astype(jnp.bfloat16)
        partial_ffn = contract_cols(activated, downward_weight[layer_index])
        saved.append(
            (
                normed,
                scaled,
                rscale,
                queries,
                key_rows,
                values,
                probs,
                probs_low,
                context_flat,
                scaled_mid,
                rscale_mid,
                normed_mid,
                preact,
                activated,
            )
        )
        ffn_part = sent_and_summed(partial_ffn.astype(jnp.bfloat16), "mp", 0)
        out_part = (mid_part.astype(jnp.float32) + ffn_part).astype(jnp.bfloat16)
        if layer_index + 1 < LAYERS:
            stream, normed = spread(out_part)
            _, scaled, rscale = normalize(stream)
            stream_part = out_part
        else:
            final_stream = gathered_copies(out_part, "mp", 0)
    gradients = []
    upstream = cotangent
    for layer_index in reversed(range(LAYERS)):
        (
            normed,
            scaled,
            rscale,
            queries,
            key_rows,
            values,
            probs,
            probs_low,
            context_flat,
            scaled_mid,
            rscale_mid,
            normed_mid,
            preact,
            activated,
        ) = saved[layer_index]
        downward_grad = contract_rows(upstream, activated)
        grad_act = jnp.dot(
            upstream, downward_weight[layer_index], preferred_element_type=jnp.float32
        ).astype(jnp.bfloat16)
        _, gate_back = jax.vjp(smooth_gate, preact)
        grad_preact = gate_back(grad_act.astype(jnp.float32))[0].astype(jnp.bfloat16)
        upward_grad = contract_rows(normed_mid, grad_preact)
        grad_normed = sum_by_parts(
            contract_cols(grad_preact, upward_weight[layer_index]).astype(jnp.bfloat16), "mp"
        )
        grad_mid = (
            upstream.astype(jnp.float32) + norm_backward(scaled_mid, rscale_mid, grad_normed)
        ).astype(jnp.bfloat16)
        output_grad = contract_rows(grad_mid, context_flat)
        grad_context = jnp.dot(
            grad_mid, output_weight[layer_index], preferred_element_type=jnp.float32
        ).astype(jnp.bfloat16)
        grad_query, grad_key, grad_value = attend_backward(
            probs,
            probs_low,
            queries,
            key_rows,
            values,
            grad_context.reshape(slates, SLATE, heads_here, HD),
        )
        grad_qkv = jnp.stack([grad_query, grad_key, grad_value], axis=2).reshape(row_count, -1)
        triple_grad = contract_rows(normed, grad_qkv).reshape(model_width, 3, -1)
        pieces = (triple_grad, output_grad, upward_grad, downward_grad)
        gradients.insert(0, pieces)
        if layer_index > 0:
            flat_triple = triple_weight[layer_index].reshape(model_width, -1)
            grad_input = sum_by_parts(
                contract_cols(grad_qkv, flat_triple).astype(jnp.bfloat16), "mp"
            )
            upstream = (
                grad_mid.astype(jnp.float32) + norm_backward(scaled, rscale, grad_input)
            ).astype(jnp.bfloat16)
    stacked = tuple(
        (
            jnp.stack([gradients[layer_pos][slot_index] for layer_pos in range(LAYERS)])
            for slot_index in range(4)
        )
    )
    merged = side_by_side(
        (
            stacked[0].astype(jnp.bfloat16),
            stacked[1].astype(jnp.bfloat16),
            stacked[2].astype(jnp.bfloat16),
            stacked[3].astype(jnp.bfloat16),
        ),
        (("dp_0", "dp_1"), "dp_2"),
        1,
        2,
    )
    return (final_stream, merged[0], merged[1], merged[2], merged[3])


def solution(mesh):
    torus = Mesh(mesh.devices.reshape(2, 4, 2, mesh.shape["mp"]), ("dp_0", "dp_1", "dp_2", "mp"))
    placed = (
        P(DP, None),
        P(DP),
        P(DP, None),
        P(None, None, None, "mp"),
        P(None, None, "mp"),
        P(None, None, "mp"),
        P(None, None, "mp"),
    )
    return jax.shard_map(
        body,
        mesh=torus,
        in_specs=placed,
        out_specs=(
            P(DP, None),
            P(None, DP, None, "mp"),
            P(None, DP, "mp"),
            P(None, DP, "mp"),
            P(None, DP, "mp"),
        ),
        check_vma=False,
    )
```

profile of v0, /device:TPU:1, one launch (start us, length us, event | category | flops | bytes accessed | tf_op | source)
XLA Modules:
  0.0 476.7 jit_solution(4142258701075386937)
XLA Ops:
  13.4 11.6 %all-to-all-start = ((bf16[16,16,1024]{2,1,0:T(8,128)(2,1)}), bf16[16,16,1024]{2,1,0:T(8,128)(2,1)S(1)}, u32[]{:S(2)}, u32[]{:S(2)}) async-start(bf16[16,16,1024]{2,1,0:T(8,128)(2,1)} %bitcast.10), calls=%async_computation | async-start | bytes 1048576 | tf_op jit(solution)/shard_map/all_to_all | solution.py:35
  25.1 14.8 %all-to-all-done = bf16[16,16,1024]{2,1,0:T(8,128)(2,1)S(1)} async-done(((bf16[16,16,1024]{2,1,0:T(8,128)(2,1)}), bf16[16,16,1024]{2,1,0:T(8,128)(2,1)S(1)}, u32[]{:S(2)}, u32[]{:S(2)}) %all-to-all-start) | async-done | bytes 524320 | tf_op jit(solution)/shard_map/all_to_all | solution.py:35
  41.7 51.4 %all-gather.4.cloned.1.call-done = bf16[256,2048]{1,0:T(8,128)(2,1)} async-done(((bf16[16,2048]{1,0:T(8,128)(2,1)}), bf16[256,2048]{1,0:T(8,128)(2,1)}) %all-gather.4.cloned.1.call-update) | async-done | bytes 1048592 | tf_op jit(solution)/shard_map/all_gather | solution.py:20
  96.0 16.3 %all_to_all.65 = bf16[16,16,1024]{2,1,0:T(8,128)(2,1)S(1)} all-to-all(bf16[16,16,1024]{2,1,0:T(8,128)(2,1)S(1)} %bitcast.242), channel_id=1, replica_groups=mesh['dp_0'=2,'dp_1'=4,'dp_2'=2,'mp'=16] {'mp'}, dimensions={0} | all-to-all | bytes 1048576 | tf_op jit(solution)/shard_map/all_to_all | solution.py:35
  113.2 54.8 %all-gather.6.cloned.1.call-done = bf16[256,2048]{1,0:T(8,128)(2,1)} async-done(((bf16[16,2048]{1,0:T(8,128)(2,1)}), bf16[256,2048]{1,0:T(8,128)(2,1)}) %all-gather.6.cloned.1.call-update) | async-done | bytes 1048592 | tf_op jit(solution)/shard_map/all_gather | solution.py:20
  170.5 16.3 %all_to_all.66 = bf16[16,16,1024]{2,1,0:T(8,128)(2,1)S(1)} all-to-all(bf16[16,16,1024]{2,1,0:T(8,128)(2,1)S(1)} %bitcast.233), channel_id=1, replica_groups=mesh['dp_0'=2,'dp_1'=4,'dp_2'=2,'mp'=16] {'mp'}, dimensions={0} | all-to-all | bytes 1048576 | tf_op jit(solution)/shard_map/all_to_all | solution.py:35
  187.7 54.9 %all-gather.8.cloned.1.call-done = bf16[256,2048]{1,0:T(8,128)(2,1)} async-done(((bf16[16,2048]{1,0:T(8,128)(2,1)}), bf16[256,2048]{1,0:T(8,128)(2,1)}) %all-gather.8.cloned.1.call-update) | async-done | bytes 1048592 | tf_op jit(solution)/shard_map/all_gather | solution.py:20
  247.5 16.3 %all_to_all.67 = bf16[16,16,1024]{2,1,0:T(8,128)(2,1)S(1)} all-to-all(bf16[16,16,1024]{2,1,0:T(8,128)(2,1)S(1)} %bitcast.234), channel_id=1, replica_groups=mesh['dp_0'=2,'dp_1'=4,'dp_2'=2,'mp'=16] {'mp'}, dimensions={0} | all-to-all | bytes 1048576 | tf_op jit(solution)/shard_map/all_to_all | solution.py:35
  264.7 6.4 %all-to-all-start.6 = ((bf16[16,16,1024]{2,1,0:T(8,128)(2,1)}), bf16[16,16,1024]{2,1,0:T(8,128)(2,1)S(1)}, u32[]{:S(2)}, u32[]{:S(2)}) async-start(bf16[16,16,1024]{2,1,0:T(8,128)(2,1)} %broadcast_in_dim.9), calls=%async_computation.6 | async-start | bytes 1048576 | tf_op jit(solution)/shard_map/all_to_all | solution.py:41
  271.3 11.3 %all-to-all-done.6 = bf16[16,16,1024]{2,1,0:T(8,128)(2,1)S(1)} async-done(((bf16[16,16,1024]{2,1,0:T(8,128)(2,1)}), bf16[16,16,1024]{2,1,0:T(8,128)(2,1)S(1)}, u32[]{:S(2)}, u32[]{:S(2)}) %all-to-all-start.6) | async-done | bytes 524320 | tf_op jit(solution)/shard_map/all_to_all | solution.py:41
  287.7 15.6 %all_to_all.68 = bf16[16,16,1024]{2,1,0:T(8,128)(2,1)S(1)} all-to-all(bf16[16,16,1024]{2,1,0:T(8,128)(2,1)S(1)} %bitcast.232), channel_id=1, replica_groups=mesh['dp_0'=2,'dp_1'=4,'dp_2'=2,'mp'=16] {'mp'}, dimensions={0} | all-to-all | bytes 1048576 | tf_op jit(solution)/shard_map/all_to_all | solution.py:35
  304.2 3.7 all-to-all-start.8
  314.6 5.4 %all-to-all-done.8 = bf16[16,16,1024]{2,1,0:T(8,128)(2,1)S(1)} async-done(((bf16[16,16,1024]{2,1,0:T(8,128)(2,1)}), bf16[16,16,1024]{2,1,0:T(8,128)(2,1)S(1)}, u32[]{:S(2)}, u32[]{:S(2)}) %all-to-all-start.8) | async-done | bytes 524320 | tf_op jit(solution)/shard_map/all_to_all | solution.py:41
  320.0 4.2 all-to-all-start.3
  327.3 12.1 %all-to-all-done.3 = bf16[16,16,1024]{2,1,0:T(8,128)(2,1)} async-done(((bf16[16,16,1024]{2,1,0:T(8,128)(2,1)}), bf16[16,16,1024]{2,1,0:T(8,128)(2,1)}, u32[]{:S(2)}, u32[]{:S(2)}) %all-to-all-start.3) | async-done | bytes 524320 | tf_op jit(solution)/shard_map/all_to_all | solution.py:35
  339.4 4.2 all-to-all-start.9
  357.5 6.5 %all-to-all-start.10 = ((bf16[16,16,1024]{2,1,0:T(8,128)(2,1)}), bf16[16,16,1024]{2,1,0:T(8,128)(2,1)S(1)}, u32[]{:S(2)}, u32[]{:S(2)}) async-start(bf16[16,16,1024]{2,1,0:T(8,128)(2,1)} %broadcast_in_dim.11), calls=%async_computation.10 | async-start | bytes 1048576 | tf_op jit(solution)/shard_map/all_to_all | solution.py:41
  373.2 2.5 all-to-all-done.10
  383.5 31.6 %all_to_all.69 = bf16[2,8,2,64,768]{4,3,1,2,0:T(8,128)(2,1)S(1)} all-to-all(bf16[2,8,2,64,768]{4,3,1,2,0:T(8,128)(2,1)S(1)} %copy.68), channel_id=1, replica_groups=mesh['dp_0'=2,'dp_1'=4,'dp_2'=2,'mp'=16] {'dp_2'}, dimensions={0} | all-to-all | bytes 6291456 | tf_op jit(solution)/shard_map/all_to_all | solution.py:35
  416.0 5.7 %all-to-all-start.4 = ((bf16[16,16,1024]{2,1,0:T(8,128)(2,1)}), bf16[16,16,1024]{2,1,0:T(8,128)(2,1)}, u32[]{:S(2)}, u32[]{:S(2)}) async-start(bf16[16,16,1024]{2,1,0:T(8,128)(2,1)} %broadcast_in_dim.8), calls=%async_computation.4 | async-start | bytes 1048576 | tf_op jit(solution)/shard_map/all_to_all | solution.py:41
  423.9 2.7 copy.70
  426.6 9.3 %all-to-all-done.4 = bf16[16,16,1024]{2,1,0:T(8,128)(2,1)} async-done(((bf16[16,16,1024]{2,1,0:T(8,128)(2,1)}), bf16[16,16,1024]{2,1,0:T(8,128)(2,1)}, u32[]{:S(2)}, u32[]{:S(2)}) %all-to-all-start.4) | async-done | bytes 524320 | tf_op jit(solution)/shard_map/all_to_all | solution.py:41
  435.9 9.2 %all-to-all-start.12 = ((bf16[8,2,64,768]{3,2,1,0:T(8,128)(2,1)}), bf16[8,2,64,768]{3,2,1,0:T(8,128)(2,1)S(1)}, u32[]{:S(2)}, u32[]{:S(2)}) async-start(bf16[8,2,64,768]{3,2,1,0:T(8,128)(2,1)} %copy.70), calls=%async_computation.12 | async-start | bytes 3145728 | tf_op jit(solution)/shard_map/all_to_all | solution.py:71
  445.1 20.6 %all-to-all-done.12 = bf16[8,2,64,768]{3,2,1,0:T(8,128)(2,1)S(1)} async-done(((bf16[8,2,64,768]{3,2,1,0:T(8,128)(2,1)}), bf16[8,2,64,768]{3,2,1,0:T(8,128)(2,1)S(1)}, u32[]{:S(2)}, u32[]{:S(2)}) %all-to-all-start.12) | async-done | bytes 1572896 | tf_op jit(solution)/shard_map/all_to_all | solution.py:71
  (174 shorter events, 74.2 us)
Async XLA Ops:
  9.1 84.0 %copy-start.11 = (bf16[2,1024,256]{2,1,0:T(8,128)(2,1)S(1)}, bf16[2,1024,256]{2,1,0:T(8,128)(2,1)}, u32[]{:S(2)}) copy-start(bf16[2,1024,256]{2,1,0:T(8,128)(2,1)} %param.12) | copy-start | bytes 3145732
  11.9 81.2 %copy-start.25 = (bf16[256,192]{0,1:T(8,128)(2,1)}, bf16[256,192]{0,1:T(8,128)(2,1)S(1)}, u32[]{:S(2)}) copy-start(bf16[256,192]{0,1:T(8,128)(2,1)S(1)} %convolution_convert_fusion.18) | copy-start | bytes 294916
  12.3 80.8 %copy-start.24 = (bf16[64,256]{1,0:T(8,128)(2,1)}, bf16[64,256]{1,0:T(8,128)(2,1)S(1)}, u32[]{:S(2)}) copy-start(bf16[64,256]{1,0:T(8,128)(2,1)S(1)} %convolution_convert_fusion.28) | copy-start | bytes 98308
  13.4 26.5 %all-to-all-start = ((bf16[16,16,1024]{2,1,0:T(8,128)(2,1)}), bf16[16,16,1024]{2,1,0:T(8,128)(2,1)S(1)}, u32[]{:S(2)}, u32[]{:S(2)}) async-start(bf16[16,16,1024]{2,1,0:T(8,128)(2,1)} %bitcast.10), calls=%async_computation | async-start | bytes 1048576 | tf_op jit(solution)/shard_map/all_to_all | solution.py:35
  25.0 68.1 %all-gather.4.cloned.1.call-start = ((), (), s32[]{:S(2)}) async-start(), calls=%async_computation.13 | async-start | bytes 1114112 | tf_op jit(solution)/shard_map/all_gather | solution.py:20
  41.6 126.4 %all-gather.6.cloned.1.call-start = ((), (), s32[]{:S(2)}) async-start(), calls=%async_computation.14 | async-start | bytes 1114112 | tf_op jit(solution)/shard_map/all_gather | solution.py:20
  113.2 129.4 %all-gather.8.cloned.1.call-start = ((), (), s32[]{:S(2)}) async-start(), calls=%async_computation.15 | async-start | bytes 1114112 | tf_op jit(solution)/shard_map/all_gather | solution.py:20
  168.0 76.6 %copy-start.6 = (bf16[256,1024]{1,0:T(8,128)(2,1)S(1)}, bf16[256,1024]{1,0:T(8,128)(2,1)}, u32[]{:S(2)}) copy-start(bf16[256,1024]{1,0:T(8,128)(2,1)} %param.9) | copy-start | bytes 1572868
  169.5 17.2 %copy-start.27 = (bf16[256,192]{0,1:T(8,128)(2,1)}, bf16[256,192]{0,1:T(8,128)(2,1)S(1)}, u32[]{:S(2)}) copy-start(bf16[256,192]{0,1:T(8,128)(2,1)S(1)} %convolution_convert_fusion.17) | copy-start | bytes 294916
  244.6 26.5 %copy-start.2 = (bf16[256,2048]{1,0:T(8,128)(2,1)S(1)}, bf16[256,2048]{1,0:T(8,128)(2,1)}, u32[]{:S(2)}) copy-start(bf16[256,2048]{1,0:T(8,128)(2,1)} %all-gather.8.cloned.1.call-done) | copy-start | bytes 3145732
  264.7 17.9 %all-to-all-start.6 = ((bf16[16,16,1024]{2,1,0:T(8,128)(2,1)}), bf16[16,16,1024]{2,1,0:T(8,128)(2,1)S(1)}, u32[]{:S(2)}, u32[]{:S(2)}) async-start(bf16[16,16,1024]{2,1,0:T(8,128)(2,1)} %broadcast_in_dim.9), calls=%async_computation.6 | async-start | bytes 1048576 | tf_op jit(solution)/shard_map/all_to_all | solution.py:41
  287.3 24.7 %copy-start.15 = (bf16[1,256,3,1,64]{1,4,3,2,0:T(8,128)(2,1)}, bf16[1,256,3,1,64]{1,4,3,2,0:T(8,128)(2,1)S(1)}, u32[]{:S(2)}) copy-start(bf16[1,256,3,1,64]{1,4,3,2,0:T(8,128)(2,1)S(1)} %pad_maximum_fusion.2) | copy-start | bytes 294916
  287.3 24.7 %copy-start.1 = (bf16[256,2048]{1,0:T(8,128)(2,1)S(1)}, bf16[256,2048]{1,0:T(8,128)(2,1)}, u32[]{:S(2)}) copy-start(bf16[256,2048]{1,0:T(8,128)(2,1)} %all-gather.4.cloned.1.call-done) | copy-start | bytes 3145732
  287.7 24.5 %copy-start = (bf16[256,2048]{1,0:T(8,128)(2,1)S(1)}, bf16[256,2048]{1,0:T(8,128)(2,1)}, u32[]{:S(2)}) copy-start(bf16[256,2048]{1,0:T(8,128)(2,1)} %all-gather.6.cloned.1.call-done) | copy-start | bytes 3145732
  304.2 15.8 %all-to-all-start.8 = ((bf16[16,16,1024]{2,1,0:T(8,128)(2,1)}), bf16[16,16,1024]{2,1,0:T(8,128)(2,1)S(1)}, u32[]{:S(2)}, u32[]{:S(2)}) async-start(bf16[16,16,1024]{2,1,0:T(8,128)(2,1)} %broadcast_in_dim.10), calls=%async_computation.8 | async-start | bytes 1048576 | tf_op jit(solution)/shard_map/all_to_all | solution.py:41
  320.0 19.4 %all-to-all-start.3 = ((bf16[16,16,1024]{2,1,0:T(8,128)(2,1)}), bf16[16,16,1024]{2,1,0:T(8,128)(2,1)}, u32[]{:S(2)}, u32[]{:S(2)}) async-start(bf16[16,16,1024]{2,1,0:T(8,128)(2,1)} %bitcast.241), calls=%async_computation.3 | async-start | bytes 1048576 | tf_op jit(solution)/shard_map/all_to_all | solution.py:35
  325.8 20.8 %copy-start.7 = (bf16[256,1024]{1,0:T(8,128)(2,1)S(1)}, bf16[256,1024]{1,0:T(8,128)(2,1)}, u32[]{:S(2)}) copy-start(bf16[256,1024]{1,0:T(8,128)(2,1)} %param.9) | copy-start | bytes 1572868
  326.2 24.6 %copy-start.22 = (bf16[256,256]{1,0:T(8,128)(2,1)}, bf16[256,256]{1,0:T(8,128)(2,1)S(1)}, u32[]{:S(2)}) copy-start(bf16[256,256]{1,0:T(8,128)(2,1)S(1)} %fusion.66) | copy-start | bytes 393220
  339.4 16.2 %all-to-all-start.9 = ((bf16[16,16,1024]{2,1,0:T(8,128)(2,1)}), bf16[16,16,1024]{2,1,0:T(8,128)(2,1)}, u32[]{:S(2)}, u32[]{:S(2)}) async-start(bf16[16,16,1024]{2,1,0:T(8,128)(2,1)} %bitcast.229), calls=%async_computation.9 | async-start | bytes 1048576 | tf_op jit(solution)/shard_map/all_to_all | solution.py:35
  353.1 18.0 %copy-start.5 = (bf16[256,1024]{1,0:T(8,128)(2,1)S(1)}, bf16[256,1024]{1,0:T(8,128)(2,1)}, u32[]{:S(2)}) copy-start(bf16[256,1024]{1,0:T(8,128)(2,1)} %copy-done.4) | copy-start | bytes 1572868
  357.5 18.1 %all-to-all-start.10 = ((bf16[16,16,1024]{2,1,0:T(8,128)(2,1)}), bf16[16,16,1024]{2,1,0:T(8,128)(2,1)S(1)}, u32[]{:S(2)}, u32[]{:S(2)}) async-start(bf16[16,16,1024]{2,1,0:T(8,128)(2,1)} %broadcast_in_dim.11), calls=%async_computation.10 | async-start | bytes 1048576 | tf_op jit(solution)/shard_map/all_to_all | solution.py:41
  383.5 31.6 %copy-start.23 = (bf16[16,1024]{1,0:T(8,128)(2,1)S(1)}, bf16[16,1024]{1,0:T(8,128)(2,1)}, u32[]{:S(2)}) copy-start(bf16[16,1024]{1,0:T(8,128)(2,1)} %fusion.96) | copy-start | bytes 98308
  416.0 19.9 %all-to-all-start.4 = ((bf16[16,16,1024]{2,1,0:T(8,128)(2,1)}), bf16[16,16,1024]{2,1,0:T(8,128)(2,1)}, u32[]{:S(2)}, u32[]{:S(2)}) async-start(bf16[16,16,1024]{2,1,0:T(8,128)(2,1)} %broadcast_in_dim.8), calls=%async_computation.4 | async-start | bytes 1048576 | tf_op jit(solution)/shard_map/all_to_all | solution.py:41
  435.9 29.8 %all-to-all-start.12 = ((bf16[8,2,64,768]{3,2,1,0:T(8,128)(2,1)}), bf16[8,2,64,768]{3,2,1,0:T(8,128)(2,1)S(1)}, u32[]{:S(2)}, u32[]{:S(2)}) async-start(bf16[8,2,64,768]{3,2,1,0:T(8,128)(2,1)} %copy.70), calls=%async_computation.12 | async-start | bytes 3145728 | tf_op jit(solution)/shard_map/all_to_all | solution.py:71
  (19 other events, 80.7 us)
Sparse Core Ops, SparseCore 0:
  41.7 51.3 all-gather.3
  113.3 54.6 all-gather.5
  187.8 54.7 all-gather.7
where the time goes:
time: 479 us; the launch traced here: 477 us
  waiting for transfers between devices  240 us (50%)
  blocking collectives  96 us (20%)
  starting transfers between devices  51.7 us (11%)
  matrix products  33.1 us (7%)
  local copies, waits for them, and re-layouts  22.8 us (5%)
  other arithmetic  18.3 us (4%)
  between operations  15.1 us (3%)
    all_gather x3, waiting for transfers between devices, sent_together(): result, at, done = (lax.all_gather(both, axis, axis=dim, tiled=True), 0, [])  161 us
    all_to_all x5, blocking collectives, sent_and_summed(): blocks = lax.all_to_all(in_blocks(x, dim, devices), axis, 0, 0, tiled=True)  96 us
    all_to_all x3, waiting for transfers between devices, sent_and_summed(): blocks = lax.all_to_all(in_blocks(x, dim, devices), axis, 0, 0, tiled=True)  29.4 us
    all_to_all x4, waiting for transfers between devices, from_everyone(): return lax.all_to_all(copies, axis, split_axis=0, concat_axis=0, tiled=True)  28.5 us
    all_to_all x4, starting transfers between devices, from_everyone(): return lax.all_to_all(copies, axis, split_axis=0, concat_axis=0, tiled=True)  22.3 us
    all_to_all x1, waiting for transfers between devices, sum_by_axis(): lax.all_to_all(nearer.astype(jnp.bfloat16), far, split_axis=0, concat_axi...  20.6 us
    all_to_all x3, starting transfers between devices, sent_and_summed(): blocks = lax.all_to_all(in_blocks(x, dim, devices), axis, 0, 0, tiled=True)  20 us
    dot_general x8, matrix products, contract_rows(): lax.dot_general(left, right, (((0,), (0,)), ((), ())), preferred_element_...  12.1 us
  transfers between devices with their start and end apart: 11, of which 11 were waited for; matrix products, arithmetic and copies ran while one was open for 7% of the time, Pallas kernels for 0%

commit v1 on v0

v1 whole, which is shorter than its diff:
```python
import jax
import jax.numpy as jnp
from jax import lax
from jax.sharding import Mesh
from jax.sharding import PartitionSpec as P

HD = 64
SLATE = 256
LAYERS = 2
DP = ("z_lo", "y", "core")
MP = "mp"

epsilon = 1e-06
bf16 = jnp.bfloat16
f32 = jnp.float32


def share_rows(x, axis):
    n = lax.axis_size(axis)
    blocks = x.reshape(n, x.shape[0] // n, x.shape[1])
    blocks = lax.all_to_all(blocks, axis, 0, 0, tiled=True)
    return jnp.sum(blocks.astype(f32), axis=0)


def all_rows(x, axis):
    n = lax.axis_size(axis)
    copies = jnp.broadcast_to(x[None], (n, *x.shape))
    blocks = lax.all_to_all(copies, axis, 0, 0, tiled=True)
    return blocks.reshape(n * x.shape[0], x.shape[1])


def normalize(stream):
    widened = stream.astype(f32)
    rscale = lax.rsqrt(jnp.mean(widened * widened, axis=-1, keepdims=True) + epsilon)
    scaled = widened * rscale
    return (scaled.astype(bf16), scaled, rscale)


def norm_backward(scaled, rscale, upward):
    inner = jnp.mean(upward * scaled, axis=-1, keepdims=True)
    return rscale * (upward - scaled * inner)


def smooth_gate(preact):
    return jax.nn.gelu(preact, approximate=True)


def dot(left, right, dims):
    return lax.dot_general(left, right, (dims, ((), ())), preferred_element_type=f32)


def contract_rows(left, right):
    return dot(left, right, ((0,), (0,)))


def contract_cols(left, right):
    return dot(left, right, ((1,), (1,)))


def attend(queries, key_rows, values, live):
    scores = contract_cols(queries, key_rows) * HD ** (-0.5)
    weights = jnp.exp(scores) * live
    probs = weights / jnp.sum(weights, axis=-1, keepdims=True)
    context = jnp.dot(probs.astype(bf16), values, preferred_element_type=f32).astype(bf16)
    return probs, context


def attend_backward(probs, queries, key_rows, values, grad_context):
    grad_prob = contract_cols(grad_context, values)
    grad_value = contract_rows(probs.astype(bf16), grad_context).astype(bf16)
    inner = jnp.sum(grad_prob * probs, axis=-1, keepdims=True)
    grad_score = (probs * (grad_prob - inner) * HD ** (-0.5)).astype(bf16)
    grad_query = jnp.dot(grad_score, key_rows, preferred_element_type=f32).astype(bf16)
    grad_key = contract_rows(grad_score, queries).astype(bf16)
    return jnp.concatenate([grad_query, grad_key, grad_value], axis=1)


def body(tokens, lengths, cotangent, triple_weight, output_weight, upward_weight, downward_weight):
    rows, width = tokens.shape
    n = lax.axis_size(MP)
    share = rows // n
    start = lax.axis_index(MP) * share

    def part(x):
        return lax.dynamic_slice_in_dim(x, start, share, 0)

    live = (jnp.arange(SLATE)[None, :] < lengths[:, None]).astype(f32)
    triple = [triple_weight[l].reshape(width, -1) for l in range(LAYERS)]
    saved = []
    stream = tokens
    stream_part = part(tokens)
    for l in range(LAYERS):
        normed, scaled, rscale = normalize(stream)
        qkv = jnp.dot(normed, triple[l], preferred_element_type=f32).astype(bf16)
        queries, key_rows, values = (qkv[:, k * HD : (k + 1) * HD] for k in range(3))
        probs, context = attend(queries, key_rows, values, live)
        partial_att = contract_cols(context, output_weight[l]).astype(bf16)
        mid_part = (stream_part.astype(f32) + share_rows(partial_att, MP)).astype(bf16)
        mid_stream = all_rows(mid_part, MP)
        normed_mid, scaled_mid, rscale_mid = normalize(mid_stream)
        preact = jnp.dot(normed_mid, upward_weight[l], preferred_element_type=f32)
        activated = smooth_gate(preact).astype(bf16)
        partial_ffn = contract_cols(activated, downward_weight[l]).astype(bf16)
        saved.append((normed, scaled, rscale, queries, key_rows, values, probs, context,
                      scaled_mid, rscale_mid, normed_mid, preact, activated))
        if l + 1 < LAYERS:
            stream_part = (mid_part.astype(f32) + share_rows(partial_ffn, MP)).astype(bf16)
            stream = all_rows(stream_part, MP)

    reduced = [None] * LAYERS
    early = []
    upstream, upstream_part = cotangent, part(cotangent)
    for l in reversed(range(LAYERS)):
        (normed, scaled, rscale, queries, key_rows, values, probs, context,
         scaled_mid, rscale_mid, normed_mid, preact, activated) = saved[l]
        grad_act = jnp.dot(upstream, downward_weight[l], preferred_element_type=f32).astype(bf16)
        _, gate_back = jax.vjp(smooth_gate, preact)
        grad_preact = gate_back(grad_act.astype(f32))[0].astype(bf16)
        partial = contract_cols(grad_preact, upward_weight[l]).astype(bf16)
        if l + 1 == LAYERS:
            both = share_rows(jnp.concatenate([partial, partial_ffn], axis=1), MP)
            final_part = (mid_part.astype(f32) + both[:, width:]).astype(bf16)
            both = all_rows(jnp.concatenate([both[:, :width].astype(bf16), final_part], axis=1), MP)
            grad_normed, final_stream = both[:, :width].astype(f32), both[:, width:]
        else:
            grad_normed = all_rows(share_rows(partial, MP).astype(bf16), MP).astype(f32)
        downward_grad = contract_rows(upstream, activated)
        upward_grad = contract_rows(normed_mid, grad_preact)
        grad_mid = (upstream.astype(f32) + norm_backward(scaled_mid, rscale_mid, grad_normed)).astype(bf16)
        output_grad = contract_rows(grad_mid, context)
        grad_context = jnp.dot(grad_mid, output_weight[l], preferred_element_type=f32).astype(bf16)
        grad_qkv = attend_backward(probs, queries, key_rows, values, grad_context)
        triple_grad = contract_rows(normed, grad_qkv)
        early.append([upward_grad, downward_grad])
        late = [triple_grad, output_grad]
        if l > 0:
            early[-1] += late
            grad_input = all_rows(
                share_rows(contract_cols(grad_qkv, triple[l]).astype(bf16), MP).astype(bf16), MP
            ).astype(f32)
            upstream = (grad_mid.astype(f32) + norm_backward(scaled, rscale, grad_input)).astype(bf16)

    def over_slates(grads):
        joined = jnp.concatenate([g.astype(bf16) for g in grads], axis=1)
        summed = share_rows(joined, DP)
        out, at = [], 0
        for g in grads:
            out.append(summed[:, at : at + g.shape[1]])
            at += g.shape[1]
        return out

    up1, down1, triple1, out1 = over_slates(early[0])
    up0, down0 = over_slates(early[1])
    triple0, out0 = over_slates(late)
    heads = triple_weight.shape[-1]
    return (
        final_stream,
        jnp.stack([t.reshape(t.shape[0], 3, heads) for t in (triple0, triple1)]),
        jnp.stack([out0, out1]),
        jnp.stack([up0, up1]),
        jnp.stack([down0, down1]),
    )


def solution(mesh):
    torus = Mesh(mesh.devices.reshape(2, 4, 2, mesh.shape["mp"]), (*DP, MP))
    placed = (
        P(DP, None),
        P(DP),
        P(DP, None),
        P(None, None, None, MP),
        P(None, None, MP),
        P(None, None, MP),
        P(None, None, MP),
    )
    return jax.shard_map(
        body,
        mesh=torus,
        in_specs=placed,
        out_specs=(
            P(DP, None),
            P(None, DP, None, MP),
            P(None, DP, MP),
            P(None, DP, MP),
            P(None, DP, MP),
        ),
        check_vma=False,
    )
```

time: 479 us -> 365 us (0.76)
  waiting for transfers between devices: 240 us -> 97.7 us
  blocking collectives: 96 us -> 148 us
  matrix products: 33.1 us -> 11.5 us
  starting transfers between devices: 51.7 us -> 72.9 us
  between operations: 15.1 us -> 2.15 us
  other arithmetic: 18.3 us -> 13.3 us
  local copies, waits for them, and re-layouts: 22.8 us -> 18 us
    all_gather x3 -> x0, waiting for transfers between devices: 161 us -> none  [sent_together(): result, at, done = (lax.all_gather(both, axis, axis=dim, tiled=True), 0, [])]
    all_to_all x5 -> x8, blocking collectives: 96 us -> 148 us  [the longest x5 91.6 us: share_rows(): blocks = lax.all_to_all(blocks, axis, 0, 0, tiled=True)]
    dot_general x35, matrix products: 33.1 us -> 11.5 us  [the longest x23 8.23 us: dot(): lax.dot_general(left, right, (dims, ((), ())), preferred_element_type=f32)]
    all_to_all x8 -> x7, starting transfers between devices: 51.6 us -> 72.9 us  [the longest x4 59.1 us: share_rows(): blocks = lax.all_to_all(blocks, axis, 0, 0, tiled=True)]
    all_to_all x8 -> x7, waiting for transfers between devices: 78.4 us -> 97.7 us  [the longest x4 49.8 us: share_rows(): blocks = lax.all_to_all(blocks, axis, 0, 0, tiled=True)]
    another operation x6 -> x4, local copies, waits for them, and re-layouts: 6.1 us -> 0.17 us  [the longest x2 0.15 us: body(): jnp.stack([out0, out1])]
    concatenate x0 -> x3, local copies, waits for them, and re-layouts: none -> 4.92 us  [over_slates(): joined = jnp.concatenate([g.astype(bf16) for g in grads], axis=1)]
  transfers between devices with their start and end apart: 11 -> 7, of which waited for: 11 -> 7; matrix products, arithmetic and copies ran while one was open for 7% -> 3% of each run, Pallas kernels for 0% -> 0%
where the time goes in v1:
time: 365 us; the launch traced here: 363 us
  blocking collectives  148 us (41%)
  waiting for transfers between devices  97.7 us (27%)
  starting transfers between devices  72.9 us (20%)
  local copies, waits for them, and re-layouts  18 us (5%)
  other arithmetic  13.3 us (4%)
  matrix products  11.5 us (3%)
    all_to_all x5, blocking collectives, share_rows(): blocks = lax.all_to_all(blocks, axis, 0, 0, tiled=True)  91.6 us
    all_to_all x4, starting transfers between devices, share_rows(): blocks = lax.all_to_all(blocks, axis, 0, 0, tiled=True)  59.1 us
    all_to_all x3, blocking collectives, all_rows(): blocks = lax.all_to_all(copies, axis, 0, 0, tiled=True)  56.1 us
    all_to_all x4, waiting for transfers between devices, share_rows(): blocks = lax.all_to_all(blocks, axis, 0, 0, tiled=True)  49.8 us
    all_to_all x3, waiting for transfers between devices, all_rows(): blocks = lax.all_to_all(copies, axis, 0, 0, tiled=True)  47.9 us
    all_to_all x3, starting transfers between devices, all_rows(): blocks = lax.all_to_all(copies, axis, 0, 0, tiled=True)  13.8 us
    dot_general x23, matrix products, dot(): lax.dot_general(left, right, (dims, ((), ())), preferred_element_type=f32)  8.23 us
  transfers between devices with their start and end apart: 7, of which 7 were waited for; matrix products, arithmetic and copies ran while one was open for 3% of the time, Pallas kernels for 0%

profile of v1, /device:TPU:1, one launch (start us, length us, event | category | flops | bytes accessed | tf_op | source)
XLA Modules:
  0.0 363.3 jit_solution(4726964083687581352)
XLA Ops:
  5.5 11.6 %all-to-all-start = ((bf16[16,16,1024]{2,1,0:T(8,128)(2,1)}), bf16[16,16,1024]{2,1,0:T(8,128)(2,1)S(1)}, u32[]{:S(2)}, u32[]{:S(2)}) async-start(bf16[16,16,1024]{2,1,0:T(8,128)(2,1)} %bitcast.4), calls=%async_computation | async-start | bytes 1048576 | tf_op jit(solution)/shard_map/all_to_all | solution.py:21
  17.1 14.8 %all-to-all-done = bf16[16,16,1024]{2,1,0:T(8,128)(2,1)S(1)} async-done(((bf16[16,16,1024]{2,1,0:T(8,128)(2,1)}), bf16[16,16,1024]{2,1,0:T(8,128)(2,1)S(1)}, u32[]{:S(2)}, u32[]{:S(2)}) %all-to-all-start) | async-done | bytes 524320 | tf_op jit(solution)/shard_map/all_to_all | solution.py:21
  32.1 22.6 %all_to_all.75 = bf16[16,16,1024]{2,1,0:T(8,128)(2,1)S(1)} all-to-all(bf16[16,16,1024]{2,1,0:T(8,128)(2,1)S(1)} %broadcast_in_dim.12), channel_id=1, replica_groups=mesh['z_lo'=2,'y'=4,'core'=2,'mp'=16] {'mp'}, dimensions={0} | all-to-all | bytes 1048576 | tf_op jit(solution)/shard_map/all_to_all | solution.py:28
  56.3 20.7 %all_to_all.76 = bf16[16,16,1024]{2,1,0:T(8,128)(2,1)S(1)} all-to-all(bf16[16,16,1024]{2,1,0:T(8,128)(2,1)S(1)} %bitcast.151), channel_id=1, replica_groups=mesh['z_lo'=2,'y'=4,'core'=2,'mp'=16] {'mp'}, dimensions={0} | all-to-all | bytes 1048576 | tf_op jit(solution)/shard_map/all_to_all | solution.py:21
  77.1 17.0 %all_to_all.77 = bf16[16,16,1024]{2,1,0:T(8,128)(2,1)S(1)} all-to-all(bf16[16,16,1024]{2,1,0:T(8,128)(2,1)S(1)} %broadcast_in_dim.13), channel_id=1, replica_groups=mesh['z_lo'=2,'y'=4,'core'=2,'mp'=16] {'mp'}, dimensions={0} | all-to-all | bytes 1048576 | tf_op jit(solution)/shard_map/all_to_all | solution.py:28
  96.6 17.1 %all_to_all.78 = bf16[16,16,1024]{2,1,0:T(8,128)(2,1)S(1)} all-to-all(bf16[16,16,1024]{2,1,0:T(8,128)(2,1)S(1)} %bitcast.148), channel_id=1, replica_groups=mesh['z_lo'=2,'y'=4,'core'=2,'mp'=16] {'mp'}, dimensions={0} | all-to-all | bytes 1048576 | tf_op jit(solution)/shard_map/all_to_all | solution.py:21
  113.8 16.5 %all_to_all.79 = bf16[16,16,1024]{2,1,0:T(8,128)(2,1)S(1)} all-to-all(bf16[16,16,1024]{2,1,0:T(8,128)(2,1)S(1)} %broadcast_in_dim.14), channel_id=1, replica_groups=mesh['z_lo'=2,'y'=4,'core'=2,'mp'=16] {'mp'}, dimensions={0} | all-to-all | bytes 1048576 | tf_op jit(solution)/shard_map/all_to_all | solution.py:28
  133.8 19.8 %all_to_all.80 = bf16[16,16,2048]{2,1,0:T(8,128)(2,1)S(1)} all-to-all(bf16[16,16,2048]{2,1,0:T(8,128)(2,1)S(1)} %bitcast.142), channel_id=1, replica_groups=mesh['z_lo'=2,'y'=4,'core'=2,'mp'=16] {'mp'}, dimensions={0} | all-to-all | bytes 2097152 | tf_op jit(solution)/shard_map/all_to_all | solution.py:21
  154.9 3.7 %all-to-all-start.7 = ((bf16[16,16,2048]{2,1,0:T(8,128)(2,1)}), bf16[16,16,2048]{2,1,0:T(8,128)(2,1)S(1)}, u32[]{:S(2)}, u32[]{:S(2)}) async-start(bf16[16,16,2048]{2,1,0:T(8,128)(2,1)} %broadcast_in_dim.15), calls=%async_computation.7 | async-start | bytes 2097152 | tf_op jit(solution)/shard_map/all_to_all | solution.py:28
  158.6 25.2 %all-to-all-done.7 = bf16[16,16,2048]{2,1,0:T(8,128)(2,1)S(1)} async-done(((bf16[16,16,2048]{2,1,0:T(8,128)(2,1)}), bf16[16,16,2048]{2,1,0:T(8,128)(2,1)S(1)}, u32[]{:S(2)}, u32[]{:S(2)}) %all-to-all-start.7) | async-done | bytes 1048608 | tf_op jit(solution)/shard_map/all_to_all | solution.py:28
  188.2 18.2 %all_to_all.81 = bf16[16,16,1024]{2,1,0:T(8,128)(2,1)S(1)} all-to-all(bf16[16,16,1024]{2,1,0:T(8,128)(2,1)S(1)} %bitcast.146), channel_id=1, replica_groups=mesh['z_lo'=2,'y'=4,'core'=2,'mp'=16] {'mp'}, dimensions={0} | all-to-all | bytes 1048576 | tf_op jit(solution)/shard_map/all_to_all | solution.py:21
  207.3 6.4 %all-to-all-start.9 = ((bf16[16,16,1024]{2,1,0:T(8,128)(2,1)}), bf16[16,16,1024]{2,1,0:T(8,128)(2,1)S(1)}, u32[]{:S(2)}, u32[]{:S(2)}) async-start(bf16[16,16,1024]{2,1,0:T(8,128)(2,1)} %broadcast_in_dim.16), calls=%async_computation.9 | async-start | bytes 1048576 | tf_op jit(solution)/shard_map/all_to_all | solution.py:28
  213.8 11.5 %all-to-all-done.9 = bf16[16,16,1024]{2,1,0:T(8,128)(2,1)S(1)} async-done(((bf16[16,16,1024]{2,1,0:T(8,128)(2,1)}), bf16[16,16,1024]{2,1,0:T(8,128)(2,1)S(1)}, u32[]{:S(2)}, u32[]{:S(2)}) %all-to-all-start.9) | async-done | bytes 524320 | tf_op jit(solution)/shard_map/all_to_all | solution.py:28
  228.6 15.9 %all_to_all.82 = bf16[16,16,1024]{2,1,0:T(8,128)(2,1)S(1)} all-to-all(bf16[16,16,1024]{2,1,0:T(8,128)(2,1)S(1)} %bitcast.150), channel_id=1, replica_groups=mesh['z_lo'=2,'y'=4,'core'=2,'mp'=16] {'mp'}, dimensions={0} | all-to-all | bytes 1048576 | tf_op jit(solution)/shard_map/all_to_all | solution.py:21
  246.8 3.8 %all-to-all-start.11 = ((bf16[16,16,1024]{2,1,0:T(8,128)(2,1)}), bf16[16,16,1024]{2,1,0:T(8,128)(2,1)S(1)}, u32[]{:S(2)}, u32[]{:S(2)}) async-start(bf16[16,16,1024]{2,1,0:T(8,128)(2,1)} %broadcast_in_dim.17), calls=%async_computation.11 | async-start | bytes 1048576 | tf_op jit(solution)/shard_map/all_to_all | solution.py:28
  250.7 11.2 %all-to-all-done.11 = bf16[16,16,1024]{2,1,0:T(8,128)(2,1)S(1)} async-done(((bf16[16,16,1024]{2,1,0:T(8,128)(2,1)}), bf16[16,16,1024]{2,1,0:T(8,128)(2,1)S(1)}, u32[]{:S(2)}, u32[]{:S(2)}) %all-to-all-start.11) | async-done | bytes 524320 | tf_op jit(solution)/shard_map/all_to_all | solution.py:28
  266.5 37.6 %all-to-all-start.12 = ((bf16[16,64,256]{2,1,0:T(8,128)(2,1)}), bf16[16,64,256]{2,1,0:T(8,128)(2,1)}, u32[]{:S(2)}, u32[]{:S(2)}) async-start(bf16[16,64,256]{2,1,0:T(8,128)(2,1)} %bitcast.24), calls=%async_computation.12 | async-start | bytes 1048576 | tf_op jit(solution)/shard_map/all_to_all | solution.py:21
  305.6 1.6 copy.23
  307.2 6.8 %all-to-all-done.12 = bf16[16,64,256]{2,1,0:T(8,128)(2,1)} async-done(((bf16[16,64,256]{2,1,0:T(8,128)(2,1)}), bf16[16,64,256]{2,1,0:T(8,128)(2,1)}, u32[]{:S(2)}, u32[]{:S(2)}) %all-to-all-start.12) | async-done | bytes 524320 | tf_op jit(solution)/shard_map/all_to_all | solution.py:21
  314.0 4.9 %all-to-all-start.13 = ((bf16[16,64,768]{2,1,0:T(8,128)(2,1)}), bf16[16,64,768]{2,1,0:T(8,128)(2,1)S(1)}, u32[]{:S(2)}, u32[]{:S(2)}) async-start(bf16[16,64,768]{2,1,0:T(8,128)(2,1)} %bitcast.140), calls=%async_computation.13 | async-start | bytes 3145728 | tf_op jit(solution)/shard_map/all_to_all | solution.py:21
  321.6 2.3 copy.25
  323.9 16.4 %all-to-all-done.13 = bf16[16,64,768]{2,1,0:T(8,128)(2,1)S(1)} async-done(((bf16[16,64,768]{2,1,0:T(8,128)(2,1)}), bf16[16,64,768]{2,1,0:T(8,128)(2,1)S(1)}, u32[]{:S(2)}, u32[]{:S(2)}) %all-to-all-start.13) | async-done | bytes 1572896 | tf_op jit(solution)/shard_map/all_to_all | solution.py:21
  340.3 5.0 %all-to-all-start.14 = ((bf16[16,64,512]{2,1,0:T(8,128)(2,1)}), bf16[16,64,512]{2,1,0:T(8,128)(2,1)}, u32[]{:S(2)}, u32[]{:S(2)}) async-start(bf16[16,64,512]{2,1,0:T(8,128)(2,1)} %bitcast.141), calls=%async_computation.14 | async-start | bytes 2097152 | tf_op jit(solution)/shard_map/all_to_all | solution.py:21
  349.3 11.8 %all-to-all-done.14 = bf16[16,64,512]{2,1,0:T(8,128)(2,1)} async-done(((bf16[16,64,512]{2,1,0:T(8,128)(2,1)}), bf16[16,64,512]{2,1,0:T(8,128)(2,1)}, u32[]{:S(2)}, u32[]{:S(2)}) %all-to-all-start.14) | async-done | bytes 1048608 | tf_op jit(solution)/shard_map/all_to_all | solution.py:21
  (202 shorter events, 39.0 us)
Async XLA Ops:
  1.9 2.4 copy-start.11
  2.1 3.4 copy-start.46
  3.2 28.8 %copy-start.39 = (bf16[256,192]{0,1:T(8,128)(2,1)}, bf16[256,192]{0,1:T(8,128)(2,1)S(1)}, u32[]{:S(2)}) copy-start(bf16[256,192]{0,1:T(8,128)(2,1)S(1)} %convolution_convert_fusion.18) | copy-start | bytes 294916
  3.5 28.5 %copy-start.42 = (f32[256]{0:T(256)}, f32[256]{0:T(256)S(1)}, u32[]{:S(2)}) copy-start(f32[256]{0:T(256)S(1)} %get-tuple-element.27) | copy-start | bytes 3076
  4.4 27.6 %copy-start.33 = (bf16[256,64]{0,1:T(8,128)(2,1)}, bf16[256,64]{0,1:T(8,128)(2,1)S(1)}, u32[]{:S(2)}) copy-start(bf16[256,64]{0,1:T(8,128)(2,1)S(1)} %convolution_convert_fusion.22) | copy-start | bytes 98308
  5.5 26.4 %all-to-all-start = ((bf16[16,16,1024]{2,1,0:T(8,128)(2,1)}), bf16[16,16,1024]{2,1,0:T(8,128)(2,1)S(1)}, u32[]{:S(2)}, u32[]{:S(2)}) async-start(bf16[16,16,1024]{2,1,0:T(8,128)(2,1)} %bitcast.4), calls=%async_computation | async-start | bytes 1048576 | tf_op jit(solution)/shard_map/all_to_all | solution.py:21
  32.0 23.0 %copy-start = (bf16[2,1024,256]{2,1,0:T(8,128)(2,1)S(1)}, bf16[2,1024,256]{2,1,0:T(8,128)(2,1)}, u32[]{:S(2)}) copy-start(bf16[2,1024,256]{2,1,0:T(8,128)(2,1)} %param.12) | copy-start | bytes 3145732
  55.9 21.1 %copy-start.25 = (f32[256,256]{1,0:T(8,128)}, f32[256,256]{1,0:T(8,128)S(1)}, u32[]{:S(2)}) copy-start(f32[256,256]{1,0:T(8,128)S(1)} %fusion.30) | copy-start | bytes 786436
  153.8 4.8 %copy-start.38 = (f32[16,16]{1,0:T(8,128)S(1)}, f32[16,16]{1,0:T(8,128)}, u32[]{:S(2)}) copy-start(f32[16,16]{1,0:T(8,128)} %copy-done.37) | copy-start | bytes 3076
  154.9 29.0 %all-to-all-start.7 = ((bf16[16,16,2048]{2,1,0:T(8,128)(2,1)}), bf16[16,16,2048]{2,1,0:T(8,128)(2,1)S(1)}, u32[]{:S(2)}, u32[]{:S(2)}) async-start(bf16[16,16,2048]{2,1,0:T(8,128)(2,1)} %broadcast_in_dim.15), calls=%async_computation.7 | async-start | bytes 2097152 | tf_op jit(solution)/shard_map/all_to_all | solution.py:28
  158.6 26.3 %copy-start.41 = (f32[256]{0:T(256)}, f32[256]{0:T(256)S(1)}, u32[]{:S(2)}) copy-start(f32[256]{0:T(256)S(1)} %rsqrt.48) | copy-start | bytes 3076
  183.8 2.5 copy-start.13
  207.3 18.0 %all-to-all-start.9 = ((bf16[16,16,1024]{2,1,0:T(8,128)(2,1)}), bf16[16,16,1024]{2,1,0:T(8,128)(2,1)S(1)}, u32[]{:S(2)}, u32[]{:S(2)}) async-start(bf16[16,16,1024]{2,1,0:T(8,128)(2,1)} %broadcast_in_dim.16), calls=%async_computation.9 | async-start | bytes 1048576 | tf_op jit(solution)/shard_map/all_to_all | solution.py:28
  244.5 17.7 %copy-start.8 = (bf16[256,1024]{1,0:T(8,128)(2,1)S(1)}, bf16[256,1024]{1,0:T(8,128)(2,1)}, u32[]{:S(2)}) copy-start(bf16[256,1024]{1,0:T(8,128)(2,1)} %copy-done.7) | copy-start | bytes 1572868
  246.8 15.0 %all-to-all-start.11 = ((bf16[16,16,1024]{2,1,0:T(8,128)(2,1)}), bf16[16,16,1024]{2,1,0:T(8,128)(2,1)S(1)}, u32[]{:S(2)}, u32[]{:S(2)}) async-start(bf16[16,16,1024]{2,1,0:T(8,128)(2,1)} %broadcast_in_dim.17), calls=%async_computation.11 | async-start | bytes 1048576 | tf_op jit(solution)/shard_map/all_to_all | solution.py:28
  265.4 38.7 %copy-start.3 = (bf16[256,1024]{1,0:T(8,128)(2,1)S(1)}, bf16[256,1024]{1,0:T(8,128)(2,1)}, u32[]{:S(2)}) copy-start(bf16[256,1024]{1,0:T(8,128)(2,1)} %param.9) | copy-start | bytes 1572868
  265.4 38.7 %copy-start.10 = (f32[256,256]{1,0:T(8,128)S(1)}, f32[256,256]{1,0:T(8,128)}, u32[]{:S(2)}) copy-start(f32[256,256]{1,0:T(8,128)} %copy-done.9) | copy-start | bytes 786436
  265.5 39.0 %copy-start.36 = (bf16[256,64]{0,1:T(8,128)(2,1)S(1)}, bf16[256,64]{0,1:T(8,128)(2,1)}, u32[]{:S(2)}) copy-start(bf16[256,64]{0,1:T(8,128)(2,1)} %copy-done.35) | copy-start | bytes 98308
  266.5 38.2 %copy-start.4 = (bf16[256,1024]{1,0:T(8,128)(2,1)S(1)}, bf16[256,1024]{1,0:T(8,128)(2,1)}, u32[]{:S(2)}) copy-start(bf16[256,1024]{1,0:T(8,128)(2,1)} %get-tuple-element.21) | copy-start | bytes 1572868
  266.5 38.2 %copy-start.18 = (bf16[256,256]{1,0:T(8,128)(2,1)S(1)}, bf16[256,256]{1,0:T(8,128)(2,1)}, u32[]{:S(2)}) copy-start(bf16[256,256]{1,0:T(8,128)(2,1)} %copy-done.17) | copy-start | bytes 393220
  266.5 47.4 %all-to-all-start.12 = ((bf16[16,64,256]{2,1,0:T(8,128)(2,1)}), bf16[16,64,256]{2,1,0:T(8,128)(2,1)}, u32[]{:S(2)}, u32[]{:S(2)}) async-start(bf16[16,64,256]{2,1,0:T(8,128)(2,1)} %bitcast.24), calls=%async_computation.12 | async-start | bytes 1048576 | tf_op jit(solution)/shard_map/all_to_all | solution.py:21
  314.0 6.3 %copy-start.6 = (bf16[256,1024]{1,0:T(8,128)(2,1)S(1)}, bf16[256,1024]{1,0:T(8,128)(2,1)}, u32[]{:S(2)}) copy-start(bf16[256,1024]{1,0:T(8,128)(2,1)} %get-tuple-element.17) | copy-start | bytes 1572868
  314.0 26.3 %all-to-all-start.13 = ((bf16[16,64,768]{2,1,0:T(8,128)(2,1)}), bf16[16,64,768]{2,1,0:T(8,128)(2,1)S(1)}, u32[]{:S(2)}, u32[]{:S(2)}) async-start(bf16[16,64,768]{2,1,0:T(8,128)(2,1)} %bitcast.140), calls=%async_computation.13 | async-start | bytes 3145728 | tf_op jit(solution)/shard_map/all_to_all | solution.py:21
  340.3 20.9 %all-to-all-start.14 = ((bf16[16,64,512]{2,1,0:T(8,128)(2,1)}), bf16[16,64,512]{2,1,0:T(8,128)(2,1)}, u32[]{:S(2)}, u32[]{:S(2)}) async-start(bf16[16,64,512]{2,1,0:T(8,128)(2,1)} %bitcast.141), calls=%async_computation.14 | async-start | bytes 2097152 | tf_op jit(solution)/shard_map/all_to_all | solution.py:21
  (33 other events, 37.7 us)

commit v2 on v1

--- a/solution.py
+++ b/solution.py
@@ -8,7 +8,7 @@
 SLATE = 256
 LAYERS = 2
 DP = ("z_lo", "y", "core")
-MP = "mp"
+MP = ("z_hi", "x")
 
 epsilon = 1e-06
 bf16 = jnp.bfloat16
@@ -27,6 +27,42 @@
     copies = jnp.broadcast_to(x[None], (n, *x.shape))
     blocks = lax.all_to_all(copies, axis, 0, 0, tiled=True)
     return blocks.reshape(n * x.shape[0], x.shape[1])
+
+
+def swapped(x, axis):
+    return lax.ppermute(x, axis, [(0, 1), (1, 0)])
+
+
+def moved(x, axis, step):
+    n = lax.axis_size(axis)
+    return lax.ppermute(x, axis, [(k, (k + step) % n) for k in range(n)])
+
+
+def pick(x, index):
+    return lax.dynamic_index_in_dim(x, index, 0, keepdims=False)
+
+
+def pair_sum(x, axis):
+    here = lax.axis_index(axis)
+    got = swapped(pick(x, 1 - here), axis)
+    return (pick(x, here).astype(f32) + got.astype(f32))
+
+
+def direct_sum(x, axis):
+    n = lax.axis_size(axis)
+    here = lax.axis_index(axis)
+    total = pick(x, here).astype(f32)
+    for step in range(1, n):
+        total = total + moved(pick(x, (here + step) % n), axis, step).astype(f32)
+    return total
+
+
+def slate_sum(grads):
+    rows, cols = grads.shape
+    parts = grads.reshape(2, 4, 2, rows // 16, cols)
+    parts = pair_sum(jnp.moveaxis(parts, 2, 0), "core").astype(bf16)
+    parts = direct_sum(jnp.moveaxis(parts, 1, 0), "y").astype(bf16)
+    return pair_sum(parts, "z_lo")
 
 
 def normalize(stream):
@@ -107,9 +143,8 @@
             stream_part = (mid_part.astype(f32) + share_rows(partial_ffn, MP)).astype(bf16)
             stream = all_rows(stream_part, MP)
 
-    reduced = [None] * LAYERS
     early = []
-    upstream, upstream_part = cotangent, part(cotangent)
+    upstream = cotangent
     for l in reversed(range(LAYERS)):
         (normed, scaled, rscale, queries, key_rows, values, probs, context,
          scaled_mid, rscale_mid, normed_mid, preact, activated) = saved[l]
@@ -118,10 +153,16 @@
         grad_preact = gate_back(grad_act.astype(f32))[0].astype(bf16)
         partial = contract_cols(grad_preact, upward_weight[l]).astype(bf16)
         if l + 1 == LAYERS:
-            both = share_rows(jnp.concatenate([partial, partial_ffn], axis=1), MP)
-            final_part = (mid_part.astype(f32) + both[:, width:]).astype(bf16)
-            both = all_rows(jnp.concatenate([both[:, :width].astype(bf16), final_part], axis=1), MP)
-            grad_normed, final_stream = both[:, :width].astype(f32), both[:, width:]
+            quarter = width // lax.axis_size("x")
+            shares = jnp.stack([partial_ffn[:, k * quarter : (k + 1) * quarter] for k in range(4)])
+            shares = direct_sum(shares, "x").astype(bf16).reshape(n, share, quarter)
+            own = share_rows(partial, MP).astype(bf16)
+            sent = jnp.concatenate([jnp.broadcast_to(own[None], (n, share, width)), shares], axis=2)
+            came = lax.all_to_all(sent, MP, 0, 0, tiled=True)
+            grad_normed = came[:, :, :width].reshape(rows, width).astype(f32)
+            ffn_part = jnp.sum(came[:, :, width:].reshape(4, 4, share, quarter).astype(f32), axis=0)
+            ffn_part = jnp.concatenate([ffn_part[k] for k in range(4)], axis=1)
+            final_part = (mid_part.astype(f32) + ffn_part).astype(bf16)
         else:
             grad_normed = all_rows(share_rows(partial, MP).astype(bf16), MP).astype(f32)
         downward_grad = contract_rows(upstream, activated)
@@ -135,23 +176,36 @@
         late = [triple_grad, output_grad]
         if l > 0:
             early[-1] += late
-            grad_input = all_rows(
-                share_rows(contract_cols(grad_qkv, triple[l]).astype(bf16), MP).astype(bf16), MP
-            ).astype(f32)
+            partial = contract_cols(grad_qkv, triple[l]).astype(bf16).reshape(n, share, width)
+            quarters = jnp.stack([final_part[:, k * quarter : (k + 1) * quarter] for k in range(4)])
+            sent = jnp.concatenate([partial, jnp.tile(quarters, (4, 1, 1))], axis=2)
+            came = lax.all_to_all(sent, MP, 0, 0, tiled=True)
+            own = jnp.sum(came[:, :, :width].astype(f32), axis=0).astype(bf16)
+            column = came[:, :, width:].reshape(rows, quarter)
+            here = lax.axis_index("x")
+            columns = [column] + [moved(column, "x", step) for step in range(1, 4)]
+            final_stream = jnp.concatenate(
+                [
+                    lax.select_n((here - k) % 4, *columns)
+                    for k in range(4)
+                ],
+                axis=1,
+            )
+            grad_input = all_rows(own, MP).astype(f32)
             upstream = (grad_mid.astype(f32) + norm_backward(scaled, rscale, grad_input)).astype(bf16)
 
-    def over_slates(grads):
+    def over_slates(grads, total):
         joined = jnp.concatenate([g.astype(bf16) for g in grads], axis=1)
-        summed = share_rows(joined, DP)
+        summed = total(joined)
         out, at = [], 0
         for g in grads:
             out.append(summed[:, at : at + g.shape[1]])
             at += g.shape[1]
         return out
 
-    up1, down1, triple1, out1 = over_slates(early[0])
-    up0, down0 = over_slates(early[1])
-    triple0, out0 = over_slates(late)
+    up1, down1, triple1, out1 = over_slates(early[0], slate_sum)
+    up0, down0 = over_slates(early[1], slate_sum)
+    triple0, out0 = over_slates(late, lambda g: share_rows(g, DP))
     heads = triple_weight.shape[-1]
     return (
         final_stream,
@@ -163,7 +217,7 @@
 
 
 def solution(mesh):
-    torus = Mesh(mesh.devices.reshape(2, 4, 2, mesh.shape["mp"]), (*DP, MP))
+    torus = Mesh(mesh.devices.reshape(2, 4, 2, 4, 4), (*DP, *MP))
     placed = (
         P(DP, None),
         P(DP),

time: 365 us -> 328 us (0.90)
  blocking collectives: 148 us -> 99.8 us
  starting transfers between devices: 72.9 us -> 88.2 us
  waiting for transfers between devices: 97.7 us -> 87 us
  matrix products: 11.5 us -> 17.1 us
    all_to_all x5 -> x2, blocking collectives: 91.6 us -> 37.1 us  [share_rows(): blocks = lax.all_to_all(blocks, axis, 0, 0, tiled=True)]
    ppermute x0 -> x16, starting transfers between devices: none -> 43.6 us  [the longest x4 27.9 us: swapped(): return lax.ppermute(x, axis, [(0, 1), (1, 0)])]
    all_to_all x4, starting transfers between devices: 59.1 us -> 23.8 us  [share_rows(): blocks = lax.all_to_all(blocks, axis, 0, 0, tiled=True)]
    all_to_all x4, waiting for transfers between devices: 49.8 us -> 19.9 us  [share_rows(): blocks = lax.all_to_all(blocks, axis, 0, 0, tiled=True)]
    ppermute x0 -> x16, waiting for transfers between devices: none -> 28.3 us  [the longest x4 18.2 us: swapped(): return lax.ppermute(x, axis, [(0, 1), (1, 0)])]
    all_to_all x3, waiting for transfers between devices: 47.9 us -> 22.3 us  [all_rows(): blocks = lax.all_to_all(copies, axis, 0, 0, tiled=True)]
    all_to_all x0 -> x1, blocking collectives: none -> 22 us  [body(): came = lax.all_to_all(sent, MP, 0, 0, tiled=True)]
    all_to_all x0 -> x1, waiting for transfers between devices: none -> 16.5 us  [body(): came = lax.all_to_all(sent, MP, 0, 0, tiled=True)]
  transfers between devices with their start and end apart: 7 -> 24, of which waited for: 7 -> 13; matrix products, arithmetic and copies ran while one was open for 3% -> 6% of each run, Pallas kernels for 0% -> 0%
where the time goes in v2:
time: 328 us; the launch traced here: 326 us
  blocking collectives  99.8 us (30%)
  starting transfers between devices  88.2 us (27%)
  waiting for transfers between devices  87 us (27%)
  local copies, waits for them, and re-layouts  17.1 us (5%)
  matrix products  17.1 us (5%)
  other arithmetic  14.3 us (4%)
    all_to_all x2, blocking collectives, all_rows(): blocks = lax.all_to_all(copies, axis, 0, 0, tiled=True)  40.6 us
    all_to_all x2, blocking collectives, share_rows(): blocks = lax.all_to_all(blocks, axis, 0, 0, tiled=True)  37.1 us
    ppermute x4, starting transfers between devices, swapped(): return lax.ppermute(x, axis, [(0, 1), (1, 0)])  27.9 us
    all_to_all x4, starting transfers between devices, share_rows(): blocks = lax.all_to_all(blocks, axis, 0, 0, tiled=True)  23.8 us
    all_to_all x3, waiting for transfers between devices, all_rows(): blocks = lax.all_to_all(copies, axis, 0, 0, tiled=True)  22.3 us
    all_to_all x1, blocking collectives, body(): came = lax.all_to_all(sent, MP, 0, 0, tiled=True)  22 us
    all_to_all x4, waiting for transfers between devices, share_rows(): blocks = lax.all_to_all(blocks, axis, 0, 0, tiled=True)  19.9 us
    ppermute x4, waiting for transfers between devices, swapped(): return lax.ppermute(x, axis, [(0, 1), (1, 0)])  18.2 us
  transfers between devices with their start and end apart: 24, of which 13 were waited for; matrix products, arithmetic and copies ran while one was open for 6% of the time, Pallas kernels for 0%

profile of v2, /device:TPU:1, one launch (start us, length us, event | category | flops | bytes accessed | tf_op | source)
XLA Modules:
  0.0 326.1 jit_solution(13612072678890115837)
XLA Ops:
  4.8 11.6 %all-to-all-start = ((bf16[16,16,1024]{2,1,0:T(8,128)(2,1)}), bf16[16,16,1024]{2,1,0:T(8,128)(2,1)S(1)}, u32[]{:S(2)}, u32[]{:S(2)}) async-start(bf16[16,16,1024]{2,1,0:T(8,128)(2,1)} %bitcast.3), calls=%async_computation | async-start | bytes 1048576 | tf_op jit(solution)/shard_map/all_to_all | solution.py:21
  16.4 14.9 %all-to-all-done = bf16[16,16,1024]{2,1,0:T(8,128)(2,1)S(1)} async-done(((bf16[16,16,1024]{2,1,0:T(8,128)(2,1)}), bf16[16,16,1024]{2,1,0:T(8,128)(2,1)S(1)}, u32[]{:S(2)}, u32[]{:S(2)}) %all-to-all-start) | async-done | bytes 524320 | tf_op jit(solution)/shard_map/all_to_all | solution.py:21
  31.4 22.6 %all_to_all.65 = bf16[16,16,1024]{2,1,0:T(8,128)(2,1)S(1)} all-to-all(bf16[16,16,1024]{2,1,0:T(8,128)(2,1)S(1)} %broadcast_in_dim.12), channel_id=1, replica_groups=mesh['z_lo'=2,'y'=4,'core'=2,'z_hi'=4,'x'=4] {'z_hi','x'}, dimensions={0} | all-to-all | bytes 1048576 | tf_op jit(solution)/shard_map/all_to_all | solution.py:28
  55.6 20.0 %all_to_all.66 = bf16[16,16,1024]{2,1,0:T(8,128)(2,1)S(1)} all-to-all(bf16[16,16,1024]{2,1,0:T(8,128)(2,1)S(1)} %bitcast.237), channel_id=1, replica_groups=mesh['z_lo'=2,'y'=4,'core'=2,'z_hi'=4,'x'=4] {'z_hi','x'}, dimensions={0} | all-to-all | bytes 1048576 | tf_op jit(solution)/shard_map/all_to_all | solution.py:21
  75.8 18.0 %all_to_all.67 = bf16[16,16,1024]{2,1,0:T(8,128)(2,1)S(1)} all-to-all(bf16[16,16,1024]{2,1,0:T(8,128)(2,1)S(1)} %broadcast_in_dim.13), channel_id=1, replica_groups=mesh['z_lo'=2,'y'=4,'core'=2,'z_hi'=4,'x'=4] {'z_hi','x'}, dimensions={0} | all-to-all | bytes 1048576 | tf_op jit(solution)/shard_map/all_to_all | solution.py:28
  95.7 17.1 %all_to_all.68 = bf16[16,16,1024]{2,1,0:T(8,128)(2,1)S(1)} all-to-all(bf16[16,16,1024]{2,1,0:T(8,128)(2,1)S(1)} %bitcast.234), channel_id=1, replica_groups=mesh['z_lo'=2,'y'=4,'core'=2,'z_hi'=4,'x'=4] {'z_hi','x'}, dimensions={0} | all-to-all | bytes 1048576 | tf_op jit(solution)/shard_map/all_to_all | solution.py:21
  113.7 3.6 %all-to-all-start.5 = ((bf16[16,16,1024]{2,1,0:T(8,128)(2,1)}), bf16[16,16,1024]{2,1,0:T(8,128)(2,1)S(1)}, u32[]{:S(2)}, u32[]{:S(2)}) async-start(bf16[16,16,1024]{2,1,0:T(8,128)(2,1)} %broadcast_in_dim.14), calls=%async_computation.5 | async-start | bytes 1048576 | tf_op jit(solution)/shard_map/all_to_all | solution.py:28
  117.4 11.3 %all-to-all-done.5 = bf16[16,16,1024]{2,1,0:T(8,128)(2,1)S(1)} async-done(((bf16[16,16,1024]{2,1,0:T(8,128)(2,1)}), bf16[16,16,1024]{2,1,0:T(8,128)(2,1)S(1)}, u32[]{:S(2)}, u32[]{:S(2)}) %all-to-all-start.5) | async-done | bytes 524320 | tf_op jit(solution)/shard_map/all_to_all | solution.py:28
  132.4 3.7 %all-to-all-start.6 = ((bf16[16,16,1024]{2,1,0:T(8,128)(2,1)}), bf16[16,16,1024]{2,1,0:T(8,128)(2,1)S(1)}, u32[]{:S(2)}, u32[]{:S(2)}) async-start(bf16[16,16,1024]{2,1,0:T(8,128)(2,1)} %bitcast.230), calls=%async_computation.6 | async-start | bytes 1048576 | tf_op jit(solution)/shard_map/all_to_all | solution.py:21
  142.1 4.6 %collective-permute-done.2 = bf16[256,256]{1,0:T(8,128)(2,1)S(1)} collective-permute-done((bf16[256,256]{1,0:T(8,128)(2,1)}, bf16[256,256]{1,0:T(8,128)(2,1)S(1)}, u32[]{:S(2)}, u32[]{:S(2)}) %collective-permute-start.2) | collective-permute-done | bytes 131104 | tf_op jit(solution)/shard_map/ppermute | solution.py:38
  151.4 5.5 %all-to-all-start.7 = ((bf16[16,16,1280]{2,1,0:T(8,128)(2,1)}), bf16[16,16,1280]{2,1,0:T(8,128)(2,1)S(1)}, u32[]{:S(2)}, u32[]{:S(2)}) async-start(bf16[16,16,1280]{2,1,0:T(8,128)(2,1)} %pad_maximum_fusion.2), calls=%async_computation.7 | async-start | bytes 1310720 | tf_op jit(solution)/shard_map/all_to_all | solution.py:161
  157.0 16.5 %all-to-all-done.7 = bf16[16,16,1280]{2,1,0:T(8,128)(2,1)S(1)} async-done(((bf16[16,16,1280]{2,1,0:T(8,128)(2,1)}), bf16[16,16,1280]{2,1,0:T(8,128)(2,1)S(1)}, u32[]{:S(2)}, u32[]{:S(2)}) %all-to-all-start.7) | async-done | bytes 655392 | tf_op jit(solution)/shard_map/all_to_all | solution.py:161
  178.6 22.0 %all_to_all.69 = bf16[16,16,1280]{2,1,0:T(8,128)(2,1)S(1)} all-to-all(bf16[16,16,1280]{2,1,0:T(8,128)(2,1)S(1)} %pad_maximum_fusion.3), channel_id=1, replica_groups=mesh['z_lo'=2,'y'=4,'core'=2,'z_hi'=4,'x'=4] {'z_hi','x'}, dimensions={0} | all-to-all | bytes 1310720 | tf_op jit(solution)/shard_map/all_to_all | solution.py:182
  201.6 4.7 %all-to-all-start.9 = ((bf16[16,16,1024]{2,1,0:T(8,128)(2,1)}), bf16[16,16,1024]{2,1,0:T(8,128)(2,1)S(1)}, u32[]{:S(2)}, u32[]{:S(2)}) async-start(bf16[16,16,1024]{2,1,0:T(8,128)(2,1)} %broadcast_in_dim.16), calls=%async_computation.9 | async-start | bytes 1048576 | tf_op jit(solution)/shard_map/all_to_all | solution.py:28
  209.4 8.8 %all-to-all-done.9 = bf16[16,16,1024]{2,1,0:T(8,128)(2,1)S(1)} async-done(((bf16[16,16,1024]{2,1,0:T(8,128)(2,1)}), bf16[16,16,1024]{2,1,0:T(8,128)(2,1)S(1)}, u32[]{:S(2)}, u32[]{:S(2)}) %all-to-all-start.9) | async-done | bytes 524320 | tf_op jit(solution)/shard_map/all_to_all | solution.py:28
  224.5 26.7 %collective-permute-start.6 = (bf16[2,4,64,768]{3,2,1,0:T(8,128)(2,1)}, bf16[2,4,64,768]{3,2,1,0:T(8,128)(2,1)}, u32[]{:S(2)}, u32[]{:S(2)}) collective-permute-start(bf16[2,4,64,768]{3,2,1,0:T(8,128)(2,1)} %get-tuple-element.15), channel_id=1, source_target_pairs={{0,16},{16,0},{1,17},{17,1},{2,18},{18,2},{3,19},{19,3},{4,20},{20... | collective-permute-start | bytes 2359304 | tf_op jit(solution)/shard_map/ppermute | solution.py:33
  252.7 3.6 %all-to-all-start.10 = ((bf16[16,16,1024]{2,1,0:T(8,128)(2,1)}), bf16[16,16,1024]{2,1,0:T(8,128)(2,1)S(1)}, u32[]{:S(2)}, u32[]{:S(2)}) async-start(bf16[16,16,1024]{2,1,0:T(8,128)(2,1)} %bitcast.41), calls=%async_computation.10 | async-start | bytes 1048576 | tf_op jit(solution)/shard_map/all_to_all | solution.py:21
  256.6 2.8 collective-permute-start.4
  263.0 2.7 collective-permute-start.9
  268.2 5.0 %all-to-all-done.10 = bf16[16,16,1024]{2,1,0:T(8,128)(2,1)S(1)} async-done(((bf16[16,16,1024]{2,1,0:T(8,128)(2,1)}), bf16[16,16,1024]{2,1,0:T(8,128)(2,1)S(1)}, u32[]{:S(2)}, u32[]{:S(2)}) %all-to-all-start.10) | async-done | bytes 524320 | tf_op jit(solution)/shard_map/all_to_all | solution.py:21
  274.2 7.1 %all-to-all-start.11 = ((bf16[16,16,1024]{2,1,0:T(8,128)(2,1)}), bf16[16,16,1024]{2,1,0:T(8,128)(2,1)S(1)}, u32[]{:S(2)}, u32[]{:S(2)}) async-start(bf16[16,16,1024]{2,1,0:T(8,128)(2,1)} %broadcast_in_dim.17), calls=%async_computation.11 | async-start | bytes 1048576 | tf_op jit(solution)/shard_map/all_to_all | solution.py:28
  283.1 11.8 %collective-permute-done.10 = bf16[64,768]{1,0:T(8,128)(2,1)S(1)} collective-permute-done((bf16[64,768]{1,0:T(8,128)(2,1)S(1)}, bf16[64,768]{1,0:T(8,128)(2,1)S(1)}, u32[]{:S(2)}, u32[]{:S(2)}) %collective-permute-start.10) | collective-permute-done | bytes 98336 | tf_op jit(solution)/shard_map/ppermute | solution.py:33
  309.5 4.9 %all-to-all-start.12 = ((bf16[16,64,256]{2,1,0:T(8,128)(2,1)}), bf16[16,64,256]{2,1,0:T(8,128)(2,1)S(1)}, u32[]{:S(2)}, u32[]{:S(2)}) async-start(bf16[16,64,256]{2,1,0:T(8,128)(2,1)} %bitcast.44), calls=%async_computation.12 | async-start | bytes 1048576 | tf_op jit(solution)/shard_map/all_to_all | solution.py:21
  317.2 6.4 %collective-permute-done.15 = bf16[64,512]{1,0:T(8,128)(2,1)S(1)} collective-permute-done((bf16[64,512]{1,0:T(8,128)(2,1)S(1)}, bf16[64,512]{1,0:T(8,128)(2,1)S(1)}, u32[]{:S(2)}, u32[]{:S(2)}) %collective-permute-start.15) | collective-permute-done | bytes 65568 | tf_op jit(solution)/shard_map/ppermute | solution.py:33
  (266 shorter events, 67.6 us)
Async XLA Ops:
  4.8 26.4 %all-to-all-start = ((bf16[16,16,1024]{2,1,0:T(8,128)(2,1)}), bf16[16,16,1024]{2,1,0:T(8,128)(2,1)S(1)}, u32[]{:S(2)}, u32[]{:S(2)}) async-start(bf16[16,16,1024]{2,1,0:T(8,128)(2,1)} %bitcast.3), calls=%async_computation | async-start | bytes 1048576 | tf_op jit(solution)/shard_map/all_to_all | solution.py:21
  113.7 14.9 %all-to-all-start.5 = ((bf16[16,16,1024]{2,1,0:T(8,128)(2,1)}), bf16[16,16,1024]{2,1,0:T(8,128)(2,1)S(1)}, u32[]{:S(2)}, u32[]{:S(2)}) async-start(bf16[16,16,1024]{2,1,0:T(8,128)(2,1)} %broadcast_in_dim.14), calls=%async_computation.5 | async-start | bytes 1048576 | tf_op jit(solution)/shard_map/all_to_all | solution.py:28
  132.4 17.9 %all-to-all-start.6 = ((bf16[16,16,1024]{2,1,0:T(8,128)(2,1)}), bf16[16,16,1024]{2,1,0:T(8,128)(2,1)S(1)}, u32[]{:S(2)}, u32[]{:S(2)}) async-start(bf16[16,16,1024]{2,1,0:T(8,128)(2,1)} %bitcast.230), calls=%async_computation.6 | async-start | bytes 1048576 | tf_op jit(solution)/shard_map/all_to_all | solution.py:21
  138.4 8.3 %collective-permute-start.2 = (bf16[256,256]{1,0:T(8,128)(2,1)}, bf16[256,256]{1,0:T(8,128)(2,1)S(1)}, u32[]{:S(2)}, u32[]{:S(2)}) collective-permute-start(bf16[256,256]{1,0:T(8,128)(2,1)} %get-tuple-element.38), channel_id=1, source_target_pairs={{0,3},{1,0},{2,1},{3,2},{4,7},{5,4},{6,5},{7,6},{8,11},{9,8},{10,9... | collective-permute-start | bytes 393224 | tf_op jit(solution)/shard_map/ppermute | solution.py:38
  141.0 7.1 %collective-permute-start.1 = (bf16[256,256]{1,0:T(8,128)(2,1)}, bf16[256,256]{1,0:T(8,128)(2,1)}, u32[]{:S(2)}, u32[]{:S(2)}) collective-permute-start(bf16[256,256]{1,0:T(8,128)(2,1)} %get-tuple-element.39), channel_id=1, source_target_pairs={{0,2},{1,3},{2,0},{3,1},{4,6},{5,7},{6,4},{7,5},{8,10},{9,11},{10,... | collective-permute-start | bytes 393224 | tf_op jit(solution)/shard_map/ppermute | solution.py:38
  141.5 7.8 %collective-permute-start = (bf16[256,256]{1,0:T(8,128)(2,1)S(1)}, bf16[256,256]{1,0:T(8,128)(2,1)}, u32[]{:S(2)}, u32[]{:S(2)}) collective-permute-start(bf16[256,256]{1,0:T(8,128)(2,1)S(1)} %get-tuple-element.37), channel_id=1, source_target_pairs={{0,1},{1,2},{2,3},{3,0},{4,5},{5,6},{6,7},{7,4},{8,9},{9,10},{10,1... | collective-permute-start | bytes 393224 | tf_op jit(solution)/shard_map/ppermute | solution.py:38
  151.4 22.0 %all-to-all-start.7 = ((bf16[16,16,1280]{2,1,0:T(8,128)(2,1)}), bf16[16,16,1280]{2,1,0:T(8,128)(2,1)S(1)}, u32[]{:S(2)}, u32[]{:S(2)}) async-start(bf16[16,16,1280]{2,1,0:T(8,128)(2,1)} %pad_maximum_fusion.2), calls=%async_computation.7 | async-start | bytes 1310720 | tf_op jit(solution)/shard_map/all_to_all | solution.py:161
  201.6 16.7 %all-to-all-start.9 = ((bf16[16,16,1024]{2,1,0:T(8,128)(2,1)}), bf16[16,16,1024]{2,1,0:T(8,128)(2,1)S(1)}, u32[]{:S(2)}, u32[]{:S(2)}) async-start(bf16[16,16,1024]{2,1,0:T(8,128)(2,1)} %broadcast_in_dim.16), calls=%async_computation.9 | async-start | bytes 1048576 | tf_op jit(solution)/shard_map/all_to_all | solution.py:28
  224.5 36.4 %collective-permute-start.6 = (bf16[2,4,64,768]{3,2,1,0:T(8,128)(2,1)}, bf16[2,4,64,768]{3,2,1,0:T(8,128)(2,1)}, u32[]{:S(2)}, u32[]{:S(2)}) collective-permute-start(bf16[2,4,64,768]{3,2,1,0:T(8,128)(2,1)} %get-tuple-element.15), channel_id=1, source_target_pairs={{0,16},{16,0},{1,17},{17,1},{2,18},{18,2},{3,19},{19,3},{4,20},{20... | collective-permute-start | bytes 2359304 | tf_op jit(solution)/shard_map/ppermute | solution.py:33
  252.7 20.5 %all-to-all-start.10 = ((bf16[16,16,1024]{2,1,0:T(8,128)(2,1)}), bf16[16,16,1024]{2,1,0:T(8,128)(2,1)S(1)}, u32[]{:S(2)}, u32[]{:S(2)}) async-start(bf16[16,16,1024]{2,1,0:T(8,128)(2,1)} %bitcast.41), calls=%async_computation.10 | async-start | bytes 1048576 | tf_op jit(solution)/shard_map/all_to_all | solution.py:21
  256.6 9.5 %collective-permute-start.4 = (bf16[256,256]{1,0:T(8,128)(2,1)S(1)}, bf16[256,256]{1,0:T(8,128)(2,1)S(1)}, u32[]{:S(2)}, u32[]{:S(2)}) collective-permute-start(bf16[256,256]{1,0:T(8,128)(2,1)S(1)} %bitcast.240), channel_id=1, source_target_pairs={{0,2},{1,3},{2,0},{3,1},{4,6},{5,7},{6,4},{7,5},{8,10},{9,11},{10,... | collective-permute-start | bytes 393224 | tf_op jit(solution)/shard_map/ppermute | solution.py:38
  259.4 7.4 %collective-permute-start.5 = (bf16[256,256]{1,0:T(8,128)(2,1)S(1)}, bf16[256,256]{1,0:T(8,128)(2,1)S(1)}, u32[]{:S(2)}, u32[]{:S(2)}) collective-permute-start(bf16[256,256]{1,0:T(8,128)(2,1)S(1)} %bitcast.241), channel_id=1, source_target_pairs={{0,3},{1,0},{2,1},{3,2},{4,7},{5,4},{6,5},{7,6},{8,11},{9,8},{10,9... | collective-permute-start | bytes 393224 | tf_op jit(solution)/shard_map/ppermute | solution.py:38
  260.3 7.0 %collective-permute-start.3 = (bf16[256,256]{1,0:T(8,128)(2,1)S(1)}, bf16[256,256]{1,0:T(8,128)(2,1)S(1)}, u32[]{:S(2)}, u32[]{:S(2)}) collective-permute-start(bf16[256,256]{1,0:T(8,128)(2,1)S(1)} %bitcast.242), channel_id=1, source_target_pairs={{0,1},{1,2},{2,3},{3,0},{4,5},{5,6},{6,7},{7,4},{8,9},{9,10},{10,1... | collective-permute-start | bytes 393224 | tf_op jit(solution)/shard_map/ppermute | solution.py:38
  263.0 18.3 %collective-permute-start.9 = (bf16[2,64,768]{2,1,0:T(8,128)(2,1)}, bf16[2,64,768]{2,1,0:T(8,128)(2,1)}, u32[]{:S(2)}, u32[]{:S(2)}) collective-permute-start(bf16[2,64,768]{2,1,0:T(8,128)(2,1)} %get-tuple-element.20), channel_id=1, source_target_pairs={{0,96},{32,0},{64,32},{96,64},{1,97},{33,1},{65,33},{97,65},{2,98}... | collective-permute-start | bytes 589832 | tf_op jit(solution)/shard_map/ppermute | solution.py:38
  265.8 15.6 %collective-permute-start.8 = (bf16[2,64,768]{2,1,0:T(8,128)(2,1)}, bf16[2,64,768]{2,1,0:T(8,128)(2,1)}, u32[]{:S(2)}, u32[]{:S(2)}) collective-permute-start(bf16[2,64,768]{2,1,0:T(8,128)(2,1)} %get-tuple-element.21), channel_id=1, source_target_pairs={{0,64},{32,96},{64,0},{96,32},{1,65},{33,97},{65,1},{97,33},{2,66}... | collective-permute-start | bytes 589832 | tf_op jit(solution)/shard_map/ppermute | solution.py:38
  266.1 15.2 %collective-permute-start.7 = (bf16[2,64,768]{2,1,0:T(8,128)(2,1)}, bf16[2,64,768]{2,1,0:T(8,128)(2,1)}, u32[]{:S(2)}, u32[]{:S(2)}) collective-permute-start(bf16[2,64,768]{2,1,0:T(8,128)(2,1)} %get-tuple-element.19), channel_id=1, source_target_pairs={{0,32},{32,64},{64,96},{96,0},{1,33},{33,65},{65,97},{97,1},{2,34}... | collective-permute-start | bytes 589832 | tf_op jit(solution)/shard_map/ppermute | solution.py:38
  274.2 23.6 %all-to-all-start.11 = ((bf16[16,16,1024]{2,1,0:T(8,128)(2,1)}), bf16[16,16,1024]{2,1,0:T(8,128)(2,1)S(1)}, u32[]{:S(2)}, u32[]{:S(2)}) async-start(bf16[16,16,1024]{2,1,0:T(8,128)(2,1)} %broadcast_in_dim.17), calls=%async_computation.11 | async-start | bytes 1048576 | tf_op jit(solution)/shard_map/all_to_all | solution.py:28
  282.6 12.3 %collective-permute-start.10 = (bf16[64,768]{1,0:T(8,128)(2,1)S(1)}, bf16[64,768]{1,0:T(8,128)(2,1)S(1)}, u32[]{:S(2)}, u32[]{:S(2)}) collective-permute-start(bf16[64,768]{1,0:T(8,128)(2,1)S(1)} %dynamic-slice_bitcast_fusion.11), channel_id=1, source_target_pairs={{0,128},{128,0},{1,129},{129,1},{2,130},{130,2},{3,131},{131,3},{4... | collective-permute-start | bytes 294920 | tf_op jit(solution)/shard_map/ppermute | solution.py:33
  301.6 2.6 collective-permute-start.11
  304.4 10.0 %collective-permute-start.14 = (bf16[2,64,512]{2,1,0:T(8,128)(2,1)S(1)}, bf16[2,64,512]{2,1,0:T(8,128)(2,1)S(1)}, u32[]{:S(2)}, u32[]{:S(2)}) collective-permute-start(bf16[2,64,512]{2,1,0:T(8,128)(2,1)S(1)} %get-tuple-element.31), channel_id=1, source_target_pairs={{0,96},{32,0},{64,32},{96,64},{1,97},{33,1},{65,33},{97,65},{2,98}... | collective-permute-start | bytes 393224 | tf_op jit(solution)/shard_map/ppermute | solution.py:38
  307.1 7.3 %collective-permute-start.13 = (bf16[2,64,512]{2,1,0:T(8,128)(2,1)S(1)}, bf16[2,64,512]{2,1,0:T(8,128)(2,1)S(1)}, u32[]{:S(2)}, u32[]{:S(2)}) collective-permute-start(bf16[2,64,512]{2,1,0:T(8,128)(2,1)S(1)} %get-tuple-element.32), channel_id=1, source_target_pairs={{0,64},{32,96},{64,0},{96,32},{1,65},{33,97},{65,1},{97,33},{2,66}... | collective-permute-start | bytes 393224 | tf_op jit(solution)/shard_map/ppermute | solution.py:38
  307.6 9.3 %collective-permute-start.12 = (bf16[2,64,512]{2,1,0:T(8,128)(2,1)S(1)}, bf16[2,64,512]{2,1,0:T(8,128)(2,1)S(1)}, u32[]{:S(2)}, u32[]{:S(2)}) collective-permute-start(bf16[2,64,512]{2,1,0:T(8,128)(2,1)S(1)} %get-tuple-element.30), channel_id=1, source_target_pairs={{0,32},{32,64},{64,96},{96,0},{1,33},{33,65},{65,97},{97,1},{2,34}... | collective-permute-start | bytes 393224 | tf_op jit(solution)/shard_map/ppermute | solution.py:38
  309.5 14.9 %all-to-all-start.12 = ((bf16[16,64,256]{2,1,0:T(8,128)(2,1)}), bf16[16,64,256]{2,1,0:T(8,128)(2,1)S(1)}, u32[]{:S(2)}, u32[]{:S(2)}) async-start(bf16[16,64,256]{2,1,0:T(8,128)(2,1)} %bitcast.44), calls=%async_computation.12 | async-start | bytes 1048576 | tf_op jit(solution)/shard_map/all_to_all | solution.py:21
  317.0 6.7 %collective-permute-start.15 = (bf16[64,512]{1,0:T(8,128)(2,1)S(1)}, bf16[64,512]{1,0:T(8,128)(2,1)S(1)}, u32[]{:S(2)}, u32[]{:S(2)}) collective-permute-start(bf16[64,512]{1,0:T(8,128)(2,1)S(1)} %dynamic-slice_bitcast_fusion.12), channel_id=1, source_target_pairs={{0,128},{128,0},{1,129},{129,1},{2,130},{130,2},{3,131},{131,3},{4... | collective-permute-start | bytes 196616 | tf_op jit(solution)/shard_map/ppermute | solution.py:33
  (55 other events, 356.3 us)

commit v3 on v1

--- a/solution.py
+++ b/solution.py
@@ -4,11 +4,12 @@
 from jax.sharding import Mesh
 from jax.sharding import PartitionSpec as P
 
+
 HD = 64
 SLATE = 256
 LAYERS = 2
 DP = ("z_lo", "y", "core")
-MP = "mp"
+MP = ("z_hi", "x")
 
 epsilon = 1e-06
 bf16 = jnp.bfloat16
@@ -27,6 +28,49 @@
     copies = jnp.broadcast_to(x[None], (n, *x.shape))
     blocks = lax.all_to_all(copies, axis, 0, 0, tiled=True)
     return blocks.reshape(n * x.shape[0], x.shape[1])
+
+
+def after(x, *others):
+    return lax.optimization_barrier((x, *others))[0]
+
+
+def swapped(x, axis):
+    return lax.ppermute(x, axis, [(0, 1), (1, 0)])
+
+
+def moved(x, axis, step):
+    n = lax.axis_size(axis)
+    return lax.ppermute(x, axis, [(k, (k + step) % n) for k in range(n)])
+
+
+def pick(x, index):
+    return lax.dynamic_index_in_dim(x, index, 0, keepdims=False)
+
+
+def core_stage(grads):
+    rows, _ = grads[0].shape
+    joined = jnp.concatenate([g.astype(bf16) for g in grads], axis=1)
+    parts = joined.reshape(8, 2, rows // 16, cols_of(grads))
+    return pair_parts(jnp.moveaxis(parts, 1, 0), "core")
+
+
+def cols_of(arrays):
+    return sum(a.shape[1] for a in arrays)
+
+
+def pair_parts(x, axis):
+    here = lax.axis_index(axis)
+    return pick(x, here), swapped(pick(x, 1 - here), axis)
+
+
+def total(parts):
+    return sum(p.astype(f32) for p in parts)
+
+
+def y_stage(parts):
+    parts = jnp.moveaxis(parts.reshape(2, 4, *parts.shape[1:]), 1, 0)
+    here = lax.axis_index("y")
+    return [pick(parts, here)] + [moved(pick(parts, (here + k) % 4), "y", k) for k in range(1, 4)]
 
 
 def normalize(stream):
@@ -75,7 +119,7 @@
     return jnp.concatenate([grad_query, grad_key, grad_value], axis=1)
 
 
-def body(tokens, lengths, cotangent, triple_weight, output_weight, upward_weight, downward_weight):
+def step(tokens, lengths, cotangent, triple_weight, output_weight, upward_weight, downward_weight):
     rows, width = tokens.shape
     n = lax.axis_size(MP)
     share = rows // n
@@ -107,63 +151,95 @@
             stream_part = (mid_part.astype(f32) + share_rows(partial_ffn, MP)).astype(bf16)
             stream = all_rows(stream_part, MP)
 
-    reduced = [None] * LAYERS
-    early = []
-    upstream, upstream_part = cotangent, part(cotangent)
-    for l in reversed(range(LAYERS)):
-        (normed, scaled, rscale, queries, key_rows, values, probs, context,
-         scaled_mid, rscale_mid, normed_mid, preact, activated) = saved[l]
-        grad_act = jnp.dot(upstream, downward_weight[l], preferred_element_type=f32).astype(bf16)
-        _, gate_back = jax.vjp(smooth_gate, preact)
-        grad_preact = gate_back(grad_act.astype(f32))[0].astype(bf16)
-        partial = contract_cols(grad_preact, upward_weight[l]).astype(bf16)
-        if l + 1 == LAYERS:
-            both = share_rows(jnp.concatenate([partial, partial_ffn], axis=1), MP)
-            final_part = (mid_part.astype(f32) + both[:, width:]).astype(bf16)
-            both = all_rows(jnp.concatenate([both[:, :width].astype(bf16), final_part], axis=1), MP)
-            grad_normed, final_stream = both[:, :width].astype(f32), both[:, width:]
-        else:
-            grad_normed = all_rows(share_rows(partial, MP).astype(bf16), MP).astype(f32)
-        downward_grad = contract_rows(upstream, activated)
-        upward_grad = contract_rows(normed_mid, grad_preact)
-        grad_mid = (upstream.astype(f32) + norm_backward(scaled_mid, rscale_mid, grad_normed)).astype(bf16)
-        output_grad = contract_rows(grad_mid, context)
-        grad_context = jnp.dot(grad_mid, output_weight[l], preferred_element_type=f32).astype(bf16)
-        grad_qkv = attend_backward(probs, queries, key_rows, values, grad_context)
-        triple_grad = contract_rows(normed, grad_qkv)
-        early.append([upward_grad, downward_grad])
-        late = [triple_grad, output_grad]
-        if l > 0:
-            early[-1] += late
-            grad_input = all_rows(
-                share_rows(contract_cols(grad_qkv, triple[l]).astype(bf16), MP).astype(bf16), MP
-            ).astype(f32)
-            upstream = (grad_mid.astype(f32) + norm_backward(scaled, rscale, grad_input)).astype(bf16)
-
-    def over_slates(grads):
-        joined = jnp.concatenate([g.astype(bf16) for g in grads], axis=1)
-        summed = share_rows(joined, DP)
-        out, at = [], 0
-        for g in grads:
-            out.append(summed[:, at : at + g.shape[1]])
-            at += g.shape[1]
-        return out
-
-    up1, down1, triple1, out1 = over_slates(early[0])
-    up0, down0 = over_slates(early[1])
-    triple0, out0 = over_slates(late)
+    top = LAYERS - 1
+    quarter = width // 4
     heads = triple_weight.shape[-1]
+    x_here = lax.axis_index("x")
+
+    (normed, scaled, rscale, queries, key_rows, values, probs, context,
+     scaled_mid, rscale_mid, normed_mid, preact, activated) = saved[top]
+    upstream = cotangent
+    grad_act = jnp.dot(upstream, downward_weight[top], preferred_element_type=f32).astype(bf16)
+    _, gate_back = jax.vjp(smooth_gate, preact)
+    grad_preact = gate_back(grad_act.astype(f32))[0].astype(bf16)
+    partial = contract_cols(grad_preact, upward_weight[top]).astype(bf16)
+    shares = jnp.stack([partial_ffn[:, k * quarter : (k + 1) * quarter] for k in range(4)])
+    shares = [pick(shares, x_here)] + [
+        moved(pick(shares, (x_here + k) % 4), "x", k) for k in range(1, 4)
+    ]
+    own = share_rows(partial, MP).astype(bf16)
+    shares = total(shares).astype(bf16).reshape(n, share, quarter)
+    sent = jnp.concatenate([jnp.broadcast_to(own[None], (n, share, width)), shares], axis=2)
+    came = lax.all_to_all(after(sent, rscale_mid), MP, 0, 0, tiled=True)
+    grad_normed = came[:, :, :width].reshape(rows, width).astype(f32)
+    ffn_part = jnp.sum(came[:, :, width:].reshape(4, 4, share, quarter).astype(f32), axis=0)
+    ffn_part = jnp.concatenate([ffn_part[k] for k in range(4)], axis=1)
+    final_part = (mid_part.astype(f32) + ffn_part).astype(bf16)
+    grad_mid = (upstream.astype(f32) + norm_backward(scaled_mid, rscale_mid, grad_normed)).astype(bf16)
+    grad_context = jnp.dot(grad_mid, output_weight[top], preferred_element_type=f32).astype(bf16)
+    grad_qkv = attend_backward(probs, queries, key_rows, values, grad_context)
+    partial = contract_cols(grad_qkv, triple[top]).astype(bf16).reshape(n, share, width)
+    quarters = jnp.stack([final_part[:, k * quarter : (k + 1) * quarter] for k in range(4)])
+    sent = jnp.concatenate([partial, jnp.tile(quarters, (4, 1, 1))], axis=2)
+    came = lax.all_to_all(sent, MP, 0, 0, tiled=True)
+    own = jnp.sum(came[:, :, :width].astype(f32), axis=0).astype(bf16)
+    column = came[:, :, width:].reshape(rows, quarter)
+    wide1 = [
+        contract_rows(normed_mid, grad_preact),
+        contract_rows(upstream, activated),
+        contract_rows(normed, grad_qkv),
+        contract_rows(grad_mid, context),
+    ]
+    sums1 = core_stage(wide1)
+    grad_input = all_rows(after(own, rscale, sums1[0]), MP).astype(f32)
+    sums1 = y_stage(total(sums1).astype(bf16))
+    grad_input = after(grad_input, sums1[0])
+    upstream = (grad_mid.astype(f32) + norm_backward(scaled, rscale, grad_input)).astype(bf16)
+    (normed, scaled, rscale, queries, key_rows, values, probs, context,
+     scaled_mid, rscale_mid, normed_mid, preact, activated) = saved[0]
+    grad_act = jnp.dot(upstream, downward_weight[0], preferred_element_type=f32).astype(bf16)
+    _, gate_back = jax.vjp(smooth_gate, preact)
+    grad_preact = gate_back(grad_act.astype(f32))[0].astype(bf16)
+    partial = contract_cols(grad_preact, upward_weight[0]).astype(bf16)
+    own = share_rows(partial, MP).astype(bf16)
+    wide0 = [contract_rows(normed_mid, grad_preact), contract_rows(upstream, activated)]
+    sums0 = core_stage(wide0)
+    sums1 = pair_parts(total(sums1).astype(bf16), "z_lo")
+    grad_normed = all_rows(after(own, rscale_mid, sums0[0], sums1[0]), MP).astype(f32)
+    sums0 = y_stage(total(sums0).astype(bf16))
+    grad_normed = after(grad_normed, sums0[0])
+    grad_mid = (upstream.astype(f32) + norm_backward(scaled_mid, rscale_mid, grad_normed)).astype(bf16)
+    grad_context = jnp.dot(grad_mid, output_weight[0], preferred_element_type=f32).astype(bf16)
+    grad_qkv = attend_backward(probs, queries, key_rows, values, grad_context)
+    late = [contract_rows(normed, grad_qkv), contract_rows(grad_mid, context)]
+    late = jnp.concatenate([g.astype(bf16) for g in late], axis=1)
+    column = after(column, late)
+    columns = [column] + [moved(column, "x", step) for step in range(1, 4)]
+    late = share_rows(late, DP)
+    sums0 = pair_parts(total(sums0).astype(bf16), "z_lo")
+    final_stream = jnp.concatenate(
+        [lax.select_n((x_here - k) % 4, *columns) for k in range(4)], axis=1
+    )
+    sums1, sums0 = total(sums1), total(sums0)
+
+    def cut(x, first, size):
+        return x[:, first : first + size]
+
+    ff = upward_weight.shape[-1]
     return (
         final_stream,
-        jnp.stack([t.reshape(t.shape[0], 3, heads) for t in (triple0, triple1)]),
-        jnp.stack([out0, out1]),
-        jnp.stack([up0, up1]),
-        jnp.stack([down0, down1]),
+        jnp.stack([
+            cut(late, 0, 3 * heads).reshape(-1, 3, heads),
+            cut(sums1, 2 * ff, 3 * heads).reshape(-1, 3, heads),
+        ]),
+        jnp.stack([cut(late, 3 * heads, heads), cut(sums1, 2 * ff + 3 * heads, heads)]),
+        jnp.stack([cut(sums0, 0, ff), cut(sums1, 0, ff)]),
+        jnp.stack([cut(sums0, ff, ff), cut(sums1, ff, ff)]),
     )
 
 
 def solution(mesh):
-    torus = Mesh(mesh.devices.reshape(2, 4, 2, mesh.shape["mp"]), (*DP, MP))
+    torus = Mesh(mesh.devices.reshape(2, 4, 2, 4, 4), (*DP, *MP))
     placed = (
         P(DP, None),
         P(DP),
@@ -174,7 +250,7 @@
         P(None, None, MP),
     )
     return jax.shard_map(
-        body,
+        step,
         mesh=torus,
         in_specs=placed,
         out_specs=(

time: 365 us -> 325 us (0.89)
  blocking collectives: 148 us -> 77.8 us
  starting transfers between devices: 72.9 us -> 106 us
  waiting for transfers between devices: 97.7 us -> 84.2 us
  other arithmetic: 13.3 us -> 20.5 us
  matrix products: 11.5 us -> 16.5 us
    all_to_all x5 -> x2, blocking collectives: 91.6 us -> 35.9 us  [share_rows(): blocks = lax.all_to_all(blocks, axis, 0, 0, tiled=True)]
    ppermute x0 -> x16, waiting for transfers between devices: none -> 41.7 us  [the longest x12 30.7 us: moved(): return lax.ppermute(x, axis, [(k, (k + step) % n) for k in range(n)])]
    ppermute x0 -> x16, starting transfers between devices: none -> 41.6 us  [the longest x4 31 us: swapped(): return lax.ppermute(x, axis, [(0, 1), (1, 0)])]
    all_to_all x3, waiting for transfers between devices: 47.9 us -> 12.2 us  [all_rows(): blocks = lax.all_to_all(copies, axis, 0, 0, tiled=True)]
    all_to_all x4, waiting for transfers between devices: 49.8 us -> 16.2 us  [share_rows(): blocks = lax.all_to_all(blocks, axis, 0, 0, tiled=True)]
    all_to_all x4, starting transfers between devices: 59.1 us -> 34.4 us  [share_rows(): blocks = lax.all_to_all(blocks, axis, 0, 0, tiled=True)]
    all_to_all x3 -> x2, blocking collectives: 56.1 us -> 41.9 us  [all_rows(): blocks = lax.all_to_all(copies, axis, 0, 0, tiled=True)]
    all_to_all x0 -> x2, waiting for transfers between devices: none -> 14.1 us  [the longest x1 14.1 us: step(): came = lax.all_to_all(after(sent, rscale_mid), MP, 0, 0, tiled=True)]
  transfers between devices with their start and end apart: 7 -> 25, of which waited for: 7 -> 19; matrix products, arithmetic and copies ran while one was open for 3% -> 7% of each run, Pallas kernels for 0% -> 0%
where the time goes in v3:
time: 325 us; the launch traced here: 324 us
  starting transfers between devices  106 us (33%)
  waiting for transfers between devices  84.2 us (26%)
  blocking collectives  77.8 us (24%)
  other arithmetic  20.5 us (6%)
  local copies, waits for them, and re-layouts  16.5 us (5%)
  matrix products  16.5 us (5%)
    all_to_all x2, blocking collectives, all_rows(): blocks = lax.all_to_all(copies, axis, 0, 0, tiled=True)  41.9 us
    all_to_all x2, blocking collectives, share_rows(): blocks = lax.all_to_all(blocks, axis, 0, 0, tiled=True)  35.9 us
    all_to_all x4, starting transfers between devices, share_rows(): blocks = lax.all_to_all(blocks, axis, 0, 0, tiled=True)  34.4 us
    ppermute x4, starting transfers between devices, swapped(): return lax.ppermute(x, axis, [(0, 1), (1, 0)])  31 us
    ppermute x12, waiting for transfers between devices, moved(): return lax.ppermute(x, axis, [(k, (k + step) % n) for k in range(n)])  30.7 us
    all_to_all x3, starting transfers between devices, all_rows(): blocks = lax.all_to_all(copies, axis, 0, 0, tiled=True)  19.4 us
    all_to_all x4, waiting for transfers between devices, share_rows(): blocks = lax.all_to_all(blocks, axis, 0, 0, tiled=True)  16.2 us
    all_to_all x1, waiting for transfers between devices, step(): came = lax.all_to_all(after(sent, rscale_mid), MP, 0, 0, tiled=True)  14.1 us
  transfers between devices with their start and end apart: 25, of which 19 were waited for; matrix products, arithmetic and copies ran while one was open for 7% of the time, Pallas kernels for 0%

profile of v3, /device:TPU:1, one launch (start us, length us, event | category | flops | bytes accessed | tf_op | source)
XLA Modules:
  0.0 323.7 jit_solution(8166228984769891707)
XLA Ops:
  5.4 11.6 %all-to-all-start = ((bf16[16,16,1024]{2,1,0:T(8,128)(2,1)}), bf16[16,16,1024]{2,1,0:T(8,128)(2,1)S(1)}, u32[]{:S(2)}, u32[]{:S(2)}) async-start(bf16[16,16,1024]{2,1,0:T(8,128)(2,1)} %bitcast.3), calls=%async_computation | async-start | bytes 1048576 | tf_op jit(solution)/shard_map/all_to_all | solution.py:22
  16.9 14.9 %all-to-all-done = bf16[16,16,1024]{2,1,0:T(8,128)(2,1)S(1)} async-done(((bf16[16,16,1024]{2,1,0:T(8,128)(2,1)}), bf16[16,16,1024]{2,1,0:T(8,128)(2,1)S(1)}, u32[]{:S(2)}, u32[]{:S(2)}) %all-to-all-start) | async-done | bytes 524320 | tf_op jit(solution)/shard_map/all_to_all | solution.py:22
  32.0 23.9 %all_to_all.65 = bf16[16,16,1024]{2,1,0:T(8,128)(2,1)S(1)} all-to-all(bf16[16,16,1024]{2,1,0:T(8,128)(2,1)S(1)} %broadcast_in_dim.12), channel_id=1, replica_groups=mesh['z_lo'=2,'y'=4,'core'=2,'z_hi'=4,'x'=4] {'z_hi','x'}, dimensions={0} | all-to-all | bytes 1048576 | tf_op jit(solution)/shard_map/all_to_all | solution.py:29
  57.5 18.9 %all_to_all.66 = bf16[16,16,1024]{2,1,0:T(8,128)(2,1)S(1)} all-to-all(bf16[16,16,1024]{2,1,0:T(8,128)(2,1)S(1)} %bitcast.231), channel_id=1, replica_groups=mesh['z_lo'=2,'y'=4,'core'=2,'z_hi'=4,'x'=4] {'z_hi','x'}, dimensions={0} | all-to-all | bytes 1048576 | tf_op jit(solution)/shard_map/all_to_all | solution.py:22
  76.6 18.0 %all_to_all.67 = bf16[16,16,1024]{2,1,0:T(8,128)(2,1)S(1)} all-to-all(bf16[16,16,1024]{2,1,0:T(8,128)(2,1)S(1)} %broadcast_in_dim.13), channel_id=1, replica_groups=mesh['z_lo'=2,'y'=4,'core'=2,'z_hi'=4,'x'=4] {'z_hi','x'}, dimensions={0} | all-to-all | bytes 1048576 | tf_op jit(solution)/shard_map/all_to_all | solution.py:29
  97.0 17.0 %all_to_all.68 = bf16[16,16,1024]{2,1,0:T(8,128)(2,1)S(1)} all-to-all(bf16[16,16,1024]{2,1,0:T(8,128)(2,1)S(1)} %bitcast.228), channel_id=1, replica_groups=mesh['z_lo'=2,'y'=4,'core'=2,'z_hi'=4,'x'=4] {'z_hi','x'}, dimensions={0} | all-to-all | bytes 1048576 | tf_op jit(solution)/shard_map/all_to_all | solution.py:22
  115.0 3.7 %all-to-all-start.5 = ((bf16[16,16,1024]{2,1,0:T(8,128)(2,1)}), bf16[16,16,1024]{2,1,0:T(8,128)(2,1)S(1)}, u32[]{:S(2)}, u32[]{:S(2)}) async-start(bf16[16,16,1024]{2,1,0:T(8,128)(2,1)} %broadcast_in_dim.14), calls=%async_computation.5 | async-start | bytes 1048576 | tf_op jit(solution)/shard_map/all_to_all | solution.py:29
  118.7 11.3 %all-to-all-done.5 = bf16[16,16,1024]{2,1,0:T(8,128)(2,1)S(1)} async-done(((bf16[16,16,1024]{2,1,0:T(8,128)(2,1)}), bf16[16,16,1024]{2,1,0:T(8,128)(2,1)S(1)}, u32[]{:S(2)}, u32[]{:S(2)}) %all-to-all-start.5) | async-done | bytes 524320 | tf_op jit(solution)/shard_map/all_to_all | solution.py:29
  133.9 3.7 %all-to-all-start.6 = ((bf16[16,16,1024]{2,1,0:T(8,128)(2,1)}), bf16[16,16,1024]{2,1,0:T(8,128)(2,1)S(1)}, u32[]{:S(2)}, u32[]{:S(2)}) async-start(bf16[16,16,1024]{2,1,0:T(8,128)(2,1)} %bitcast.224), calls=%async_computation.6 | async-start | bytes 1048576 | tf_op jit(solution)/shard_map/all_to_all | solution.py:22
  139.9 2.6 collective-permute-start.2
  143.7 4.9 %collective-permute-done.2 = bf16[256,256]{1,0:T(8,128)(2,1)S(1)} collective-permute-done((bf16[256,256]{1,0:T(8,128)(2,1)}, bf16[256,256]{1,0:T(8,128)(2,1)S(1)}, u32[]{:S(2)}, u32[]{:S(2)}) %collective-permute-start.2) | collective-permute-done | bytes 131104 | tf_op jit(solution)/shard_map/ppermute | solution.py:43
  152.6 5.6 %all-to-all-start.7 = ((bf16[16,16,1280]{2,1,0:T(8,128)(2,1)}), bf16[16,16,1280]{2,1,0:T(8,128)(2,1)S(1)}, u32[]{:S(2)}, u32[]{:S(2)}) async-start(bf16[16,16,1280]{2,1,0:T(8,128)(2,1)} %pad_maximum_fusion.2), calls=%async_computation.7 | async-start | bytes 1310720 | tf_op jit(solution)/shard_map/all_to_all | solution.py:173
  160.6 14.1 %all-to-all-done.7 = bf16[16,16,1280]{2,1,0:T(8,128)(2,1)S(1)} async-done(((bf16[16,16,1280]{2,1,0:T(8,128)(2,1)}), bf16[16,16,1280]{2,1,0:T(8,128)(2,1)S(1)}, u32[]{:S(2)}, u32[]{:S(2)}) %all-to-all-start.7) | async-done | bytes 655392 | tf_op jit(solution)/shard_map/all_to_all | solution.py:173
  181.5 4.6 %all-to-all-start.8 = ((bf16[16,16,1280]{2,1,0:T(8,128)(2,1)}), bf16[16,16,1280]{2,1,0:T(8,128)(2,1)}, u32[]{:S(2)}, u32[]{:S(2)}) async-start(bf16[16,16,1280]{2,1,0:T(8,128)(2,1)} %pad_maximum_fusion.3), calls=%async_computation.8 | async-start | bytes 1310720 | tf_op jit(solution)/shard_map/all_to_all | solution.py:184
  190.8 27.8 %collective-permute-start.3 = (bf16[8,64,768]{2,1,0:T(8,128)(2,1)}, bf16[8,64,768]{2,1,0:T(8,128)(2,1)}, u32[]{:S(2)}, u32[]{:S(2)}) collective-permute-start(bf16[8,64,768]{2,1,0:T(8,128)(2,1)} %dynamic-slice_bitcast_fusion), channel_id=1, source_target_pairs={{0,16},{16,0},{1,17},{17,1},{2,18},{18,2},{3,19},{19,3},{4,20},{20... | collective-permute-start | bytes 2359304 | tf_op jit(solution)/shard_map/ppermute | solution.py:38
  225.1 9.0 %all-to-all-start.9 = ((bf16[16,16,1024]{2,1,0:T(8,128)(2,1)}), bf16[16,16,1024]{2,1,0:T(8,128)(2,1)S(1)}, u32[]{:S(2)}, u32[]{:S(2)}) async-start(bf16[16,16,1024]{2,1,0:T(8,128)(2,1)} %broadcast_in_dim.16), calls=%async_computation.9 | async-start | bytes 1048576 | tf_op jit(solution)/shard_map/all_to_all | solution.py:29
  237.6 2.6 collective-permute-done.6
  242.6 5.5 %collective-permute-done.4 = bf16[2,64,768]{2,1,0:T(8,128)(2,1)S(1)} collective-permute-done((bf16[2,64,768]{2,1,0:T(8,128)(2,1)S(1)}, bf16[2,64,768]{2,1,0:T(8,128)(2,1)S(1)}, u32[]{:S(2)}, u32[]{:S(2)}) %collective-permute-start.4) | collective-permute-done | bytes 196640 | tf_op jit(solution)/shard_map/ppermute | solution.py:43
  252.7 9.0 %all-to-all-start.10 = ((bf16[16,16,1024]{2,1,0:T(8,128)(2,1)}), bf16[16,16,1024]{2,1,0:T(8,128)(2,1)S(1)}, u32[]{:S(2)}, u32[]{:S(2)}) async-start(bf16[16,16,1024]{2,1,0:T(8,128)(2,1)} %bitcast.47), calls=%async_computation.10 | async-start | bytes 1048576 | tf_op jit(solution)/shard_map/all_to_all | solution.py:22
  264.7 8.7 %collective-permute-done.11 = bf16[64,768]{1,0:T(8,128)(2,1)S(1)} collective-permute-done((bf16[64,768]{1,0:T(8,128)(2,1)S(1)}, bf16[64,768]{1,0:T(8,128)(2,1)S(1)}, u32[]{:S(2)}, u32[]{:S(2)}) %collective-permute-start.11) | collective-permute-done | bytes 98336 | tf_op jit(solution)/shard_map/ppermute | solution.py:38
  276.9 6.7 %all-to-all-start.11 = ((bf16[16,16,1024]{2,1,0:T(8,128)(2,1)}), bf16[16,16,1024]{2,1,0:T(8,128)(2,1)S(1)}, u32[]{:S(2)}, u32[]{:S(2)}) async-start(bf16[16,16,1024]{2,1,0:T(8,128)(2,1)} %broadcast_in_dim.17), calls=%async_computation.11 | async-start | bytes 1048576 | tf_op jit(solution)/shard_map/all_to_all | solution.py:29
  289.9 3.1 collective-permute-done.12
  300.5 10.1 %all-to-all-start.12 = ((bf16[16,64,256]{2,1,0:T(8,128)(2,1)}), bf16[16,64,256]{2,1,0:T(8,128)(2,1)S(1)}, u32[]{:S(2)}, u32[]{:S(2)}) async-start(bf16[16,64,256]{2,1,0:T(8,128)(2,1)} %bitcast.59), calls=%async_computation.12 | async-start | bytes 1048576 | tf_op jit(solution)/shard_map/all_to_all | solution.py:22
  315.2 3.0 collective-permute-done.9
  (271 shorter events, 80.8 us)
Async XLA Ops:
  5.4 26.5 %all-to-all-start = ((bf16[16,16,1024]{2,1,0:T(8,128)(2,1)}), bf16[16,16,1024]{2,1,0:T(8,128)(2,1)S(1)}, u32[]{:S(2)}, u32[]{:S(2)}) async-start(bf16[16,16,1024]{2,1,0:T(8,128)(2,1)} %bitcast.3), calls=%async_computation | async-start | bytes 1048576 | tf_op jit(solution)/shard_map/all_to_all | solution.py:22
  115.0 15.0 %all-to-all-start.5 = ((bf16[16,16,1024]{2,1,0:T(8,128)(2,1)}), bf16[16,16,1024]{2,1,0:T(8,128)(2,1)S(1)}, u32[]{:S(2)}, u32[]{:S(2)}) async-start(bf16[16,16,1024]{2,1,0:T(8,128)(2,1)} %broadcast_in_dim.14), calls=%async_computation.5 | async-start | bytes 1048576 | tf_op jit(solution)/shard_map/all_to_all | solution.py:29
  133.9 17.6 %all-to-all-start.6 = ((bf16[16,16,1024]{2,1,0:T(8,128)(2,1)}), bf16[16,16,1024]{2,1,0:T(8,128)(2,1)S(1)}, u32[]{:S(2)}, u32[]{:S(2)}) async-start(bf16[16,16,1024]{2,1,0:T(8,128)(2,1)} %bitcast.224), calls=%async_computation.6 | async-start | bytes 1048576 | tf_op jit(solution)/shard_map/all_to_all | solution.py:22
  139.9 8.6 %collective-permute-start.2 = (bf16[256,256]{1,0:T(8,128)(2,1)}, bf16[256,256]{1,0:T(8,128)(2,1)S(1)}, u32[]{:S(2)}, u32[]{:S(2)}) collective-permute-start(bf16[256,256]{1,0:T(8,128)(2,1)} %get-tuple-element.50), channel_id=1, source_target_pairs={{0,3},{1,0},{2,1},{3,2},{4,7},{5,4},{6,5},{7,6},{8,11},{9,8},{10,9... | collective-permute-start | bytes 393224 | tf_op jit(solution)/shard_map/ppermute | solution.py:43
  142.5 7.0 %collective-permute-start.1 = (bf16[256,256]{1,0:T(8,128)(2,1)S(1)}, bf16[256,256]{1,0:T(8,128)(2,1)S(1)}, u32[]{:S(2)}, u32[]{:S(2)}) collective-permute-start(bf16[256,256]{1,0:T(8,128)(2,1)S(1)} %get-tuple-element.51), channel_id=1, source_target_pairs={{0,2},{1,3},{2,0},{3,1},{4,6},{5,7},{6,4},{7,5},{8,10},{9,11},{10,... | collective-permute-start | bytes 393224 | tf_op jit(solution)/shard_map/ppermute | solution.py:43
  143.1 7.5 %collective-permute-start = (bf16[256,256]{1,0:T(8,128)(2,1)S(1)}, bf16[256,256]{1,0:T(8,128)(2,1)}, u32[]{:S(2)}, u32[]{:S(2)}) collective-permute-start(bf16[256,256]{1,0:T(8,128)(2,1)S(1)} %get-tuple-element.49), channel_id=1, source_target_pairs={{0,1},{1,2},{2,3},{3,0},{4,5},{5,6},{6,7},{7,4},{8,9},{9,10},{10,1... | collective-permute-start | bytes 393224 | tf_op jit(solution)/shard_map/ppermute | solution.py:43
  152.6 22.1 %all-to-all-start.7 = ((bf16[16,16,1280]{2,1,0:T(8,128)(2,1)}), bf16[16,16,1280]{2,1,0:T(8,128)(2,1)S(1)}, u32[]{:S(2)}, u32[]{:S(2)}) async-start(bf16[16,16,1280]{2,1,0:T(8,128)(2,1)} %pad_maximum_fusion.2), calls=%async_computation.7 | async-start | bytes 1310720 | tf_op jit(solution)/shard_map/all_to_all | solution.py:173
  181.5 41.5 %all-to-all-start.8 = ((bf16[16,16,1280]{2,1,0:T(8,128)(2,1)}), bf16[16,16,1280]{2,1,0:T(8,128)(2,1)}, u32[]{:S(2)}, u32[]{:S(2)}) async-start(bf16[16,16,1280]{2,1,0:T(8,128)(2,1)} %pad_maximum_fusion.3), calls=%async_computation.8 | async-start | bytes 1310720 | tf_op jit(solution)/shard_map/all_to_all | solution.py:184
  190.8 30.0 %collective-permute-start.3 = (bf16[8,64,768]{2,1,0:T(8,128)(2,1)}, bf16[8,64,768]{2,1,0:T(8,128)(2,1)}, u32[]{:S(2)}, u32[]{:S(2)}) collective-permute-start(bf16[8,64,768]{2,1,0:T(8,128)(2,1)} %dynamic-slice_bitcast_fusion), channel_id=1, source_target_pairs={{0,16},{16,0},{1,17},{17,1},{2,18},{18,2},{3,19},{19,3},{4,20},{20... | collective-permute-start | bytes 2359304 | tf_op jit(solution)/shard_map/ppermute | solution.py:38
  225.1 23.2 %all-to-all-start.9 = ((bf16[16,16,1024]{2,1,0:T(8,128)(2,1)}), bf16[16,16,1024]{2,1,0:T(8,128)(2,1)S(1)}, u32[]{:S(2)}, u32[]{:S(2)}) async-start(bf16[16,16,1024]{2,1,0:T(8,128)(2,1)} %broadcast_in_dim.16), calls=%async_computation.9 | async-start | bytes 1048576 | tf_op jit(solution)/shard_map/all_to_all | solution.py:29
  234.3 5.9 %collective-permute-start.6 = (bf16[2,64,768]{2,1,0:T(8,128)(2,1)S(1)}, bf16[2,64,768]{2,1,0:T(8,128)(2,1)S(1)}, u32[]{:S(2)}, u32[]{:S(2)}) collective-permute-start(bf16[2,64,768]{2,1,0:T(8,128)(2,1)S(1)} %get-tuple-element.36), channel_id=1, source_target_pairs={{0,96},{32,0},{64,32},{96,64},{1,97},{33,1},{65,33},{97,65},{2,98}... | collective-permute-start | bytes 589832 | tf_op jit(solution)/shard_map/ppermute | solution.py:43
  235.6 7.1 %collective-permute-start.5 = (bf16[2,64,768]{2,1,0:T(8,128)(2,1)S(1)}, bf16[2,64,768]{2,1,0:T(8,128)(2,1)S(1)}, u32[]{:S(2)}, u32[]{:S(2)}) collective-permute-start(bf16[2,64,768]{2,1,0:T(8,128)(2,1)S(1)} %get-tuple-element.37), channel_id=1, source_target_pairs={{0,64},{32,96},{64,0},{96,32},{1,65},{33,97},{65,1},{97,33},{2,66}... | collective-permute-start | bytes 589832 | tf_op jit(solution)/shard_map/ppermute | solution.py:43
  236.3 11.8 %collective-permute-start.4 = (bf16[2,64,768]{2,1,0:T(8,128)(2,1)S(1)}, bf16[2,64,768]{2,1,0:T(8,128)(2,1)S(1)}, u32[]{:S(2)}, u32[]{:S(2)}) collective-permute-start(bf16[2,64,768]{2,1,0:T(8,128)(2,1)S(1)} %get-tuple-element.35), channel_id=1, source_target_pairs={{0,32},{32,64},{64,96},{96,0},{1,33},{33,65},{65,97},{97,1},{2,34}... | collective-permute-start | bytes 589832 | tf_op jit(solution)/shard_map/ppermute | solution.py:43
  252.7 23.3 %all-to-all-start.10 = ((bf16[16,16,1024]{2,1,0:T(8,128)(2,1)}), bf16[16,16,1024]{2,1,0:T(8,128)(2,1)S(1)}, u32[]{:S(2)}, u32[]{:S(2)}) async-start(bf16[16,16,1024]{2,1,0:T(8,128)(2,1)} %bitcast.47), calls=%async_computation.10 | async-start | bytes 1048576 | tf_op jit(solution)/shard_map/all_to_all | solution.py:22
  263.8 9.7 %collective-permute-start.7 = (bf16[8,64,512]{2,1,0:T(8,128)(2,1)S(1)}, bf16[8,64,512]{2,1,0:T(8,128)(2,1)}, u32[]{:S(2)}, u32[]{:S(2)}) collective-permute-start(bf16[8,64,512]{2,1,0:T(8,128)(2,1)S(1)} %dynamic-slice_bitcast_fusion.2), channel_id=1, source_target_pairs={{0,16},{16,0},{1,17},{17,1},{2,18},{18,2},{3,19},{19,3},{4,20},{20... | collective-permute-start | bytes 1572872 | tf_op jit(solution)/shard_map/ppermute | solution.py:38
  264.6 8.8 %collective-permute-start.11 = (bf16[64,768]{1,0:T(8,128)(2,1)S(1)}, bf16[64,768]{1,0:T(8,128)(2,1)S(1)}, u32[]{:S(2)}, u32[]{:S(2)}) collective-permute-start(bf16[64,768]{1,0:T(8,128)(2,1)S(1)} %dynamic-slice_bitcast_fusion.15), channel_id=1, source_target_pairs={{0,128},{128,0},{1,129},{129,1},{2,130},{130,2},{3,131},{131,3},{4... | collective-permute-start | bytes 294920 | tf_op jit(solution)/shard_map/ppermute | solution.py:38
  276.9 19.3 %all-to-all-start.11 = ((bf16[16,16,1024]{2,1,0:T(8,128)(2,1)}), bf16[16,16,1024]{2,1,0:T(8,128)(2,1)S(1)}, u32[]{:S(2)}, u32[]{:S(2)}) async-start(bf16[16,16,1024]{2,1,0:T(8,128)(2,1)} %broadcast_in_dim.17), calls=%async_computation.11 | async-start | bytes 1048576 | tf_op jit(solution)/shard_map/all_to_all | solution.py:29
  284.2 5.6 %collective-permute-start.13 = (bf16[2,64,512]{2,1,0:T(8,128)(2,1)S(1)}, bf16[2,64,512]{2,1,0:T(8,128)(2,1)S(1)}, u32[]{:S(2)}, u32[]{:S(2)}) collective-permute-start(bf16[2,64,512]{2,1,0:T(8,128)(2,1)S(1)} %get-tuple-element.48), channel_id=1, source_target_pairs={{0,64},{32,96},{64,0},{96,32},{1,65},{33,97},{65,1},{97,33},{2,66}... | collective-permute-start | bytes 393224 | tf_op jit(solution)/shard_map/ppermute | solution.py:43
  285.6 7.4 %collective-permute-start.12 = (bf16[2,64,512]{2,1,0:T(8,128)(2,1)S(1)}, bf16[2,64,512]{2,1,0:T(8,128)(2,1)S(1)}, u32[]{:S(2)}, u32[]{:S(2)}) collective-permute-start(bf16[2,64,512]{2,1,0:T(8,128)(2,1)S(1)} %get-tuple-element.46), channel_id=1, source_target_pairs={{0,32},{32,64},{64,96},{96,0},{1,33},{33,65},{65,97},{97,1},{2,34}... | collective-permute-start | bytes 393224 | tf_op jit(solution)/shard_map/ppermute | solution.py:43
  293.1 18.5 %collective-permute-start.15 = (bf16[64,512]{1,0:T(8,128)(2,1)S(1)}, bf16[64,512]{1,0:T(8,128)(2,1)S(1)}, u32[]{:S(2)}, u32[]{:S(2)}) collective-permute-start(bf16[64,512]{1,0:T(8,128)(2,1)S(1)} %dynamic-slice_bitcast_fusion.17), channel_id=1, source_target_pairs={{0,128},{128,0},{1,129},{129,1},{2,130},{130,2},{3,131},{131,3},{4... | collective-permute-start | bytes 196616 | tf_op jit(solution)/shard_map/ppermute | solution.py:38
  300.5 21.5 %all-to-all-start.12 = ((bf16[16,64,256]{2,1,0:T(8,128)(2,1)}), bf16[16,64,256]{2,1,0:T(8,128)(2,1)S(1)}, u32[]{:S(2)}, u32[]{:S(2)}) async-start(bf16[16,64,256]{2,1,0:T(8,128)(2,1)} %bitcast.59), calls=%async_computation.12 | async-start | bytes 1048576 | tf_op jit(solution)/shard_map/all_to_all | solution.py:22
  311.7 6.5 %collective-permute-start.9 = (bf16[256,256]{1,0:T(8,128)(2,1)S(1)}, bf16[256,256]{1,0:T(8,128)(2,1)S(1)}, u32[]{:S(2)}, u32[]{:S(2)}) collective-permute-start(bf16[256,256]{1,0:T(8,128)(2,1)S(1)} %bitcast.234), channel_id=1, source_target_pairs={{0,2},{1,3},{2,0},{3,1},{4,6},{5,7},{6,4},{7,5},{8,10},{9,11},{10,... | collective-permute-start | bytes 393224 | tf_op jit(solution)/shard_map/ppermute | solution.py:43
  312.8 6.3 %collective-permute-start.10 = (bf16[256,256]{1,0:T(8,128)(2,1)S(1)}, bf16[256,256]{1,0:T(8,128)(2,1)S(1)}, u32[]{:S(2)}, u32[]{:S(2)}) collective-permute-start(bf16[256,256]{1,0:T(8,128)(2,1)S(1)} %bitcast.235), channel_id=1, source_target_pairs={{0,3},{1,0},{2,1},{3,2},{4,7},{5,4},{6,5},{7,6},{8,11},{9,8},{10,9... | collective-permute-start | bytes 393224 | tf_op jit(solution)/shard_map/ppermute | solution.py:43
  314.4 6.6 %collective-permute-start.8 = (bf16[256,256]{1,0:T(8,128)(2,1)S(1)}, bf16[256,256]{1,0:T(8,128)(2,1)S(1)}, u32[]{:S(2)}, u32[]{:S(2)}) collective-permute-start(bf16[256,256]{1,0:T(8,128)(2,1)S(1)} %bitcast.236), channel_id=1, source_target_pairs={{0,1},{1,2},{2,3},{3,0},{4,5},{5,6},{6,7},{7,4},{8,9},{9,10},{10,1... | collective-permute-start | bytes 393224 | tf_op jit(solution)/shard_map/ppermute | solution.py:43
  (57 other events, 233.2 us)

commit v4 on v3

--- a/solution.py
+++ b/solution.py
@@ -11,6 +11,7 @@
 DP = ("z_lo", "y", "core")
 MP = ("z_hi", "x")
 
+
 epsilon = 1e-06
 bf16 = jnp.bfloat16
 f32 = jnp.float32
@@ -34,10 +35,6 @@
     return lax.optimization_barrier((x, *others))[0]
 
 
-def swapped(x, axis):
-    return lax.ppermute(x, axis, [(0, 1), (1, 0)])
-
-
 def moved(x, axis, step):
     n = lax.axis_size(axis)
     return lax.ppermute(x, axis, [(k, (k + step) % n) for k in range(n)])
@@ -47,30 +44,25 @@
     return lax.dynamic_index_in_dim(x, index, 0, keepdims=False)
 
 
-def core_stage(grads):
-    rows, _ = grads[0].shape
-    joined = jnp.concatenate([g.astype(bf16) for g in grads], axis=1)
-    parts = joined.reshape(8, 2, rows // 16, cols_of(grads))
-    return pair_parts(jnp.moveaxis(parts, 1, 0), "core")
-
-
-def cols_of(arrays):
-    return sum(a.shape[1] for a in arrays)
-
-
-def pair_parts(x, axis):
-    here = lax.axis_index(axis)
-    return pick(x, here), swapped(pick(x, 1 - here), axis)
-
-
 def total(parts):
     return sum(p.astype(f32) for p in parts)
 
 
-def y_stage(parts):
-    parts = jnp.moveaxis(parts.reshape(2, 4, *parts.shape[1:]), 1, 0)
+def y_stage(grads):
+    joined = jnp.concatenate([g.astype(bf16) for g in grads], axis=1)
+    rows, cols = joined.shape
+    parts = jnp.moveaxis(joined.reshape(2, 4, 2, rows // 16, cols), 1, 0)
     here = lax.axis_index("y")
-    return [pick(parts, here)] + [moved(pick(parts, (here + k) % 4), "y", k) for k in range(1, 4)]
+    sent = [pick(parts, (here + k) % 4) for k in range(1, 4)]
+    return [pick(parts, here)] + [moved(s, "y", k) for k, s in enumerate(sent, 1)], sent
+
+
+def quad_stage(parts):
+    axes = ("z_lo", "core")
+    here = lax.axis_index(axes)
+    return [pick(parts, here)] + [
+        lax.ppermute(pick(parts, here ^ k), axes, [(i, i ^ k) for i in range(4)]) for k in range(1, 4)
+    ]
 
 
 def normalize(stream):
@@ -83,6 +75,11 @@
 def norm_backward(scaled, rscale, upward):
     inner = jnp.mean(upward * scaled, axis=-1, keepdims=True)
     return rscale * (upward - scaled * inner)
+
+
+def norm_added(upstream, stream, grad):
+    _, scaled, rscale = normalize(stream)
+    return (upstream.astype(f32) + norm_backward(scaled, rscale, grad)).astype(bf16)
 
 
 def smooth_gate(preact):
@@ -130,23 +127,23 @@
 
     live = (jnp.arange(SLATE)[None, :] < lengths[:, None]).astype(f32)
     triple = [triple_weight[l].reshape(width, -1) for l in range(LAYERS)]
-    saved = []
+    saved, owned = [], []
     stream = tokens
     stream_part = part(tokens)
     for l in range(LAYERS):
-        normed, scaled, rscale = normalize(stream)
+        normed = normalize(stream)[0]
         qkv = jnp.dot(normed, triple[l], preferred_element_type=f32).astype(bf16)
         queries, key_rows, values = (qkv[:, k * HD : (k + 1) * HD] for k in range(3))
         probs, context = attend(queries, key_rows, values, live)
         partial_att = contract_cols(context, output_weight[l]).astype(bf16)
         mid_part = (stream_part.astype(f32) + share_rows(partial_att, MP)).astype(bf16)
         mid_stream = all_rows(mid_part, MP)
-        normed_mid, scaled_mid, rscale_mid = normalize(mid_stream)
+        normed_mid = normalize(mid_stream)[0]
         preact = jnp.dot(normed_mid, upward_weight[l], preferred_element_type=f32)
         activated = smooth_gate(preact).astype(bf16)
         partial_ffn = contract_cols(activated, downward_weight[l]).astype(bf16)
-        saved.append((normed, scaled, rscale, queries, key_rows, values, probs, context,
-                      scaled_mid, rscale_mid, normed_mid, preact, activated))
+        saved.append((normed, queries, key_rows, values, probs, context, normed_mid, preact, activated))
+        owned.append((stream_part, mid_part))
         if l + 1 < LAYERS:
             stream_part = (mid_part.astype(f32) + share_rows(partial_ffn, MP)).astype(bf16)
             stream = all_rows(stream_part, MP)
@@ -156,9 +153,9 @@
     heads = triple_weight.shape[-1]
     x_here = lax.axis_index("x")
 
-    (normed, scaled, rscale, queries, key_rows, values, probs, context,
-     scaled_mid, rscale_mid, normed_mid, preact, activated) = saved[top]
-    upstream = cotangent
+    normed, queries, key_rows, values, probs, context, normed_mid, preact, activated = saved[top]
+    stream_part, mid_part = owned[top]
+    upstream, upstream_part = cotangent, part(cotangent)
     grad_act = jnp.dot(upstream, downward_weight[top], preferred_element_type=f32).astype(bf16)
     _, gate_back = jax.vjp(smooth_gate, preact)
     grad_preact = gate_back(grad_act.astype(f32))[0].astype(bf16)
@@ -167,22 +164,23 @@
     shares = [pick(shares, x_here)] + [
         moved(pick(shares, (x_here + k) % 4), "x", k) for k in range(1, 4)
     ]
-    own = share_rows(partial, MP).astype(bf16)
+    grad_normed = share_rows(partial, MP)
+    own = upstream_part = norm_added(upstream_part, mid_part, grad_normed)
     shares = total(shares).astype(bf16).reshape(n, share, quarter)
     sent = jnp.concatenate([jnp.broadcast_to(own[None], (n, share, width)), shares], axis=2)
-    came = lax.all_to_all(after(sent, rscale_mid), MP, 0, 0, tiled=True)
-    grad_normed = came[:, :, :width].reshape(rows, width).astype(f32)
+    came = lax.all_to_all(sent, MP, 0, 0, tiled=True)
+    grad_mid = came[:, :, :width].reshape(rows, width)
     ffn_part = jnp.sum(came[:, :, width:].reshape(4, 4, share, quarter).astype(f32), axis=0)
     ffn_part = jnp.concatenate([ffn_part[k] for k in range(4)], axis=1)
     final_part = (mid_part.astype(f32) + ffn_part).astype(bf16)
-    grad_mid = (upstream.astype(f32) + norm_backward(scaled_mid, rscale_mid, grad_normed)).astype(bf16)
     grad_context = jnp.dot(grad_mid, output_weight[top], preferred_element_type=f32).astype(bf16)
     grad_qkv = attend_backward(probs, queries, key_rows, values, grad_context)
     partial = contract_cols(grad_qkv, triple[top]).astype(bf16).reshape(n, share, width)
     quarters = jnp.stack([final_part[:, k * quarter : (k + 1) * quarter] for k in range(4)])
     sent = jnp.concatenate([partial, jnp.tile(quarters, (4, 1, 1))], axis=2)
     came = lax.all_to_all(sent, MP, 0, 0, tiled=True)
-    own = jnp.sum(came[:, :, :width].astype(f32), axis=0).astype(bf16)
+    grad_input = jnp.sum(came[:, :, :width].astype(f32), axis=0)
+    own = upstream_part = norm_added(upstream_part, stream_part, grad_input)
     column = came[:, :, width:].reshape(rows, quarter)
     wide1 = [
         contract_rows(normed_mid, grad_preact),
@@ -190,51 +188,49 @@
         contract_rows(normed, grad_qkv),
         contract_rows(grad_mid, context),
     ]
-    sums1 = core_stage(wide1)
-    grad_input = all_rows(after(own, rscale, sums1[0]), MP).astype(f32)
-    sums1 = y_stage(total(sums1).astype(bf16))
-    grad_input = after(grad_input, sums1[0])
-    upstream = (grad_mid.astype(f32) + norm_backward(scaled, rscale, grad_input)).astype(bf16)
-    (normed, scaled, rscale, queries, key_rows, values, probs, context,
-     scaled_mid, rscale_mid, normed_mid, preact, activated) = saved[0]
+    sums1, sent1 = y_stage(wide1)
+    upstream = all_rows(after(own, *sent1), MP)
+    normed, queries, key_rows, values, probs, context, normed_mid, preact, activated = saved[0]
+    mid_part = owned[0][1]
     grad_act = jnp.dot(upstream, downward_weight[0], preferred_element_type=f32).astype(bf16)
     _, gate_back = jax.vjp(smooth_gate, preact)
     grad_preact = gate_back(grad_act.astype(f32))[0].astype(bf16)
     partial = contract_cols(grad_preact, upward_weight[0]).astype(bf16)
-    own = share_rows(partial, MP).astype(bf16)
+    grad_normed = share_rows(partial, MP)
+    own = norm_added(upstream_part, mid_part, grad_normed)
     wide0 = [contract_rows(normed_mid, grad_preact), contract_rows(upstream, activated)]
-    sums0 = core_stage(wide0)
-    sums1 = pair_parts(total(sums1).astype(bf16), "z_lo")
-    grad_normed = all_rows(after(own, rscale_mid, sums0[0], sums1[0]), MP).astype(f32)
-    sums0 = y_stage(total(sums0).astype(bf16))
-    grad_normed = after(grad_normed, sums0[0])
-    grad_mid = (upstream.astype(f32) + norm_backward(scaled_mid, rscale_mid, grad_normed)).astype(bf16)
+    sums0, sent0 = y_stage(wide0)
+    grad_mid = all_rows(after(own, *sent0), MP)
     grad_context = jnp.dot(grad_mid, output_weight[0], preferred_element_type=f32).astype(bf16)
     grad_qkv = attend_backward(probs, queries, key_rows, values, grad_context)
     late = [contract_rows(normed, grad_qkv), contract_rows(grad_mid, context)]
     late = jnp.concatenate([g.astype(bf16) for g in late], axis=1)
     column = after(column, late)
     columns = [column] + [moved(column, "x", step) for step in range(1, 4)]
+    sums1 = total(sums1).astype(bf16)
+    sums0 = total(sums0).astype(bf16)
+    sums = jnp.concatenate([sums1, sums0], axis=3)
+    sums = quad_stage(sums.reshape(4, *sums.shape[2:]))
     late = share_rows(late, DP)
-    sums0 = pair_parts(total(sums0).astype(bf16), "z_lo")
     final_stream = jnp.concatenate(
         [lax.select_n((x_here - k) % 4, *columns) for k in range(4)], axis=1
     )
-    sums1, sums0 = total(sums1), total(sums0)
+    sums = total(sums)
 
     def cut(x, first, size):
         return x[:, first : first + size]
 
     ff = upward_weight.shape[-1]
+    first0 = 2 * ff + 4 * heads
     return (
         final_stream,
         jnp.stack([
             cut(late, 0, 3 * heads).reshape(-1, 3, heads),
-            cut(sums1, 2 * ff, 3 * heads).reshape(-1, 3, heads),
+            cut(sums, 2 * ff, 3 * heads).reshape(-1, 3, heads),
         ]),
-        jnp.stack([cut(late, 3 * heads, heads), cut(sums1, 2 * ff + 3 * heads, heads)]),
-        jnp.stack([cut(sums0, 0, ff), cut(sums1, 0, ff)]),
-        jnp.stack([cut(sums0, ff, ff), cut(sums1, ff, ff)]),
+        jnp.stack([cut(late, 3 * heads, heads), cut(sums, 2 * ff + 3 * heads, heads)]),
+        jnp.stack([cut(sums, first0, ff), cut(sums, 0, ff)]),
+        jnp.stack([cut(sums, first0 + ff, ff), cut(sums, ff, ff)]),
     )
 
 

time: 325 us -> 324 us (level)
  starting transfers between devices: 106 us -> 96.1 us
  local copies, waits for them, and re-layouts: 16.5 us -> 20.4 us
    all_to_all x1 -> x2, waiting for transfers between devices: 0.01 us -> 23.8 us  [step(): came = lax.all_to_all(sent, MP, 0, 0, tiled=True)]
    ppermute x12, waiting for transfers between devices: 30.7 us -> 16.5 us  [moved(): return lax.ppermute(x, axis, [(k, (k + step) % n) for k in range(n)])]
    all_to_all x1 -> x0, waiting for transfers between devices: 14.1 us -> none  [step(): came = lax.all_to_all(after(sent, rscale_mid), MP, 0, 0, tiled=True)]
    all_to_all x3, waiting for transfers between devices: 12.2 us -> 25.5 us  [all_rows(): blocks = lax.all_to_all(copies, axis, 0, 0, tiled=True)]
    ppermute x4 -> x3, waiting for transfers between devices: 11 us -> 0.01 us  [quad_stage(): lax.ppermute(pick(parts, here ^ k), axes, [(i, i ^ k) for i in range(4)])]
    all_to_all x4, starting transfers between devices: 34.4 us -> 27.9 us  [share_rows(): blocks = lax.all_to_all(blocks, axis, 0, 0, tiled=True)]
    all_to_all x1 -> x2, starting transfers between devices: 4.58 us -> 10.5 us  [step(): came = lax.all_to_all(sent, MP, 0, 0, tiled=True)]
    all_to_all x1 -> x0, starting transfers between devices: 5.65 us -> none  [step(): came = lax.all_to_all(after(sent, rscale_mid), MP, 0, 0, tiled=True)]
  transfers between devices with their start and end apart: 25 -> 24, of which waited for: 19 -> 12; matrix products, arithmetic and copies ran while one was open for 7% -> 9% of each run, Pallas kernels for 0% -> 0%
where the time goes in v4:
time: 324 us; the launch traced here: 322 us
  starting transfers between devices  96.1 us (30%)
  waiting for transfers between devices  83.2 us (26%)
  blocking collectives  77.6 us (24%)
  other arithmetic  23.6 us (7%)
  local copies, waits for them, and re-layouts  20.4 us (6%)
  matrix products  18.4 us (6%)
    all_to_all x2, blocking collectives, all_rows(): blocks = lax.all_to_all(copies, axis, 0, 0, tiled=True)  40.5 us
    all_to_all x2, blocking collectives, share_rows(): blocks = lax.all_to_all(blocks, axis, 0, 0, tiled=True)  37.2 us
    ppermute x3, starting transfers between devices, quad_stage(): lax.ppermute(pick(parts, here ^ k), axes, [(i, i ^ k) for i in range(4)])  29 us
    all_to_all x4, starting transfers between devices, share_rows(): blocks = lax.all_to_all(blocks, axis, 0, 0, tiled=True)  27.9 us
    all_to_all x3, waiting for transfers between devices, all_rows(): blocks = lax.all_to_all(copies, axis, 0, 0, tiled=True)  25.5 us
    all_to_all x2, waiting for transfers between devices, step(): came = lax.all_to_all(sent, MP, 0, 0, tiled=True)  23.8 us
    all_to_all x4, waiting for transfers between devices, share_rows(): blocks = lax.all_to_all(blocks, axis, 0, 0, tiled=True)  17.3 us
    ppermute x12, waiting for transfers between devices, moved(): return lax.ppermute(x, axis, [(k, (k + step) % n) for k in range(n)])  16.5 us
  transfers between devices with their start and end apart: 24, of which 12 were waited for; matrix products, arithmetic and copies ran while one was open for 9% of the time, Pallas kernels for 0%

profile of v4, /device:TPU:1, one launch (start us, length us, event | category | flops | bytes accessed | tf_op | source)
XLA Modules:
  0.0 322.1 jit_solution(17679885935224107719)
XLA Ops:
  5.9 11.6 %all-to-all-start = ((bf16[16,16,1024]{2,1,0:T(8,128)(2,1)}), bf16[16,16,1024]{2,1,0:T(8,128)(2,1)S(1)}, u32[]{:S(2)}, u32[]{:S(2)}) async-start(bf16[16,16,1024]{2,1,0:T(8,128)(2,1)} %bitcast.3), calls=%async_computation | async-start | bytes 1048576 | tf_op jit(solution)/shard_map/all_to_all | solution.py:23
  17.5 14.9 %all-to-all-done = bf16[16,16,1024]{2,1,0:T(8,128)(2,1)S(1)} async-done(((bf16[16,16,1024]{2,1,0:T(8,128)(2,1)}), bf16[16,16,1024]{2,1,0:T(8,128)(2,1)S(1)}, u32[]{:S(2)}, u32[]{:S(2)}) %all-to-all-start) | async-done | bytes 524320 | tf_op jit(solution)/shard_map/all_to_all | solution.py:23
  33.2 22.6 %all_to_all.65 = bf16[16,16,1024]{2,1,0:T(8,128)(2,1)S(1)} all-to-all(bf16[16,16,1024]{2,1,0:T(8,128)(2,1)S(1)} %broadcast_in_dim.12), channel_id=1, replica_groups=mesh['z_lo'=2,'y'=4,'core'=2,'z_hi'=4,'x'=4] {'z_hi','x'}, dimensions={0} | all-to-all | bytes 1048576 | tf_op jit(solution)/shard_map/all_to_all | solution.py:30
  57.3 20.2 %all_to_all.66 = bf16[16,16,1024]{2,1,0:T(8,128)(2,1)S(1)} all-to-all(bf16[16,16,1024]{2,1,0:T(8,128)(2,1)S(1)} %bitcast.203), channel_id=1, replica_groups=mesh['z_lo'=2,'y'=4,'core'=2,'z_hi'=4,'x'=4] {'z_hi','x'}, dimensions={0} | all-to-all | bytes 1048576 | tf_op jit(solution)/shard_map/all_to_all | solution.py:23
  78.4 17.9 %all_to_all.67 = bf16[16,16,1024]{2,1,0:T(8,128)(2,1)S(1)} all-to-all(bf16[16,16,1024]{2,1,0:T(8,128)(2,1)S(1)} %broadcast_in_dim.13), channel_id=1, replica_groups=mesh['z_lo'=2,'y'=4,'core'=2,'z_hi'=4,'x'=4] {'z_hi','x'}, dimensions={0} | all-to-all | bytes 1048576 | tf_op jit(solution)/shard_map/all_to_all | solution.py:30
  98.7 17.0 %all_to_all.68 = bf16[16,16,1024]{2,1,0:T(8,128)(2,1)S(1)} all-to-all(bf16[16,16,1024]{2,1,0:T(8,128)(2,1)S(1)} %bitcast.200), channel_id=1, replica_groups=mesh['z_lo'=2,'y'=4,'core'=2,'z_hi'=4,'x'=4] {'z_hi','x'}, dimensions={0} | all-to-all | bytes 1048576 | tf_op jit(solution)/shard_map/all_to_all | solution.py:23
  117.9 3.7 %all-to-all-start.5 = ((bf16[16,16,1024]{2,1,0:T(8,128)(2,1)}), bf16[16,16,1024]{2,1,0:T(8,128)(2,1)S(1)}, u32[]{:S(2)}, u32[]{:S(2)}) async-start(bf16[16,16,1024]{2,1,0:T(8,128)(2,1)} %broadcast_in_dim.14), calls=%async_computation.5 | async-start | bytes 1048576 | tf_op jit(solution)/shard_map/all_to_all | solution.py:30
  121.6 11.3 %all-to-all-done.5 = bf16[16,16,1024]{2,1,0:T(8,128)(2,1)S(1)} async-done(((bf16[16,16,1024]{2,1,0:T(8,128)(2,1)}), bf16[16,16,1024]{2,1,0:T(8,128)(2,1)S(1)}, u32[]{:S(2)}, u32[]{:S(2)}) %all-to-all-start.5) | async-done | bytes 524320 | tf_op jit(solution)/shard_map/all_to_all | solution.py:30
  136.5 3.7 %all-to-all-start.6 = ((bf16[16,16,1024]{2,1,0:T(8,128)(2,1)}), bf16[16,16,1024]{2,1,0:T(8,128)(2,1)S(1)}, u32[]{:S(2)}, u32[]{:S(2)}) async-start(bf16[16,16,1024]{2,1,0:T(8,128)(2,1)} %bitcast.195), calls=%async_computation.6 | async-start | bytes 1048576 | tf_op jit(solution)/shard_map/all_to_all | solution.py:23
  149.3 2.9 collective-permute-done.1
  157.3 6.0 %all-to-all-start.7 = ((bf16[16,16,1280]{2,1,0:T(8,128)(2,1)}), bf16[16,16,1280]{2,1,0:T(8,128)(2,1)}, u32[]{:S(2)}, u32[]{:S(2)}) async-start(bf16[16,16,1280]{2,1,0:T(8,128)(2,1)} %pad_maximum_fusion.2), calls=%async_computation.7 | async-start | bytes 1310720 | tf_op jit(solution)/shard_map/all_to_all | solution.py:171
  167.1 12.0 %all-to-all-done.7 = bf16[16,16,1280]{2,1,0:T(8,128)(2,1)} async-done(((bf16[16,16,1280]{2,1,0:T(8,128)(2,1)}), bf16[16,16,1280]{2,1,0:T(8,128)(2,1)}, u32[]{:S(2)}, u32[]{:S(2)}) %all-to-all-start.7) | async-done | bytes 655392 | tf_op jit(solution)/shard_map/all_to_all | solution.py:171
  185.6 4.6 %all-to-all-start.8 = ((bf16[16,16,1280]{2,1,0:T(8,128)(2,1)}), bf16[16,16,1280]{2,1,0:T(8,128)(2,1)}, u32[]{:S(2)}, u32[]{:S(2)}) async-start(bf16[16,16,1280]{2,1,0:T(8,128)(2,1)} %pad_maximum_fusion.3), calls=%async_computation.8 | async-start | bytes 1310720 | tf_op jit(solution)/shard_map/all_to_all | solution.py:181
  196.7 11.9 %all-to-all-done.8 = bf16[16,16,1280]{2,1,0:T(8,128)(2,1)} async-done(((bf16[16,16,1280]{2,1,0:T(8,128)(2,1)}), bf16[16,16,1280]{2,1,0:T(8,128)(2,1)}, u32[]{:S(2)}, u32[]{:S(2)}) %all-to-all-start.8) | async-done | bytes 655392 | tf_op jit(solution)/shard_map/all_to_all | solution.py:181
  210.9 4.2 %all-to-all-start.9 = ((bf16[16,16,1024]{2,1,0:T(8,128)(2,1)}), bf16[16,16,1024]{2,1,0:T(8,128)(2,1)}, u32[]{:S(2)}, u32[]{:S(2)}) async-start(bf16[16,16,1024]{2,1,0:T(8,128)(2,1)} %broadcast_in_dim.16), calls=%async_computation.9 | async-start | bytes 1048576 | tf_op jit(solution)/shard_map/all_to_all | solution.py:30
  215.3 14.2 %all-to-all-done.9 = bf16[16,16,1024]{2,1,0:T(8,128)(2,1)} async-done(((bf16[16,16,1024]{2,1,0:T(8,128)(2,1)}), bf16[16,16,1024]{2,1,0:T(8,128)(2,1)}, u32[]{:S(2)}, u32[]{:S(2)}) %all-to-all-start.9) | async-done | bytes 524320 | tf_op jit(solution)/shard_map/all_to_all | solution.py:30
  232.3 6.4 %all-to-all-start.10 = ((bf16[16,16,1024]{2,1,0:T(8,128)(2,1)}), bf16[16,16,1024]{2,1,0:T(8,128)(2,1)}, u32[]{:S(2)}, u32[]{:S(2)}) async-start(bf16[16,16,1024]{2,1,0:T(8,128)(2,1)} %bitcast.196), calls=%async_computation.10 | async-start | bytes 1048576 | tf_op jit(solution)/shard_map/all_to_all | solution.py:23
  238.8 2.8 collective-permute-start.8
  251.3 2.4 all-to-all-done.10
  256.1 6.6 %all-to-all-start.11 = ((bf16[16,16,1024]{2,1,0:T(8,128)(2,1)}), bf16[16,16,1024]{2,1,0:T(8,128)(2,1)S(1)}, u32[]{:S(2)}, u32[]{:S(2)}) async-start(bf16[16,16,1024]{2,1,0:T(8,128)(2,1)} %broadcast_in_dim.17), calls=%async_computation.11 | async-start | bytes 1048576 | tf_op jit(solution)/shard_map/all_to_all | solution.py:30
  265.2 4.1 %collective-permute-done.9 = bf16[2,2,64,512]{3,2,1,0:T(8,128)(2,1)S(1)} collective-permute-done((bf16[2,2,64,512]{3,2,1,0:T(8,128)(2,1)S(1)}, bf16[2,2,64,512]{3,2,1,0:T(8,128)(2,1)S(1)}, u32[]{:S(2)}, u32[]{:S(2)}) %collective-permute-start.9) | collective-permute-done | bytes 262176 | tf_op jit(solution)/shard_map/ppermute | solution.py:40
  270.5 27.5 %collective-permute-start.12 = (bf16[64,1280]{1,0:T(8,128)(2,1)S(1)}, bf16[64,1280]{1,0:T(8,128)(2,1)S(1)}, u32[]{:S(2)}, u32[]{:S(2)}) collective-permute-start(bf16[64,1280]{1,0:T(8,128)(2,1)S(1)} %get-tuple-element.40), channel_id=1, source_target_pairs={{0,16},{16,0},{128,144},{144,128},{1,17},{17,1},{129,145},{145,129... | collective-permute-start | bytes 491528 | tf_op jit(solution)/shard_map/ppermute | solution.py:64
  302.5 6.2 %all-to-all-start.12 = ((bf16[16,64,256]{2,1,0:T(8,128)(2,1)}), bf16[16,64,256]{2,1,0:T(8,128)(2,1)S(1)}, u32[]{:S(2)}, u32[]{:S(2)}) async-start(bf16[16,64,256]{2,1,0:T(8,128)(2,1)} %bitcast.53), calls=%async_computation.12 | async-start | bytes 1048576 | tf_op jit(solution)/shard_map/all_to_all | solution.py:23
  315.8 3.6 %collective-permute-done.3 = bf16[256,256]{1,0:T(8,128)(2,1)S(1)} collective-permute-done((bf16[256,256]{1,0:T(8,128)(2,1)S(1)}, bf16[256,256]{1,0:T(8,128)(2,1)S(1)}, u32[]{:S(2)}, u32[]{:S(2)}) %collective-permute-start.3) | collective-permute-done | bytes 131104 | tf_op jit(solution)/shard_map/ppermute | solution.py:40
  (258 shorter events, 81.2 us)
Async XLA Ops:
  5.9 26.5 %all-to-all-start = ((bf16[16,16,1024]{2,1,0:T(8,128)(2,1)}), bf16[16,16,1024]{2,1,0:T(8,128)(2,1)S(1)}, u32[]{:S(2)}, u32[]{:S(2)}) async-start(bf16[16,16,1024]{2,1,0:T(8,128)(2,1)} %bitcast.3), calls=%async_computation | async-start | bytes 1048576 | tf_op jit(solution)/shard_map/all_to_all | solution.py:23
  117.9 15.0 %all-to-all-start.5 = ((bf16[16,16,1024]{2,1,0:T(8,128)(2,1)}), bf16[16,16,1024]{2,1,0:T(8,128)(2,1)S(1)}, u32[]{:S(2)}, u32[]{:S(2)}) async-start(bf16[16,16,1024]{2,1,0:T(8,128)(2,1)} %broadcast_in_dim.14), calls=%async_computation.5 | async-start | bytes 1048576 | tf_op jit(solution)/shard_map/all_to_all | solution.py:30
  136.5 16.4 %all-to-all-start.6 = ((bf16[16,16,1024]{2,1,0:T(8,128)(2,1)}), bf16[16,16,1024]{2,1,0:T(8,128)(2,1)S(1)}, u32[]{:S(2)}, u32[]{:S(2)}) async-start(bf16[16,16,1024]{2,1,0:T(8,128)(2,1)} %bitcast.195), calls=%async_computation.6 | async-start | bytes 1048576 | tf_op jit(solution)/shard_map/all_to_all | solution.py:23
  141.9 7.4 %collective-permute-start = (bf16[256,256]{1,0:T(8,128)(2,1)S(1)}, bf16[256,256]{1,0:T(8,128)(2,1)S(1)}, u32[]{:S(2)}, u32[]{:S(2)}) collective-permute-start(bf16[256,256]{1,0:T(8,128)(2,1)S(1)} %get-tuple-element.47), channel_id=1, source_target_pairs={{0,1},{1,2},{2,3},{3,0},{4,5},{5,6},{6,7},{7,4},{8,9},{9,10},{10,1... | collective-permute-start | bytes 393224 | tf_op jit(solution)/shard_map/ppermute | solution.py:40
  143.3 6.0 %collective-permute-start.2 = (bf16[256,256]{1,0:T(8,128)(2,1)S(1)}, bf16[256,256]{1,0:T(8,128)(2,1)S(1)}, u32[]{:S(2)}, u32[]{:S(2)}) collective-permute-start(bf16[256,256]{1,0:T(8,128)(2,1)S(1)} %get-tuple-element.48), channel_id=1, source_target_pairs={{0,3},{1,0},{2,1},{3,2},{4,7},{5,4},{6,5},{7,6},{8,11},{9,8},{10,9... | collective-permute-start | bytes 393224 | tf_op jit(solution)/shard_map/ppermute | solution.py:40
  144.6 7.6 %collective-permute-start.1 = (bf16[256,256]{1,0:T(8,128)(2,1)S(1)}, bf16[256,256]{1,0:T(8,128)(2,1)S(1)}, u32[]{:S(2)}, u32[]{:S(2)}) collective-permute-start(bf16[256,256]{1,0:T(8,128)(2,1)S(1)} %get-tuple-element.49), channel_id=1, source_target_pairs={{0,2},{1,3},{2,0},{3,1},{4,6},{5,7},{6,4},{7,5},{8,10},{9,11},{10,... | collective-permute-start | bytes 393224 | tf_op jit(solution)/shard_map/ppermute | solution.py:40
  157.3 21.8 %all-to-all-start.7 = ((bf16[16,16,1280]{2,1,0:T(8,128)(2,1)}), bf16[16,16,1280]{2,1,0:T(8,128)(2,1)}, u32[]{:S(2)}, u32[]{:S(2)}) async-start(bf16[16,16,1280]{2,1,0:T(8,128)(2,1)} %pad_maximum_fusion.2), calls=%async_computation.7 | async-start | bytes 1310720 | tf_op jit(solution)/shard_map/all_to_all | solution.py:171
  185.6 22.9 %all-to-all-start.8 = ((bf16[16,16,1280]{2,1,0:T(8,128)(2,1)}), bf16[16,16,1280]{2,1,0:T(8,128)(2,1)}, u32[]{:S(2)}, u32[]{:S(2)}) async-start(bf16[16,16,1280]{2,1,0:T(8,128)(2,1)} %pad_maximum_fusion.3), calls=%async_computation.8 | async-start | bytes 1310720 | tf_op jit(solution)/shard_map/all_to_all | solution.py:181
  210.9 18.7 %all-to-all-start.9 = ((bf16[16,16,1024]{2,1,0:T(8,128)(2,1)}), bf16[16,16,1024]{2,1,0:T(8,128)(2,1)}, u32[]{:S(2)}, u32[]{:S(2)}) async-start(bf16[16,16,1024]{2,1,0:T(8,128)(2,1)} %broadcast_in_dim.16), calls=%async_computation.9 | async-start | bytes 1048576 | tf_op jit(solution)/shard_map/all_to_all | solution.py:30
  232.3 21.5 %all-to-all-start.10 = ((bf16[16,16,1024]{2,1,0:T(8,128)(2,1)}), bf16[16,16,1024]{2,1,0:T(8,128)(2,1)}, u32[]{:S(2)}, u32[]{:S(2)}) async-start(bf16[16,16,1024]{2,1,0:T(8,128)(2,1)} %bitcast.196), calls=%async_computation.10 | async-start | bytes 1048576 | tf_op jit(solution)/shard_map/all_to_all | solution.py:23
  238.8 23.8 %collective-permute-start.8 = (bf16[2,2,64,768]{3,2,1,0:T(8,128)(2,1)}, bf16[2,2,64,768]{3,2,1,0:T(8,128)(2,1)}, u32[]{:S(2)}, u32[]{:S(2)}) collective-permute-start(bf16[2,2,64,768]{3,2,1,0:T(8,128)(2,1)} %get-tuple-element.32), channel_id=1, source_target_pairs={{0,96},{32,0},{64,32},{96,64},{1,97},{33,1},{65,33},{97,65},{2,98}... | collective-permute-start | bytes 1179656 | tf_op jit(solution)/shard_map/ppermute | solution.py:40
  241.6 21.1 %collective-permute-start.7 = (bf16[2,2,64,768]{3,2,1,0:T(8,128)(2,1)}, bf16[2,2,64,768]{3,2,1,0:T(8,128)(2,1)}, u32[]{:S(2)}, u32[]{:S(2)}) collective-permute-start(bf16[2,2,64,768]{3,2,1,0:T(8,128)(2,1)} %get-tuple-element.33), channel_id=1, source_target_pairs={{0,64},{32,96},{64,0},{96,32},{1,65},{33,97},{65,1},{97,33},{2,66}... | collective-permute-start | bytes 1179656 | tf_op jit(solution)/shard_map/ppermute | solution.py:40
  242.0 20.8 %collective-permute-start.6 = (bf16[2,2,64,768]{3,2,1,0:T(8,128)(2,1)}, bf16[2,2,64,768]{3,2,1,0:T(8,128)(2,1)}, u32[]{:S(2)}, u32[]{:S(2)}) collective-permute-start(bf16[2,2,64,768]{3,2,1,0:T(8,128)(2,1)} %get-tuple-element.34), channel_id=1, source_target_pairs={{0,32},{32,64},{64,96},{96,0},{1,33},{33,65},{65,97},{97,1},{2,34}... | collective-permute-start | bytes 1179656 | tf_op jit(solution)/shard_map/ppermute | solution.py:40
  247.9 17.2 %collective-permute-start.11 = (bf16[2,2,64,512]{3,2,1,0:T(8,128)(2,1)}, bf16[2,2,64,512]{3,2,1,0:T(8,128)(2,1)}, u32[]{:S(2)}, u32[]{:S(2)}) collective-permute-start(bf16[2,2,64,512]{3,2,1,0:T(8,128)(2,1)} %get-tuple-element.35), channel_id=1, source_target_pairs={{0,96},{32,0},{64,32},{96,64},{1,97},{33,1},{65,33},{97,65},{2,98}... | collective-permute-start | bytes 786440 | tf_op jit(solution)/shard_map/ppermute | solution.py:40
  249.9 15.2 %collective-permute-start.10 = (bf16[2,2,64,512]{3,2,1,0:T(8,128)(2,1)}, bf16[2,2,64,512]{3,2,1,0:T(8,128)(2,1)}, u32[]{:S(2)}, u32[]{:S(2)}) collective-permute-start(bf16[2,2,64,512]{3,2,1,0:T(8,128)(2,1)} %get-tuple-element.36), channel_id=1, source_target_pairs={{0,64},{32,96},{64,0},{96,32},{1,65},{33,97},{65,1},{97,33},{2,66}... | collective-permute-start | bytes 786440 | tf_op jit(solution)/shard_map/ppermute | solution.py:40
  256.1 43.4 %all-to-all-start.11 = ((bf16[16,16,1024]{2,1,0:T(8,128)(2,1)}), bf16[16,16,1024]{2,1,0:T(8,128)(2,1)S(1)}, u32[]{:S(2)}, u32[]{:S(2)}) async-start(bf16[16,16,1024]{2,1,0:T(8,128)(2,1)} %broadcast_in_dim.17), calls=%async_computation.11 | async-start | bytes 1048576 | tf_op jit(solution)/shard_map/all_to_all | solution.py:30
  262.7 6.6 %collective-permute-start.9 = (bf16[2,2,64,512]{3,2,1,0:T(8,128)(2,1)S(1)}, bf16[2,2,64,512]{3,2,1,0:T(8,128)(2,1)S(1)}, u32[]{:S(2)}, u32[]{:S(2)}) collective-permute-start(bf16[2,2,64,512]{3,2,1,0:T(8,128)(2,1)S(1)} %copy-done.27), channel_id=1, source_target_pairs={{0,32},{32,64},{64,96},{96,0},{1,33},{33,65},{65,97},{97,1},{2,34}... | collective-permute-start | bytes 786440 | tf_op jit(solution)/shard_map/ppermute | solution.py:40
  270.5 38.2 %collective-permute-start.12 = (bf16[64,1280]{1,0:T(8,128)(2,1)S(1)}, bf16[64,1280]{1,0:T(8,128)(2,1)S(1)}, u32[]{:S(2)}, u32[]{:S(2)}) collective-permute-start(bf16[64,1280]{1,0:T(8,128)(2,1)S(1)} %get-tuple-element.40), channel_id=1, source_target_pairs={{0,16},{16,0},{128,144},{144,128},{1,17},{17,1},{129,145},{145,129... | collective-permute-start | bytes 491528 | tf_op jit(solution)/shard_map/ppermute | solution.py:64
  298.0 10.7 %collective-permute-start.14 = (bf16[64,1280]{1,0:T(8,128)(2,1)S(1)}, bf16[64,1280]{1,0:T(8,128)(2,1)S(1)}, u32[]{:S(2)}, u32[]{:S(2)}) collective-permute-start(bf16[64,1280]{1,0:T(8,128)(2,1)S(1)} %get-tuple-element.41), channel_id=1, source_target_pairs={{0,144},{16,128},{128,16},{144,0},{1,145},{17,129},{129,17},{145,1... | collective-permute-start | bytes 491528 | tf_op jit(solution)/shard_map/ppermute | solution.py:64
  298.1 10.7 %collective-permute-start.13 = (bf16[64,1280]{1,0:T(8,128)(2,1)S(1)}, bf16[64,1280]{1,0:T(8,128)(2,1)S(1)}, u32[]{:S(2)}, u32[]{:S(2)}) collective-permute-start(bf16[64,1280]{1,0:T(8,128)(2,1)S(1)} %get-tuple-element.42), channel_id=1, source_target_pairs={{0,128},{16,144},{128,0},{144,16},{1,129},{17,145},{129,1},{145,17... | collective-permute-start | bytes 491528 | tf_op jit(solution)/shard_map/ppermute | solution.py:64
  302.5 17.9 %all-to-all-start.12 = ((bf16[16,64,256]{2,1,0:T(8,128)(2,1)}), bf16[16,64,256]{2,1,0:T(8,128)(2,1)S(1)}, u32[]{:S(2)}, u32[]{:S(2)}) async-start(bf16[16,64,256]{2,1,0:T(8,128)(2,1)} %bitcast.53), calls=%async_computation.12 | async-start | bytes 1048576 | tf_op jit(solution)/shard_map/all_to_all | solution.py:23
  308.9 4.9 %collective-permute-start.5 = (bf16[256,256]{1,0:T(8,128)(2,1)S(1)}, bf16[256,256]{1,0:T(8,128)(2,1)S(1)}, u32[]{:S(2)}, u32[]{:S(2)}) collective-permute-start(bf16[256,256]{1,0:T(8,128)(2,1)S(1)} %bitcast.206), channel_id=1, source_target_pairs={{0,3},{1,0},{2,1},{3,2},{4,7},{5,4},{6,5},{7,6},{8,11},{9,8},{10,9... | collective-permute-start | bytes 393224 | tf_op jit(solution)/shard_map/ppermute | solution.py:40
  310.2 5.6 %collective-permute-start.4 = (bf16[256,256]{1,0:T(8,128)(2,1)S(1)}, bf16[256,256]{1,0:T(8,128)(2,1)S(1)}, u32[]{:S(2)}, u32[]{:S(2)}) collective-permute-start(bf16[256,256]{1,0:T(8,128)(2,1)S(1)} %bitcast.207), channel_id=1, source_target_pairs={{0,2},{1,3},{2,0},{3,1},{4,6},{5,7},{6,4},{7,5},{8,10},{9,11},{10,... | collective-permute-start | bytes 393224 | tf_op jit(solution)/shard_map/ppermute | solution.py:40
  310.9 8.5 %collective-permute-start.3 = (bf16[256,256]{1,0:T(8,128)(2,1)S(1)}, bf16[256,256]{1,0:T(8,128)(2,1)S(1)}, u32[]{:S(2)}, u32[]{:S(2)}) collective-permute-start(bf16[256,256]{1,0:T(8,128)(2,1)S(1)} %bitcast.208), channel_id=1, source_target_pairs={{0,1},{1,2},{2,3},{3,0},{4,5},{5,6},{6,7},{7,4},{8,9},{9,10},{10,1... | collective-permute-start | bytes 393224 | tf_op jit(solution)/shard_map/ppermute | solution.py:40
  (53 other events, 467.0 us)

commit v5 on v4

--- a/solution.py
+++ b/solution.py
@@ -10,6 +10,7 @@
 LAYERS = 2
 DP = ("z_lo", "y", "core")
 MP = ("z_hi", "x")
+QUAD = ("z_lo", "core")
 
 
 epsilon = 1e-06
@@ -40,46 +41,44 @@
     return lax.ppermute(x, axis, [(k, (k + step) % n) for k in range(n)])
 
 
+def unsigned(index):
+    return index.astype(jnp.uint32)
+
+
 def pick(x, index):
-    return lax.dynamic_index_in_dim(x, index, 0, keepdims=False)
+    return lax.dynamic_slice_in_dim(x, index, 1, 0)[0]
 
 
 def total(parts):
     return sum(p.astype(f32) for p in parts)
 
 
-def y_stage(grads):
+def y_stage(grads, turns):
     joined = jnp.concatenate([g.astype(bf16) for g in grads], axis=1)
     rows, cols = joined.shape
     parts = jnp.moveaxis(joined.reshape(2, 4, 2, rows // 16, cols), 1, 0)
-    here = lax.axis_index("y")
-    sent = [pick(parts, (here + k) % 4) for k in range(1, 4)]
-    return [pick(parts, here)] + [moved(s, "y", k) for k, s in enumerate(sent, 1)], sent
-
-
-def quad_stage(parts):
-    axes = ("z_lo", "core")
-    here = lax.axis_index(axes)
-    return [pick(parts, here)] + [
-        lax.ppermute(pick(parts, here ^ k), axes, [(i, i ^ k) for i in range(4)]) for k in range(1, 4)
+    sent = [pick(parts, turns[k]) for k in range(1, 4)]
+    return [pick(parts, turns[0])] + [moved(s, "y", k) for k, s in enumerate(sent, 1)], sent
+
+
+def quad_stage(parts, turns):
+    return [pick(parts, turns[0])] + [
+        lax.ppermute(pick(parts, turns[k]), QUAD, [(i, i ^ k) for i in range(4)]) for k in range(1, 4)
     ]
 
 
 def normalize(stream):
     widened = stream.astype(f32)
     rscale = lax.rsqrt(jnp.mean(widened * widened, axis=-1, keepdims=True) + epsilon)
-    scaled = widened * rscale
-    return (scaled.astype(bf16), scaled, rscale)
-
-
-def norm_backward(scaled, rscale, upward):
-    inner = jnp.mean(upward * scaled, axis=-1, keepdims=True)
-    return rscale * (upward - scaled * inner)
-
-
-def norm_added(upstream, stream, grad):
-    _, scaled, rscale = normalize(stream)
-    return (upstream.astype(f32) + norm_backward(scaled, rscale, grad)).astype(bf16)
+    return lax.optimization_barrier((widened * rscale).astype(bf16))
+
+
+def norm_backward(stream, upward):
+    widened = after(stream, upward).astype(f32)
+    upward = upward.astype(f32)
+    rscale = lax.rsqrt(jnp.mean(widened * widened, axis=-1, keepdims=True) + epsilon)
+    inner = rscale * jnp.mean(upward * widened, axis=-1, keepdims=True)
+    return rscale * (upward - widened * rscale * inner)
 
 
 def smooth_gate(preact):
@@ -120,30 +119,40 @@
     rows, width = tokens.shape
     n = lax.axis_size(MP)
     share = rows // n
-    start = lax.axis_index(MP) * share
+    x_here, y_here, quad_here = (unsigned(lax.axis_index(a)) for a in ("x", "y", QUAD))
+    start, *places = lax.optimization_barrier((
+        unsigned(lax.axis_index(MP) * share),
+        *((x_here + k) & 3 for k in range(4)),
+        *((x_here - k) & 3 for k in range(4)),
+        *((y_here + k) & 3 for k in range(4)),
+        *(quad_here ^ k for k in range(4)),
+    ))
+    x_turns, x_slots, y_turns, quad_turns = (places[k : k + 4] for k in range(0, 16, 4))
 
     def part(x):
         return lax.dynamic_slice_in_dim(x, start, share, 0)
 
     live = (jnp.arange(SLATE)[None, :] < lengths[:, None]).astype(f32)
     triple = [triple_weight[l].reshape(width, -1) for l in range(LAYERS)]
-    saved, owned = [], []
+    saved = []
     stream = tokens
     stream_part = part(tokens)
     for l in range(LAYERS):
-        normed = normalize(stream)[0]
+        normed = normalize(stream)
         qkv = jnp.dot(normed, triple[l], preferred_element_type=f32).astype(bf16)
         queries, key_rows, values = (qkv[:, k * HD : (k + 1) * HD] for k in range(3))
         probs, context = attend(queries, key_rows, values, live)
         partial_att = contract_cols(context, output_weight[l]).astype(bf16)
+        if l == 0:
+            partial_att = after(partial_att, *places)
         mid_part = (stream_part.astype(f32) + share_rows(partial_att, MP)).astype(bf16)
         mid_stream = all_rows(mid_part, MP)
-        normed_mid = normalize(mid_stream)[0]
+        normed_mid = normalize(mid_stream)
         preact = jnp.dot(normed_mid, upward_weight[l], preferred_element_type=f32)
         activated = smooth_gate(preact).astype(bf16)
         partial_ffn = contract_cols(activated, downward_weight[l]).astype(bf16)
-        saved.append((normed, queries, key_rows, values, probs, context, normed_mid, preact, activated))
-        owned.append((stream_part, mid_part))
+        saved.append((normed, stream, queries, key_rows, values, probs, context,
+                      mid_stream, normed_mid, preact, activated))
         if l + 1 < LAYERS:
             stream_part = (mid_part.astype(f32) + share_rows(partial_ffn, MP)).astype(bf16)
             stream = all_rows(stream_part, MP)
@@ -151,36 +160,34 @@
     top = LAYERS - 1
     quarter = width // 4
     heads = triple_weight.shape[-1]
-    x_here = lax.axis_index("x")
-
-    normed, queries, key_rows, values, probs, context, normed_mid, preact, activated = saved[top]
-    stream_part, mid_part = owned[top]
-    upstream, upstream_part = cotangent, part(cotangent)
+
+    (normed, stream, queries, key_rows, values, probs, context,
+     mid_stream, normed_mid, preact, activated) = saved[top]
+    upstream = cotangent
     grad_act = jnp.dot(upstream, downward_weight[top], preferred_element_type=f32).astype(bf16)
     _, gate_back = jax.vjp(smooth_gate, preact)
     grad_preact = gate_back(grad_act.astype(f32))[0].astype(bf16)
     partial = contract_cols(grad_preact, upward_weight[top]).astype(bf16)
     shares = jnp.stack([partial_ffn[:, k * quarter : (k + 1) * quarter] for k in range(4)])
-    shares = [pick(shares, x_here)] + [
-        moved(pick(shares, (x_here + k) % 4), "x", k) for k in range(1, 4)
+    shares = [pick(shares, x_turns[0])] + [
+        moved(pick(shares, x_turns[k]), "x", k) for k in range(1, 4)
     ]
-    grad_normed = share_rows(partial, MP)
-    own = upstream_part = norm_added(upstream_part, mid_part, grad_normed)
+    own = share_rows(partial, MP).astype(bf16)
     shares = total(shares).astype(bf16).reshape(n, share, quarter)
     sent = jnp.concatenate([jnp.broadcast_to(own[None], (n, share, width)), shares], axis=2)
     came = lax.all_to_all(sent, MP, 0, 0, tiled=True)
-    grad_mid = came[:, :, :width].reshape(rows, width)
+    grad_normed = came[:, :, :width].reshape(rows, width)
     ffn_part = jnp.sum(came[:, :, width:].reshape(4, 4, share, quarter).astype(f32), axis=0)
     ffn_part = jnp.concatenate([ffn_part[k] for k in range(4)], axis=1)
     final_part = (mid_part.astype(f32) + ffn_part).astype(bf16)
+    grad_mid = (upstream.astype(f32) + norm_backward(mid_stream, grad_normed)).astype(bf16)
     grad_context = jnp.dot(grad_mid, output_weight[top], preferred_element_type=f32).astype(bf16)
     grad_qkv = attend_backward(probs, queries, key_rows, values, grad_context)
     partial = contract_cols(grad_qkv, triple[top]).astype(bf16).reshape(n, share, width)
     quarters = jnp.stack([final_part[:, k * quarter : (k + 1) * quarter] for k in range(4)])
     sent = jnp.concatenate([partial, jnp.tile(quarters, (4, 1, 1))], axis=2)
     came = lax.all_to_all(sent, MP, 0, 0, tiled=True)
-    grad_input = jnp.sum(came[:, :, :width].astype(f32), axis=0)
-    own = upstream_part = norm_added(upstream_part, stream_part, grad_input)
+    own = jnp.sum(came[:, :, :width].astype(f32), axis=0).astype(bf16)
     column = came[:, :, width:].reshape(rows, quarter)
     wide1 = [
         contract_rows(normed_mid, grad_preact),
@@ -188,19 +195,20 @@
         contract_rows(normed, grad_qkv),
         contract_rows(grad_mid, context),
     ]
-    sums1, sent1 = y_stage(wide1)
-    upstream = all_rows(after(own, *sent1), MP)
-    normed, queries, key_rows, values, probs, context, normed_mid, preact, activated = saved[0]
-    mid_part = owned[0][1]
+    sums1, sent1 = y_stage(wide1, y_turns)
+    grad_input = all_rows(after(own, *sent1), MP)
+    upstream = (grad_mid.astype(f32) + norm_backward(stream, grad_input)).astype(bf16)
+    (normed, stream, queries, key_rows, values, probs, context,
+     mid_stream, normed_mid, preact, activated) = saved[0]
     grad_act = jnp.dot(upstream, downward_weight[0], preferred_element_type=f32).astype(bf16)
     _, gate_back = jax.vjp(smooth_gate, preact)
     grad_preact = gate_back(grad_act.astype(f32))[0].astype(bf16)
     partial = contract_cols(grad_preact, upward_weight[0]).astype(bf16)
-    grad_normed = share_rows(partial, MP)
-    own = norm_added(upstream_part, mid_part, grad_normed)
+    own = share_rows(partial, MP).astype(bf16)
     wide0 = [contract_rows(normed_mid, grad_preact), contract_rows(upstream, activated)]
-    sums0, sent0 = y_stage(wide0)
-    grad_mid = all_rows(after(own, *sent0), MP)
+    sums0, sent0 = y_stage(wide0, y_turns)
+    grad_normed = all_rows(after(own, *sent0), MP)
+    grad_mid = (upstream.astype(f32) + norm_backward(mid_stream, grad_normed)).astype(bf16)
     grad_context = jnp.dot(grad_mid, output_weight[0], preferred_element_type=f32).astype(bf16)
     grad_qkv = attend_backward(probs, queries, key_rows, values, grad_context)
     late = [contract_rows(normed, grad_qkv), contract_rows(grad_mid, context)]
@@ -210,10 +218,10 @@
     sums1 = total(sums1).astype(bf16)
     sums0 = total(sums0).astype(bf16)
     sums = jnp.concatenate([sums1, sums0], axis=3)
-    sums = quad_stage(sums.reshape(4, *sums.shape[2:]))
+    sums = quad_stage(sums.reshape(4, *sums.shape[2:]), quad_turns)
     late = share_rows(late, DP)
     final_stream = jnp.concatenate(
-        [lax.select_n((x_here - k) % 4, *columns) for k in range(4)], axis=1
+        [lax.select_n(x_slots[k].astype(jnp.int32), *columns) for k in range(4)], axis=1
     )
     sums = total(sums)
 

time: 324 us -> 325 us (level)
  blocking collectives: 77.6 us -> 120 us
  waiting for transfers between devices: 83.2 us -> 52.8 us
  starting transfers between devices: 96.1 us -> 89 us
    all_to_all x2 -> x3, blocking collectives: 37.2 us -> 64.1 us  [share_rows(): blocks = lax.all_to_all(blocks, axis, 0, 0, tiled=True)]
    all_to_all x4 -> x3, waiting for transfers between devices: 17.3 us -> 0.01 us  [share_rows(): blocks = lax.all_to_all(blocks, axis, 0, 0, tiled=True)]
    all_to_all x2 -> x3, blocking collectives: 40.5 us -> 55.9 us  [all_rows(): blocks = lax.all_to_all(copies, axis, 0, 0, tiled=True)]
    all_to_all x3 -> x2, waiting for transfers between devices: 25.5 us -> 12.9 us  [all_rows(): blocks = lax.all_to_all(copies, axis, 0, 0, tiled=True)]
    all_to_all x4 -> x3, starting transfers between devices: 27.9 us -> 16.6 us  [share_rows(): blocks = lax.all_to_all(blocks, axis, 0, 0, tiled=True)]
    all_to_all x3 -> x2, starting transfers between devices: 14.5 us -> 13.2 us  [all_rows(): blocks = lax.all_to_all(copies, axis, 0, 0, tiled=True)]
  transfers between devices with their start and end apart: 24 -> 22, of which waited for: 12 -> 10; matrix products, arithmetic and copies ran while one was open for 9% -> 8% of each run, Pallas kernels for 0% -> 0%
where the time goes in v5:
time: 325 us; the launch traced here: 324 us
  blocking collectives  120 us (37%)
  starting transfers between devices  89 us (27%)
  waiting for transfers between devices  52.8 us (16%)
  other arithmetic  22.9 us (7%)
  local copies, waits for them, and re-layouts  21 us (6%)
  matrix products  15.5 us (5%)
    all_to_all x3, blocking collectives, share_rows(): blocks = lax.all_to_all(blocks, axis, 0, 0, tiled=True)  64.1 us
    all_to_all x3, blocking collectives, all_rows(): blocks = lax.all_to_all(copies, axis, 0, 0, tiled=True)  55.9 us
    ppermute x3, starting transfers between devices, quad_stage(): lax.ppermute(pick(parts, turns[k]), QUAD, [(i, i ^ k) for i in range(4)])  30.3 us
    all_to_all x2, waiting for transfers between devices, step(): came = lax.all_to_all(sent, MP, 0, 0, tiled=True)  23.3 us
    ppermute x12, starting transfers between devices, moved(): return lax.ppermute(x, axis, [(k, (k + step) % n) for k in range(n)])  17.4 us
    all_to_all x3, starting transfers between devices, share_rows(): blocks = lax.all_to_all(blocks, axis, 0, 0, tiled=True)  16.6 us
    ppermute x12, waiting for transfers between devices, moved(): return lax.ppermute(x, axis, [(k, (k + step) % n) for k in range(n)])  16.6 us
    all_to_all x2, starting transfers between devices, all_rows(): blocks = lax.all_to_all(copies, axis, 0, 0, tiled=True)  13.2 us
  transfers between devices with their start and end apart: 22, of which 10 were waited for; matrix products, arithmetic and copies ran while one was open for 8% of the time, Pallas kernels for 0%

profile of v5, /device:TPU:1, one launch (start us, length us, event | category | flops | bytes accessed | tf_op | source)
XLA Modules:
  0.0 323.6 jit_solution(14103163564564764899)
XLA Ops:
  6.0 26.2 %all_to_all.65 = bf16[16,16,1024]{2,1,0:T(8,128)(2,1)S(1)} all-to-all(bf16[16,16,1024]{2,1,0:T(8,128)(2,1)S(1)} %bitcast.199), channel_id=1, replica_groups=mesh['z_lo'=2,'y'=4,'core'=2,'z_hi'=4,'x'=4] {'z_hi','x'}, dimensions={0} | all-to-all | bytes 1048576 | tf_op jit(solution)/shard_map/all_to_all | solution.py:24
  33.2 22.6 %all_to_all.66 = bf16[16,16,1024]{2,1,0:T(8,128)(2,1)S(1)} all-to-all(bf16[16,16,1024]{2,1,0:T(8,128)(2,1)S(1)} %broadcast_in_dim.12), channel_id=1, replica_groups=mesh['z_lo'=2,'y'=4,'core'=2,'z_hi'=4,'x'=4] {'z_hi','x'}, dimensions={0} | all-to-all | bytes 1048576 | tf_op jit(solution)/shard_map/all_to_all | solution.py:31
  58.1 20.7 %all_to_all.67 = bf16[16,16,1024]{2,1,0:T(8,128)(2,1)S(1)} all-to-all(bf16[16,16,1024]{2,1,0:T(8,128)(2,1)S(1)} %bitcast.203), channel_id=1, replica_groups=mesh['z_lo'=2,'y'=4,'core'=2,'z_hi'=4,'x'=4] {'z_hi','x'}, dimensions={0} | all-to-all | bytes 1048576 | tf_op jit(solution)/shard_map/all_to_all | solution.py:24
  78.9 17.0 %all_to_all.68 = bf16[16,16,1024]{2,1,0:T(8,128)(2,1)S(1)} all-to-all(bf16[16,16,1024]{2,1,0:T(8,128)(2,1)S(1)} %broadcast_in_dim.13), channel_id=1, replica_groups=mesh['z_lo'=2,'y'=4,'core'=2,'z_hi'=4,'x'=4] {'z_hi','x'}, dimensions={0} | all-to-all | bytes 1048576 | tf_op jit(solution)/shard_map/all_to_all | solution.py:31
  97.7 17.2 %all_to_all.69 = bf16[16,16,1024]{2,1,0:T(8,128)(2,1)S(1)} all-to-all(bf16[16,16,1024]{2,1,0:T(8,128)(2,1)S(1)} %bitcast.200), channel_id=1, replica_groups=mesh['z_lo'=2,'y'=4,'core'=2,'z_hi'=4,'x'=4] {'z_hi','x'}, dimensions={0} | all-to-all | bytes 1048576 | tf_op jit(solution)/shard_map/all_to_all | solution.py:24
  115.7 16.3 %all_to_all.70 = bf16[16,16,1024]{2,1,0:T(8,128)(2,1)S(1)} all-to-all(bf16[16,16,1024]{2,1,0:T(8,128)(2,1)S(1)} %broadcast_in_dim.14), channel_id=1, replica_groups=mesh['z_lo'=2,'y'=4,'core'=2,'z_hi'=4,'x'=4] {'z_hi','x'}, dimensions={0} | all-to-all | bytes 1048576 | tf_op jit(solution)/shard_map/all_to_all | solution.py:31
  137.0 3.7 %all-to-all-start.6 = ((bf16[16,16,1024]{2,1,0:T(8,128)(2,1)}), bf16[16,16,1024]{2,1,0:T(8,128)(2,1)S(1)}, u32[]{:S(2)}, u32[]{:S(2)}) async-start(bf16[16,16,1024]{2,1,0:T(8,128)(2,1)} %bitcast.197), calls=%async_computation.6 | async-start | bytes 1048576 | tf_op jit(solution)/shard_map/all_to_all | solution.py:24
  148.3 3.2 collective-permute-done.1
  155.5 6.8 %all-to-all-start.7 = ((bf16[16,16,1280]{2,1,0:T(8,128)(2,1)}), bf16[16,16,1280]{2,1,0:T(8,128)(2,1)}, u32[]{:S(2)}, u32[]{:S(2)}) async-start(bf16[16,16,1280]{2,1,0:T(8,128)(2,1)} %pad_maximum_fusion.2), calls=%async_computation.7 | async-start | bytes 1310720 | tf_op jit(solution)/shard_map/all_to_all | solution.py:178
  162.4 12.1 %all-to-all-done.7 = bf16[16,16,1280]{2,1,0:T(8,128)(2,1)} async-done(((bf16[16,16,1280]{2,1,0:T(8,128)(2,1)}), bf16[16,16,1280]{2,1,0:T(8,128)(2,1)}, u32[]{:S(2)}, u32[]{:S(2)}) %all-to-all-start.7) | async-done | bytes 655392 | tf_op jit(solution)/shard_map/all_to_all | solution.py:178
  180.8 4.6 %all-to-all-start.8 = ((bf16[16,16,1280]{2,1,0:T(8,128)(2,1)}), bf16[16,16,1280]{2,1,0:T(8,128)(2,1)}, u32[]{:S(2)}, u32[]{:S(2)}) async-start(bf16[16,16,1280]{2,1,0:T(8,128)(2,1)} %pad_maximum_fusion.3), calls=%async_computation.8 | async-start | bytes 1310720 | tf_op jit(solution)/shard_map/all_to_all | solution.py:189
  190.8 11.2 %all-to-all-done.8 = bf16[16,16,1280]{2,1,0:T(8,128)(2,1)} async-done(((bf16[16,16,1280]{2,1,0:T(8,128)(2,1)}), bf16[16,16,1280]{2,1,0:T(8,128)(2,1)}, u32[]{:S(2)}, u32[]{:S(2)}) %all-to-all-start.8) | async-done | bytes 655392 | tf_op jit(solution)/shard_map/all_to_all | solution.py:189
  204.0 4.2 %all-to-all-start.9 = ((bf16[16,16,1024]{2,1,0:T(8,128)(2,1)}), bf16[16,16,1024]{2,1,0:T(8,128)(2,1)}, u32[]{:S(2)}, u32[]{:S(2)}) async-start(bf16[16,16,1024]{2,1,0:T(8,128)(2,1)} %broadcast_in_dim.16), calls=%async_computation.9 | async-start | bytes 1048576 | tf_op jit(solution)/shard_map/all_to_all | solution.py:31
  208.3 12.9 %all-to-all-done.9 = bf16[16,16,1024]{2,1,0:T(8,128)(2,1)} async-done(((bf16[16,16,1024]{2,1,0:T(8,128)(2,1)}), bf16[16,16,1024]{2,1,0:T(8,128)(2,1)}, u32[]{:S(2)}, u32[]{:S(2)}) %all-to-all-start.9) | async-done | bytes 524320 | tf_op jit(solution)/shard_map/all_to_all | solution.py:31
  226.6 7.4 %all-to-all-start.10 = ((bf16[16,16,1024]{2,1,0:T(8,128)(2,1)}), bf16[16,16,1024]{2,1,0:T(8,128)(2,1)S(1)}, u32[]{:S(2)}, u32[]{:S(2)}) async-start(bf16[16,16,1024]{2,1,0:T(8,128)(2,1)} %bitcast.196), calls=%async_computation.10 | async-start | bytes 1048576 | tf_op jit(solution)/shard_map/all_to_all | solution.py:24
  234.0 5.8 %collective-permute-start.8 = (bf16[2,2,64,768]{3,2,1,0:T(8,128)(2,1)}, bf16[2,2,64,768]{3,2,1,0:T(8,128)(2,1)}, u32[]{:S(2)}, u32[]{:S(2)}) collective-permute-start(bf16[2,2,64,768]{3,2,1,0:T(8,128)(2,1)} %get-tuple-element.69), channel_id=1, source_target_pairs={{0,96},{32,0},{64,32},{96,64},{1,97},{33,1},{65,33},{97,65},{2,98}... | collective-permute-start | bytes 1179656 | tf_op jit(solution)/shard_map/ppermute | solution.py:41
  243.6 2.3 copy.29
  245.9 2.0 dynamic-slice_bitcast_fusion.3
  252.2 8.9 %all-to-all-start.11 = ((bf16[16,16,1024]{2,1,0:T(8,128)(2,1)}), bf16[16,16,1024]{2,1,0:T(8,128)(2,1)S(1)}, u32[]{:S(2)}, u32[]{:S(2)}) async-start(bf16[16,16,1024]{2,1,0:T(8,128)(2,1)} %broadcast_in_dim.17), calls=%async_computation.11 | async-start | bytes 1048576 | tf_op jit(solution)/shard_map/all_to_all | solution.py:31
  263.6 4.3 %collective-permute-done.9 = bf16[2,2,64,512]{3,2,1,0:T(8,128)(2,1)S(1)} collective-permute-done((bf16[2,2,64,512]{3,2,1,0:T(8,128)(2,1)S(1)}, bf16[2,2,64,512]{3,2,1,0:T(8,128)(2,1)S(1)}, u32[]{:S(2)}, u32[]{:S(2)}) %collective-permute-start.9) | collective-permute-done | bytes 262176 | tf_op jit(solution)/shard_map/ppermute | solution.py:41
  270.0 29.0 %collective-permute-start.12 = (bf16[64,1280]{1,0:T(8,128)(2,1)}, bf16[64,1280]{1,0:T(8,128)(2,1)S(1)}, u32[]{:S(2)}, u32[]{:S(2)}) collective-permute-start(bf16[64,1280]{1,0:T(8,128)(2,1)} %get-tuple-element.77), channel_id=1, source_target_pairs={{0,16},{16,0},{128,144},{144,128},{1,17},{17,1},{129,145},{145,129... | collective-permute-start | bytes 491528 | tf_op jit(solution)/shard_map/ppermute | solution.py:66
  304.1 5.5 %all-to-all-start.12 = ((bf16[16,64,256]{2,1,0:T(8,128)(2,1)}), bf16[16,64,256]{2,1,0:T(8,128)(2,1)S(1)}, u32[]{:S(2)}, u32[]{:S(2)}) async-start(bf16[16,64,256]{2,1,0:T(8,128)(2,1)} %bitcast.50), calls=%async_computation.12 | async-start | bytes 1048576 | tf_op jit(solution)/shard_map/all_to_all | solution.py:24
  314.7 2.3 collective-permute-done.4
  317.0 3.9 %collective-permute-done.3 = bf16[256,256]{1,0:T(8,128)(2,1)S(1)} collective-permute-done((bf16[256,256]{1,0:T(8,128)(2,1)S(1)}, bf16[256,256]{1,0:T(8,128)(2,1)S(1)}, u32[]{:S(2)}, u32[]{:S(2)}) %collective-permute-start.3) | collective-permute-done | bytes 131104 | tf_op jit(solution)/shard_map/ppermute | solution.py:41
  (231 shorter events, 71.0 us)
Async XLA Ops:
  4.3 28.0 %copy-start.25 = (bf16[256,192]{0,1:T(8,128)(2,1)}, bf16[256,192]{0,1:T(8,128)(2,1)S(1)}, u32[]{:S(2)}) copy-start(bf16[256,192]{0,1:T(8,128)(2,1)S(1)} %convolution_convert_fusion.18) | copy-start | bytes 294916
  137.0 15.2 %all-to-all-start.6 = ((bf16[16,16,1024]{2,1,0:T(8,128)(2,1)}), bf16[16,16,1024]{2,1,0:T(8,128)(2,1)S(1)}, u32[]{:S(2)}, u32[]{:S(2)}) async-start(bf16[16,16,1024]{2,1,0:T(8,128)(2,1)} %bitcast.197), calls=%async_computation.6 | async-start | bytes 1048576 | tf_op jit(solution)/shard_map/all_to_all | solution.py:24
  142.3 5.8 %collective-permute-start = (bf16[256,256]{1,0:T(8,128)(2,1)S(1)}, bf16[256,256]{1,0:T(8,128)(2,1)S(1)}, u32[]{:S(2)}, u32[]{:S(2)}) collective-permute-start(bf16[256,256]{1,0:T(8,128)(2,1)S(1)} %get-tuple-element.84), channel_id=1, source_target_pairs={{0,1},{1,2},{2,3},{3,0},{4,5},{5,6},{6,7},{7,4},{8,9},{9,10},{10,1... | collective-permute-start | bytes 393224 | tf_op jit(solution)/shard_map/ppermute | solution.py:41
  143.8 4.5 %collective-permute-start.2 = (bf16[256,256]{1,0:T(8,128)(2,1)S(1)}, bf16[256,256]{1,0:T(8,128)(2,1)S(1)}, u32[]{:S(2)}, u32[]{:S(2)}) collective-permute-start(bf16[256,256]{1,0:T(8,128)(2,1)S(1)} %get-tuple-element.85), channel_id=1, source_target_pairs={{0,3},{1,0},{2,1},{3,2},{4,7},{5,4},{6,5},{7,6},{8,11},{9,8},{10,9... | collective-permute-start | bytes 393224 | tf_op jit(solution)/shard_map/ppermute | solution.py:41
  145.1 6.4 %collective-permute-start.1 = (bf16[256,256]{1,0:T(8,128)(2,1)S(1)}, bf16[256,256]{1,0:T(8,128)(2,1)S(1)}, u32[]{:S(2)}, u32[]{:S(2)}) collective-permute-start(bf16[256,256]{1,0:T(8,128)(2,1)S(1)} %get-tuple-element.86), channel_id=1, source_target_pairs={{0,2},{1,3},{2,0},{3,1},{4,6},{5,7},{6,4},{7,5},{8,10},{9,11},{10,... | collective-permute-start | bytes 393224 | tf_op jit(solution)/shard_map/ppermute | solution.py:41
  155.5 19.0 %all-to-all-start.7 = ((bf16[16,16,1280]{2,1,0:T(8,128)(2,1)}), bf16[16,16,1280]{2,1,0:T(8,128)(2,1)}, u32[]{:S(2)}, u32[]{:S(2)}) async-start(bf16[16,16,1280]{2,1,0:T(8,128)(2,1)} %pad_maximum_fusion.2), calls=%async_computation.7 | async-start | bytes 1310720 | tf_op jit(solution)/shard_map/all_to_all | solution.py:178
  180.8 21.2 %all-to-all-start.8 = ((bf16[16,16,1280]{2,1,0:T(8,128)(2,1)}), bf16[16,16,1280]{2,1,0:T(8,128)(2,1)}, u32[]{:S(2)}, u32[]{:S(2)}) async-start(bf16[16,16,1280]{2,1,0:T(8,128)(2,1)} %pad_maximum_fusion.3), calls=%async_computation.8 | async-start | bytes 1310720 | tf_op jit(solution)/shard_map/all_to_all | solution.py:189
  204.0 17.2 %all-to-all-start.9 = ((bf16[16,16,1024]{2,1,0:T(8,128)(2,1)}), bf16[16,16,1024]{2,1,0:T(8,128)(2,1)}, u32[]{:S(2)}, u32[]{:S(2)}) async-start(bf16[16,16,1024]{2,1,0:T(8,128)(2,1)} %broadcast_in_dim.16), calls=%async_computation.9 | async-start | bytes 1048576 | tf_op jit(solution)/shard_map/all_to_all | solution.py:31
  226.6 24.7 %all-to-all-start.10 = ((bf16[16,16,1024]{2,1,0:T(8,128)(2,1)}), bf16[16,16,1024]{2,1,0:T(8,128)(2,1)S(1)}, u32[]{:S(2)}, u32[]{:S(2)}) async-start(bf16[16,16,1024]{2,1,0:T(8,128)(2,1)} %bitcast.196), calls=%async_computation.10 | async-start | bytes 1048576 | tf_op jit(solution)/shard_map/all_to_all | solution.py:24
  234.0 27.1 %collective-permute-start.8 = (bf16[2,2,64,768]{3,2,1,0:T(8,128)(2,1)}, bf16[2,2,64,768]{3,2,1,0:T(8,128)(2,1)}, u32[]{:S(2)}, u32[]{:S(2)}) collective-permute-start(bf16[2,2,64,768]{3,2,1,0:T(8,128)(2,1)} %get-tuple-element.69), channel_id=1, source_target_pairs={{0,96},{32,0},{64,32},{96,64},{1,97},{33,1},{65,33},{97,65},{2,98}... | collective-permute-start | bytes 1179656 | tf_op jit(solution)/shard_map/ppermute | solution.py:41
  239.8 21.5 %collective-permute-start.7 = (bf16[2,2,64,768]{3,2,1,0:T(8,128)(2,1)}, bf16[2,2,64,768]{3,2,1,0:T(8,128)(2,1)}, u32[]{:S(2)}, u32[]{:S(2)}) collective-permute-start(bf16[2,2,64,768]{3,2,1,0:T(8,128)(2,1)} %get-tuple-element.70), channel_id=1, source_target_pairs={{0,64},{32,96},{64,0},{96,32},{1,65},{33,97},{65,1},{97,33},{2,66}... | collective-permute-start | bytes 1179656 | tf_op jit(solution)/shard_map/ppermute | solution.py:41
  240.1 21.2 %collective-permute-start.6 = (bf16[2,2,64,768]{3,2,1,0:T(8,128)(2,1)}, bf16[2,2,64,768]{3,2,1,0:T(8,128)(2,1)}, u32[]{:S(2)}, u32[]{:S(2)}) collective-permute-start(bf16[2,2,64,768]{3,2,1,0:T(8,128)(2,1)} %get-tuple-element.71), channel_id=1, source_target_pairs={{0,32},{32,64},{64,96},{96,0},{1,33},{33,65},{65,97},{97,1},{2,34}... | collective-permute-start | bytes 1179656 | tf_op jit(solution)/shard_map/ppermute | solution.py:41
  247.9 15.8 %collective-permute-start.11 = (bf16[2,2,64,512]{3,2,1,0:T(8,128)(2,1)}, bf16[2,2,64,512]{3,2,1,0:T(8,128)(2,1)}, u32[]{:S(2)}, u32[]{:S(2)}) collective-permute-start(bf16[2,2,64,512]{3,2,1,0:T(8,128)(2,1)} %get-tuple-element.72), channel_id=1, source_target_pairs={{0,96},{32,0},{64,32},{96,64},{1,97},{33,1},{65,33},{97,65},{2,98}... | collective-permute-start | bytes 786440 | tf_op jit(solution)/shard_map/ppermute | solution.py:41
  249.8 13.9 %collective-permute-start.10 = (bf16[2,2,64,512]{3,2,1,0:T(8,128)(2,1)}, bf16[2,2,64,512]{3,2,1,0:T(8,128)(2,1)}, u32[]{:S(2)}, u32[]{:S(2)}) collective-permute-start(bf16[2,2,64,512]{3,2,1,0:T(8,128)(2,1)} %get-tuple-element.73), channel_id=1, source_target_pairs={{0,64},{32,96},{64,0},{96,32},{1,65},{33,97},{65,1},{97,33},{2,66}... | collective-permute-start | bytes 786440 | tf_op jit(solution)/shard_map/ppermute | solution.py:41
  252.2 48.1 %all-to-all-start.11 = ((bf16[16,16,1024]{2,1,0:T(8,128)(2,1)}), bf16[16,16,1024]{2,1,0:T(8,128)(2,1)S(1)}, u32[]{:S(2)}, u32[]{:S(2)}) async-start(bf16[16,16,1024]{2,1,0:T(8,128)(2,1)} %broadcast_in_dim.17), calls=%async_computation.11 | async-start | bytes 1048576 | tf_op jit(solution)/shard_map/all_to_all | solution.py:31
  261.1 6.8 %collective-permute-start.9 = (bf16[2,2,64,512]{3,2,1,0:T(8,128)(2,1)S(1)}, bf16[2,2,64,512]{3,2,1,0:T(8,128)(2,1)S(1)}, u32[]{:S(2)}, u32[]{:S(2)}) collective-permute-start(bf16[2,2,64,512]{3,2,1,0:T(8,128)(2,1)S(1)} %get-tuple-element.74), channel_id=1, source_target_pairs={{0,32},{32,64},{64,96},{96,0},{1,33},{33,65},{65,97},{97,1},{2,34}... | collective-permute-start | bytes 786440 | tf_op jit(solution)/shard_map/ppermute | solution.py:41
  269.2 31.4 %copy-start.8 = (bf16[256,1024]{1,0:T(8,128)(2,1)S(1)}, bf16[256,1024]{1,0:T(8,128)(2,1)}, u32[]{:S(2)}) copy-start(bf16[256,1024]{1,0:T(8,128)(2,1)} %copy-done.7) | copy-start | bytes 1572868
  270.0 39.7 %collective-permute-start.12 = (bf16[64,1280]{1,0:T(8,128)(2,1)}, bf16[64,1280]{1,0:T(8,128)(2,1)S(1)}, u32[]{:S(2)}, u32[]{:S(2)}) collective-permute-start(bf16[64,1280]{1,0:T(8,128)(2,1)} %get-tuple-element.77), channel_id=1, source_target_pairs={{0,16},{16,0},{128,144},{144,128},{1,17},{17,1},{129,145},{145,129... | collective-permute-start | bytes 491528 | tf_op jit(solution)/shard_map/ppermute | solution.py:66
  298.9 10.7 %collective-permute-start.14 = (bf16[64,1280]{1,0:T(8,128)(2,1)S(1)}, bf16[64,1280]{1,0:T(8,128)(2,1)S(1)}, u32[]{:S(2)}, u32[]{:S(2)}) collective-permute-start(bf16[64,1280]{1,0:T(8,128)(2,1)S(1)} %get-tuple-element.78), channel_id=1, source_target_pairs={{0,144},{16,128},{128,16},{144,0},{1,145},{17,129},{129,17},{145,1... | collective-permute-start | bytes 491528 | tf_op jit(solution)/shard_map/ppermute | solution.py:66
  298.9 10.7 %collective-permute-start.13 = (bf16[64,1280]{1,0:T(8,128)(2,1)S(1)}, bf16[64,1280]{1,0:T(8,128)(2,1)S(1)}, u32[]{:S(2)}, u32[]{:S(2)}) collective-permute-start(bf16[64,1280]{1,0:T(8,128)(2,1)S(1)} %get-tuple-element.79), channel_id=1, source_target_pairs={{0,128},{16,144},{128,0},{144,16},{1,129},{17,145},{129,1},{145,17... | collective-permute-start | bytes 491528 | tf_op jit(solution)/shard_map/ppermute | solution.py:66
  304.1 17.8 %all-to-all-start.12 = ((bf16[16,64,256]{2,1,0:T(8,128)(2,1)}), bf16[16,64,256]{2,1,0:T(8,128)(2,1)S(1)}, u32[]{:S(2)}, u32[]{:S(2)}) async-start(bf16[16,64,256]{2,1,0:T(8,128)(2,1)} %bitcast.50), calls=%async_computation.12 | async-start | bytes 1048576 | tf_op jit(solution)/shard_map/all_to_all | solution.py:24
  309.8 4.9 %collective-permute-start.5 = (bf16[256,256]{1,0:T(8,128)(2,1)S(1)}, bf16[256,256]{1,0:T(8,128)(2,1)S(1)}, u32[]{:S(2)}, u32[]{:S(2)}) collective-permute-start(bf16[256,256]{1,0:T(8,128)(2,1)S(1)} %bitcast.206), channel_id=1, source_target_pairs={{0,3},{1,0},{2,1},{3,2},{4,7},{5,4},{6,5},{7,6},{8,11},{9,8},{10,9... | collective-permute-start | bytes 393224 | tf_op jit(solution)/shard_map/ppermute | solution.py:41
  311.3 5.7 %collective-permute-start.4 = (bf16[256,256]{1,0:T(8,128)(2,1)S(1)}, bf16[256,256]{1,0:T(8,128)(2,1)S(1)}, u32[]{:S(2)}, u32[]{:S(2)}) collective-permute-start(bf16[256,256]{1,0:T(8,128)(2,1)S(1)} %bitcast.207), channel_id=1, source_target_pairs={{0,2},{1,3},{2,0},{3,1},{4,6},{5,7},{6,4},{7,5},{8,10},{9,11},{10,... | collective-permute-start | bytes 393224 | tf_op jit(solution)/shard_map/ppermute | solution.py:41
  311.9 9.0 %collective-permute-start.3 = (bf16[256,256]{1,0:T(8,128)(2,1)S(1)}, bf16[256,256]{1,0:T(8,128)(2,1)S(1)}, u32[]{:S(2)}, u32[]{:S(2)}) collective-permute-start(bf16[256,256]{1,0:T(8,128)(2,1)S(1)} %bitcast.208), channel_id=1, source_target_pairs={{0,1},{1,2},{2,3},{3,0},{4,5},{5,6},{6,7},{7,4},{8,9},{9,10},{10,1... | collective-permute-start | bytes 393224 | tf_op jit(solution)/shard_map/ppermute | solution.py:41
  (41 other events, 181.0 us)

commit v6 on v4

--- a/solution.py
+++ b/solution.py
@@ -75,11 +75,6 @@
 def norm_backward(scaled, rscale, upward):
     inner = jnp.mean(upward * scaled, axis=-1, keepdims=True)
     return rscale * (upward - scaled * inner)
-
-
-def norm_added(upstream, stream, grad):
-    _, scaled, rscale = normalize(stream)
-    return (upstream.astype(f32) + norm_backward(scaled, rscale, grad)).astype(bf16)
 
 
 def smooth_gate(preact):
@@ -127,23 +122,23 @@
 
     live = (jnp.arange(SLATE)[None, :] < lengths[:, None]).astype(f32)
     triple = [triple_weight[l].reshape(width, -1) for l in range(LAYERS)]
-    saved, owned = [], []
+    saved = []
     stream = tokens
     stream_part = part(tokens)
     for l in range(LAYERS):
-        normed = normalize(stream)[0]
+        normed, scaled, rscale = normalize(stream)
         qkv = jnp.dot(normed, triple[l], preferred_element_type=f32).astype(bf16)
         queries, key_rows, values = (qkv[:, k * HD : (k + 1) * HD] for k in range(3))
         probs, context = attend(queries, key_rows, values, live)
         partial_att = contract_cols(context, output_weight[l]).astype(bf16)
         mid_part = (stream_part.astype(f32) + share_rows(partial_att, MP)).astype(bf16)
         mid_stream = all_rows(mid_part, MP)
-        normed_mid = normalize(mid_stream)[0]
+        normed_mid, scaled_mid, rscale_mid = normalize(mid_stream)
         preact = jnp.dot(normed_mid, upward_weight[l], preferred_element_type=f32)
         activated = smooth_gate(preact).astype(bf16)
         partial_ffn = contract_cols(activated, downward_weight[l]).astype(bf16)
-        saved.append((normed, queries, key_rows, values, probs, context, normed_mid, preact, activated))
-        owned.append((stream_part, mid_part))
+        saved.append((normed, scaled, rscale, queries, key_rows, values, probs, context,
+                      scaled_mid, rscale_mid, normed_mid, preact, activated))
         if l + 1 < LAYERS:
             stream_part = (mid_part.astype(f32) + share_rows(partial_ffn, MP)).astype(bf16)
             stream = all_rows(stream_part, MP)
@@ -153,9 +148,9 @@
     heads = triple_weight.shape[-1]
     x_here = lax.axis_index("x")
 
-    normed, queries, key_rows, values, probs, context, normed_mid, preact, activated = saved[top]
-    stream_part, mid_part = owned[top]
-    upstream, upstream_part = cotangent, part(cotangent)
+    (normed, scaled, rscale, queries, key_rows, values, probs, context,
+     scaled_mid, rscale_mid, normed_mid, preact, activated) = saved[top]
+    upstream = cotangent
     grad_act = jnp.dot(upstream, downward_weight[top], preferred_element_type=f32).astype(bf16)
     _, gate_back = jax.vjp(smooth_gate, preact)
     grad_preact = gate_back(grad_act.astype(f32))[0].astype(bf16)
@@ -164,23 +159,22 @@
     shares = [pick(shares, x_here)] + [
         moved(pick(shares, (x_here + k) % 4), "x", k) for k in range(1, 4)
     ]
-    grad_normed = share_rows(partial, MP)
-    own = upstream_part = norm_added(upstream_part, mid_part, grad_normed)
+    own = share_rows(partial, MP).astype(bf16)
     shares = total(shares).astype(bf16).reshape(n, share, quarter)
     sent = jnp.concatenate([jnp.broadcast_to(own[None], (n, share, width)), shares], axis=2)
-    came = lax.all_to_all(sent, MP, 0, 0, tiled=True)
-    grad_mid = came[:, :, :width].reshape(rows, width)
+    came = lax.all_to_all(after(sent, rscale_mid), MP, 0, 0, tiled=True)
+    grad_normed = came[:, :, :width].reshape(rows, width).astype(f32)
     ffn_part = jnp.sum(came[:, :, width:].reshape(4, 4, share, quarter).astype(f32), axis=0)
     ffn_part = jnp.concatenate([ffn_part[k] for k in range(4)], axis=1)
     final_part = (mid_part.astype(f32) + ffn_part).astype(bf16)
+    grad_mid = (upstream.astype(f32) + norm_backward(scaled_mid, rscale_mid, grad_normed)).astype(bf16)
     grad_context = jnp.dot(grad_mid, output_weight[top], preferred_element_type=f32).astype(bf16)
     grad_qkv = attend_backward(probs, queries, key_rows, values, grad_context)
     partial = contract_cols(grad_qkv, triple[top]).astype(bf16).reshape(n, share, width)
     quarters = jnp.stack([final_part[:, k * quarter : (k + 1) * quarter] for k in range(4)])
     sent = jnp.concatenate([partial, jnp.tile(quarters, (4, 1, 1))], axis=2)
     came = lax.all_to_all(sent, MP, 0, 0, tiled=True)
-    grad_input = jnp.sum(came[:, :, :width].astype(f32), axis=0)
-    own = upstream_part = norm_added(upstream_part, stream_part, grad_input)
+    own = jnp.sum(came[:, :, :width].astype(f32), axis=0).astype(bf16)
     column = came[:, :, width:].reshape(rows, quarter)
     wide1 = [
         contract_rows(normed_mid, grad_preact),
@@ -189,18 +183,19 @@
         contract_rows(grad_mid, context),
     ]
     sums1, sent1 = y_stage(wide1)
-    upstream = all_rows(after(own, *sent1), MP)
-    normed, queries, key_rows, values, probs, context, normed_mid, preact, activated = saved[0]
-    mid_part = owned[0][1]
+    grad_input = all_rows(after(own, rscale, *sent1), MP).astype(f32)
+    upstream = (grad_mid.astype(f32) + norm_backward(scaled, rscale, grad_input)).astype(bf16)
+    (normed, scaled, rscale, queries, key_rows, values, probs, context,
+     scaled_mid, rscale_mid, normed_mid, preact, activated) = saved[0]
     grad_act = jnp.dot(upstream, downward_weight[0], preferred_element_type=f32).astype(bf16)
     _, gate_back = jax.vjp(smooth_gate, preact)
     grad_preact = gate_back(grad_act.astype(f32))[0].astype(bf16)
     partial = contract_cols(grad_preact, upward_weight[0]).astype(bf16)
-    grad_normed = share_rows(partial, MP)
-    own = norm_added(upstream_part, mid_part, grad_normed)
+    own = share_rows(partial, MP).astype(bf16)
     wide0 = [contract_rows(normed_mid, grad_preact), contract_rows(upstream, activated)]
     sums0, sent0 = y_stage(wide0)
-    grad_mid = all_rows(after(own, *sent0), MP)
+    grad_normed = all_rows(after(own, rscale_mid, *sent0), MP).astype(f32)
+    grad_mid = (upstream.astype(f32) + norm_backward(scaled_mid, rscale_mid, grad_normed)).astype(bf16)
     grad_context = jnp.dot(grad_mid, output_weight[0], preferred_element_type=f32).astype(bf16)
     grad_qkv = attend_backward(probs, queries, key_rows, values, grad_context)
     late = [contract_rows(normed, grad_qkv), contract_rows(grad_mid, context)]

time: 324 us -> 312 us (0.963)
  other arithmetic: 23.6 us -> 17.4 us
  waiting for transfers between devices: 83.2 us -> 79.7 us
    all_to_all x2 -> x1, waiting for transfers between devices: 23.8 us -> 6.8 us  [step(): came = lax.all_to_all(sent, MP, 0, 0, tiled=True)]
    all_to_all x0 -> x1, waiting for transfers between devices: none -> 15.2 us  [step(): came = lax.all_to_all(after(sent, rscale_mid), MP, 0, 0, tiled=True)]
    all_to_all x2 -> x1, starting transfers between devices: 10.5 us -> 3.9 us  [step(): came = lax.all_to_all(sent, MP, 0, 0, tiled=True)]
    all_to_all x0 -> x1, starting transfers between devices: none -> 5.69 us  [step(): came = lax.all_to_all(after(sent, rscale_mid), MP, 0, 0, tiled=True)]
where the time goes in v6:
time: 312 us; the launch traced here: 310 us
  starting transfers between devices  97.3 us (31%)
  waiting for transfers between devices  79.7 us (26%)
  blocking collectives  77.7 us (25%)
  local copies, waits for them, and re-layouts  20.1 us (6%)
  other arithmetic  17.4 us (6%)
  matrix products  15.6 us (5%)
    all_to_all x2, blocking collectives, all_rows(): blocks = lax.all_to_all(copies, axis, 0, 0, tiled=True)  40.6 us
    all_to_all x2, blocking collectives, share_rows(): blocks = lax.all_to_all(blocks, axis, 0, 0, tiled=True)  37.1 us
    ppermute x3, starting transfers between devices, quad_stage(): lax.ppermute(pick(parts, here ^ k), axes, [(i, i ^ k) for i in range(4)])  30.3 us
    all_to_all x4, starting transfers between devices, share_rows(): blocks = lax.all_to_all(blocks, axis, 0, 0, tiled=True)  28.2 us
    all_to_all x3, waiting for transfers between devices, all_rows(): blocks = lax.all_to_all(copies, axis, 0, 0, tiled=True)  23.6 us
    all_to_all x4, waiting for transfers between devices, share_rows(): blocks = lax.all_to_all(blocks, axis, 0, 0, tiled=True)  18.2 us
    ppermute x12, waiting for transfers between devices, moved(): return lax.ppermute(x, axis, [(k, (k + step) % n) for k in range(n)])  15.8 us
    all_to_all x1, waiting for transfers between devices, step(): came = lax.all_to_all(after(sent, rscale_mid), MP, 0, 0, tiled=True)  15.2 us
  transfers between devices with their start and end apart: 24, of which 12 were waited for; matrix products, arithmetic and copies ran while one was open for 9% of the time, Pallas kernels for 0%

profile of v6, /device:TPU:1, one launch (start us, length us, event | category | flops | bytes accessed | tf_op | source)
XLA Modules:
  0.0 310.4 jit_solution(8485163615080279156)
XLA Ops:
  5.9 11.6 %all-to-all-start = ((bf16[16,16,1024]{2,1,0:T(8,128)(2,1)}), bf16[16,16,1024]{2,1,0:T(8,128)(2,1)S(1)}, u32[]{:S(2)}, u32[]{:S(2)}) async-start(bf16[16,16,1024]{2,1,0:T(8,128)(2,1)} %bitcast.3), calls=%async_computation | async-start | bytes 1048576 | tf_op jit(solution)/shard_map/all_to_all | solution.py:23
  17.5 14.8 %all-to-all-done = bf16[16,16,1024]{2,1,0:T(8,128)(2,1)S(1)} async-done(((bf16[16,16,1024]{2,1,0:T(8,128)(2,1)}), bf16[16,16,1024]{2,1,0:T(8,128)(2,1)S(1)}, u32[]{:S(2)}, u32[]{:S(2)}) %all-to-all-start) | async-done | bytes 524320 | tf_op jit(solution)/shard_map/all_to_all | solution.py:23
  32.5 22.6 %all_to_all.65 = bf16[16,16,1024]{2,1,0:T(8,128)(2,1)S(1)} all-to-all(bf16[16,16,1024]{2,1,0:T(8,128)(2,1)S(1)} %broadcast_in_dim.12), channel_id=1, replica_groups=mesh['z_lo'=2,'y'=4,'core'=2,'z_hi'=4,'x'=4] {'z_hi','x'}, dimensions={0} | all-to-all | bytes 1048576 | tf_op jit(solution)/shard_map/all_to_all | solution.py:30
  56.7 20.0 %all_to_all.66 = bf16[16,16,1024]{2,1,0:T(8,128)(2,1)S(1)} all-to-all(bf16[16,16,1024]{2,1,0:T(8,128)(2,1)S(1)} %bitcast.224), channel_id=1, replica_groups=mesh['z_lo'=2,'y'=4,'core'=2,'z_hi'=4,'x'=4] {'z_hi','x'}, dimensions={0} | all-to-all | bytes 1048576 | tf_op jit(solution)/shard_map/all_to_all | solution.py:23
  76.9 18.0 %all_to_all.67 = bf16[16,16,1024]{2,1,0:T(8,128)(2,1)S(1)} all-to-all(bf16[16,16,1024]{2,1,0:T(8,128)(2,1)S(1)} %broadcast_in_dim.13), channel_id=1, replica_groups=mesh['z_lo'=2,'y'=4,'core'=2,'z_hi'=4,'x'=4] {'z_hi','x'}, dimensions={0} | all-to-all | bytes 1048576 | tf_op jit(solution)/shard_map/all_to_all | solution.py:30
  97.1 17.0 %all_to_all.68 = bf16[16,16,1024]{2,1,0:T(8,128)(2,1)S(1)} all-to-all(bf16[16,16,1024]{2,1,0:T(8,128)(2,1)S(1)} %bitcast.221), channel_id=1, replica_groups=mesh['z_lo'=2,'y'=4,'core'=2,'z_hi'=4,'x'=4] {'z_hi','x'}, dimensions={0} | all-to-all | bytes 1048576 | tf_op jit(solution)/shard_map/all_to_all | solution.py:23
  115.1 4.4 %all-to-all-start.5 = ((bf16[16,16,1024]{2,1,0:T(8,128)(2,1)}), bf16[16,16,1024]{2,1,0:T(8,128)(2,1)S(1)}, u32[]{:S(2)}, u32[]{:S(2)}) async-start(bf16[16,16,1024]{2,1,0:T(8,128)(2,1)} %broadcast_in_dim.14), calls=%async_computation.5 | async-start | bytes 1048576 | tf_op jit(solution)/shard_map/all_to_all | solution.py:30
  119.5 11.3 %all-to-all-done.5 = bf16[16,16,1024]{2,1,0:T(8,128)(2,1)S(1)} async-done(((bf16[16,16,1024]{2,1,0:T(8,128)(2,1)}), bf16[16,16,1024]{2,1,0:T(8,128)(2,1)S(1)}, u32[]{:S(2)}, u32[]{:S(2)}) %all-to-all-start.5) | async-done | bytes 524320 | tf_op jit(solution)/shard_map/all_to_all | solution.py:30
  133.8 3.7 %all-to-all-start.6 = ((bf16[16,16,1024]{2,1,0:T(8,128)(2,1)}), bf16[16,16,1024]{2,1,0:T(8,128)(2,1)S(1)}, u32[]{:S(2)}, u32[]{:S(2)}) async-start(bf16[16,16,1024]{2,1,0:T(8,128)(2,1)} %bitcast.15), calls=%async_computation.6 | async-start | bytes 1048576 | tf_op jit(solution)/shard_map/all_to_all | solution.py:23
  144.0 3.2 %collective-permute-done = bf16[256,256]{1,0:T(8,128)(2,1)S(1)} collective-permute-done((bf16[256,256]{1,0:T(8,128)(2,1)}, bf16[256,256]{1,0:T(8,128)(2,1)S(1)}, u32[]{:S(2)}, u32[]{:S(2)}) %collective-permute-start) | collective-permute-done | bytes 131104 | tf_op jit(solution)/shard_map/ppermute | solution.py:40
  147.2 2.7 collective-permute-done.1
  152.0 5.7 %all-to-all-start.7 = ((bf16[16,16,1280]{2,1,0:T(8,128)(2,1)}), bf16[16,16,1280]{2,1,0:T(8,128)(2,1)S(1)}, u32[]{:S(2)}, u32[]{:S(2)}) async-start(bf16[16,16,1280]{2,1,0:T(8,128)(2,1)} %pad_maximum_fusion.2), calls=%async_computation.7 | async-start | bytes 1310720 | tf_op jit(solution)/shard_map/all_to_all | solution.py:165
  158.8 15.2 %all-to-all-done.7 = bf16[16,16,1280]{2,1,0:T(8,128)(2,1)S(1)} async-done(((bf16[16,16,1280]{2,1,0:T(8,128)(2,1)}), bf16[16,16,1280]{2,1,0:T(8,128)(2,1)S(1)}, u32[]{:S(2)}, u32[]{:S(2)}) %all-to-all-start.7) | async-done | bytes 655392 | tf_op jit(solution)/shard_map/all_to_all | solution.py:165
  180.0 3.9 %all-to-all-start.8 = ((bf16[16,16,1280]{2,1,0:T(8,128)(2,1)}), bf16[16,16,1280]{2,1,0:T(8,128)(2,1)S(1)}, u32[]{:S(2)}, u32[]{:S(2)}) async-start(bf16[16,16,1280]{2,1,0:T(8,128)(2,1)} %pad_maximum_fusion.3), calls=%async_computation.8 | async-start | bytes 1310720 | tf_op jit(solution)/shard_map/all_to_all | solution.py:176
  193.1 6.8 %all-to-all-done.8 = bf16[16,16,1280]{2,1,0:T(8,128)(2,1)S(1)} async-done(((bf16[16,16,1280]{2,1,0:T(8,128)(2,1)}), bf16[16,16,1280]{2,1,0:T(8,128)(2,1)S(1)}, u32[]{:S(2)}, u32[]{:S(2)}) %all-to-all-start.8) | async-done | bytes 655392 | tf_op jit(solution)/shard_map/all_to_all | solution.py:176
  200.9 4.3 %all-to-all-start.9 = ((bf16[16,16,1024]{2,1,0:T(8,128)(2,1)}), bf16[16,16,1024]{2,1,0:T(8,128)(2,1)S(1)}, u32[]{:S(2)}, u32[]{:S(2)}) async-start(bf16[16,16,1024]{2,1,0:T(8,128)(2,1)} %broadcast_in_dim.16), calls=%async_computation.9 | async-start | bytes 1048576 | tf_op jit(solution)/shard_map/all_to_all | solution.py:30
  205.4 12.3 %all-to-all-done.9 = bf16[16,16,1024]{2,1,0:T(8,128)(2,1)S(1)} async-done(((bf16[16,16,1024]{2,1,0:T(8,128)(2,1)}), bf16[16,16,1024]{2,1,0:T(8,128)(2,1)S(1)}, u32[]{:S(2)}, u32[]{:S(2)}) %all-to-all-start.9) | async-done | bytes 524320 | tf_op jit(solution)/shard_map/all_to_all | solution.py:30
  221.9 5.7 %all-to-all-start.10 = ((bf16[16,16,1024]{2,1,0:T(8,128)(2,1)}), bf16[16,16,1024]{2,1,0:T(8,128)(2,1)S(1)}, u32[]{:S(2)}, u32[]{:S(2)}) async-start(bf16[16,16,1024]{2,1,0:T(8,128)(2,1)} %bitcast.46), calls=%async_computation.10 | async-start | bytes 1048576 | tf_op jit(solution)/shard_map/all_to_all | solution.py:23
  233.2 2.7 collective-permute-start.11
  235.9 3.4 %all-to-all-done.10 = bf16[16,16,1024]{2,1,0:T(8,128)(2,1)S(1)} async-done(((bf16[16,16,1024]{2,1,0:T(8,128)(2,1)}), bf16[16,16,1024]{2,1,0:T(8,128)(2,1)S(1)}, u32[]{:S(2)}, u32[]{:S(2)}) %all-to-all-start.10) | async-done | bytes 524320 | tf_op jit(solution)/shard_map/all_to_all | solution.py:23
  240.2 6.3 %all-to-all-start.11 = ((bf16[16,16,1024]{2,1,0:T(8,128)(2,1)}), bf16[16,16,1024]{2,1,0:T(8,128)(2,1)S(1)}, u32[]{:S(2)}, u32[]{:S(2)}) async-start(bf16[16,16,1024]{2,1,0:T(8,128)(2,1)} %broadcast_in_dim.17), calls=%async_computation.11 | async-start | bytes 1048576 | tf_op jit(solution)/shard_map/all_to_all | solution.py:30
  255.0 29.0 %collective-permute-start.12 = (bf16[64,1280]{1,0:T(8,128)(2,1)}, bf16[64,1280]{1,0:T(8,128)(2,1)S(1)}, u32[]{:S(2)}, u32[]{:S(2)}) collective-permute-start(bf16[64,1280]{1,0:T(8,128)(2,1)} %get-tuple-element.29), channel_id=1, source_target_pairs={{0,16},{16,0},{128,144},{144,128},{1,17},{17,1},{129,145},{145,129... | collective-permute-start | bytes 491528 | tf_op jit(solution)/shard_map/ppermute | solution.py:64
  289.8 7.2 %all-to-all-start.12 = ((bf16[16,64,256]{2,1,0:T(8,128)(2,1)}), bf16[16,64,256]{2,1,0:T(8,128)(2,1)S(1)}, u32[]{:S(2)}, u32[]{:S(2)}) async-start(bf16[16,64,256]{2,1,0:T(8,128)(2,1)} %bitcast.53), calls=%async_computation.12 | async-start | bytes 1048576 | tf_op jit(solution)/shard_map/all_to_all | solution.py:23
  304.2 3.6 %collective-permute-done.3 = bf16[256,256]{1,0:T(8,128)(2,1)S(1)} collective-permute-done((bf16[256,256]{1,0:T(8,128)(2,1)S(1)}, bf16[256,256]{1,0:T(8,128)(2,1)S(1)}, u32[]{:S(2)}, u32[]{:S(2)}) %collective-permute-start.3) | collective-permute-done | bytes 131104 | tf_op jit(solution)/shard_map/ppermute | solution.py:40
  (259 shorter events, 72.3 us)
Async XLA Ops:
  5.9 26.4 %all-to-all-start = ((bf16[16,16,1024]{2,1,0:T(8,128)(2,1)}), bf16[16,16,1024]{2,1,0:T(8,128)(2,1)S(1)}, u32[]{:S(2)}, u32[]{:S(2)}) async-start(bf16[16,16,1024]{2,1,0:T(8,128)(2,1)} %bitcast.3), calls=%async_computation | async-start | bytes 1048576 | tf_op jit(solution)/shard_map/all_to_all | solution.py:23
  115.1 15.8 %all-to-all-start.5 = ((bf16[16,16,1024]{2,1,0:T(8,128)(2,1)}), bf16[16,16,1024]{2,1,0:T(8,128)(2,1)S(1)}, u32[]{:S(2)}, u32[]{:S(2)}) async-start(bf16[16,16,1024]{2,1,0:T(8,128)(2,1)} %broadcast_in_dim.14), calls=%async_computation.5 | async-start | bytes 1048576 | tf_op jit(solution)/shard_map/all_to_all | solution.py:30
  133.8 17.2 %all-to-all-start.6 = ((bf16[16,16,1024]{2,1,0:T(8,128)(2,1)}), bf16[16,16,1024]{2,1,0:T(8,128)(2,1)S(1)}, u32[]{:S(2)}, u32[]{:S(2)}) async-start(bf16[16,16,1024]{2,1,0:T(8,128)(2,1)} %bitcast.15), calls=%async_computation.6 | async-start | bytes 1048576 | tf_op jit(solution)/shard_map/all_to_all | solution.py:23
  139.7 7.5 %collective-permute-start = (bf16[256,256]{1,0:T(8,128)(2,1)}, bf16[256,256]{1,0:T(8,128)(2,1)S(1)}, u32[]{:S(2)}, u32[]{:S(2)}) collective-permute-start(bf16[256,256]{1,0:T(8,128)(2,1)} %get-tuple-element.38), channel_id=1, source_target_pairs={{0,1},{1,2},{2,3},{3,0},{4,5},{5,6},{6,7},{7,4},{8,9},{9,10},{10,1... | collective-permute-start | bytes 393224 | tf_op jit(solution)/shard_map/ppermute | solution.py:40
  141.1 6.2 %collective-permute-start.2 = (bf16[256,256]{1,0:T(8,128)(2,1)S(1)}, bf16[256,256]{1,0:T(8,128)(2,1)S(1)}, u32[]{:S(2)}, u32[]{:S(2)}) collective-permute-start(bf16[256,256]{1,0:T(8,128)(2,1)S(1)} %get-tuple-element.39), channel_id=1, source_target_pairs={{0,3},{1,0},{2,1},{3,2},{4,7},{5,4},{6,5},{7,6},{8,11},{9,8},{10,9... | collective-permute-start | bytes 393224 | tf_op jit(solution)/shard_map/ppermute | solution.py:40
  142.4 7.6 %collective-permute-start.1 = (bf16[256,256]{1,0:T(8,128)(2,1)S(1)}, bf16[256,256]{1,0:T(8,128)(2,1)}, u32[]{:S(2)}, u32[]{:S(2)}) collective-permute-start(bf16[256,256]{1,0:T(8,128)(2,1)S(1)} %get-tuple-element.40), channel_id=1, source_target_pairs={{0,2},{1,3},{2,0},{3,1},{4,6},{5,7},{6,4},{7,5},{8,10},{9,11},{10,... | collective-permute-start | bytes 393224 | tf_op jit(solution)/shard_map/ppermute | solution.py:40
  152.0 22.0 %all-to-all-start.7 = ((bf16[16,16,1280]{2,1,0:T(8,128)(2,1)}), bf16[16,16,1280]{2,1,0:T(8,128)(2,1)S(1)}, u32[]{:S(2)}, u32[]{:S(2)}) async-start(bf16[16,16,1280]{2,1,0:T(8,128)(2,1)} %pad_maximum_fusion.2), calls=%async_computation.7 | async-start | bytes 1310720 | tf_op jit(solution)/shard_map/all_to_all | solution.py:165
  180.0 19.9 %all-to-all-start.8 = ((bf16[16,16,1280]{2,1,0:T(8,128)(2,1)}), bf16[16,16,1280]{2,1,0:T(8,128)(2,1)S(1)}, u32[]{:S(2)}, u32[]{:S(2)}) async-start(bf16[16,16,1280]{2,1,0:T(8,128)(2,1)} %pad_maximum_fusion.3), calls=%async_computation.8 | async-start | bytes 1310720 | tf_op jit(solution)/shard_map/all_to_all | solution.py:176
  200.9 16.9 %all-to-all-start.9 = ((bf16[16,16,1024]{2,1,0:T(8,128)(2,1)}), bf16[16,16,1024]{2,1,0:T(8,128)(2,1)S(1)}, u32[]{:S(2)}, u32[]{:S(2)}) async-start(bf16[16,16,1024]{2,1,0:T(8,128)(2,1)} %broadcast_in_dim.16), calls=%async_computation.9 | async-start | bytes 1048576 | tf_op jit(solution)/shard_map/all_to_all | solution.py:30
  221.9 17.4 %all-to-all-start.10 = ((bf16[16,16,1024]{2,1,0:T(8,128)(2,1)}), bf16[16,16,1024]{2,1,0:T(8,128)(2,1)S(1)}, u32[]{:S(2)}, u32[]{:S(2)}) async-start(bf16[16,16,1024]{2,1,0:T(8,128)(2,1)} %bitcast.46), calls=%async_computation.10 | async-start | bytes 1048576 | tf_op jit(solution)/shard_map/all_to_all | solution.py:23
  227.8 18.7 %collective-permute-start.8 = (bf16[2,2,64,768]{3,2,1,0:T(8,128)(2,1)}, bf16[2,2,64,768]{3,2,1,0:T(8,128)(2,1)}, u32[]{:S(2)}, u32[]{:S(2)}) collective-permute-start(bf16[2,2,64,768]{3,2,1,0:T(8,128)(2,1)} %get-tuple-element.21), channel_id=1, source_target_pairs={{0,96},{32,0},{64,32},{96,64},{1,97},{33,1},{65,33},{97,65},{2,98}... | collective-permute-start | bytes 1179656 | tf_op jit(solution)/shard_map/ppermute | solution.py:40
  229.0 19.1 %collective-permute-start.7 = (bf16[2,2,64,768]{3,2,1,0:T(8,128)(2,1)}, bf16[2,2,64,768]{3,2,1,0:T(8,128)(2,1)}, u32[]{:S(2)}, u32[]{:S(2)}) collective-permute-start(bf16[2,2,64,768]{3,2,1,0:T(8,128)(2,1)} %get-tuple-element.22), channel_id=1, source_target_pairs={{0,64},{32,96},{64,0},{96,32},{1,65},{33,97},{65,1},{97,33},{2,66}... | collective-permute-start | bytes 1179656 | tf_op jit(solution)/shard_map/ppermute | solution.py:40
  231.1 17.0 %collective-permute-start.6 = (bf16[2,2,64,768]{3,2,1,0:T(8,128)(2,1)S(1)}, bf16[2,2,64,768]{3,2,1,0:T(8,128)(2,1)}, u32[]{:S(2)}, u32[]{:S(2)}) collective-permute-start(bf16[2,2,64,768]{3,2,1,0:T(8,128)(2,1)S(1)} %get-tuple-element.23), channel_id=1, source_target_pairs={{0,32},{32,64},{64,96},{96,0},{1,33},{33,65},{65,97},{97,1},{2,34}... | collective-permute-start | bytes 1179656 | tf_op jit(solution)/shard_map/ppermute | solution.py:40
  233.2 17.3 %collective-permute-start.11 = (bf16[2,2,64,512]{3,2,1,0:T(8,128)(2,1)}, bf16[2,2,64,512]{3,2,1,0:T(8,128)(2,1)S(1)}, u32[]{:S(2)}, u32[]{:S(2)}) collective-permute-start(bf16[2,2,64,512]{3,2,1,0:T(8,128)(2,1)} %get-tuple-element.24), channel_id=1, source_target_pairs={{0,96},{32,0},{64,32},{96,64},{1,97},{33,1},{65,33},{97,65},{2,98}... | collective-permute-start | bytes 786440 | tf_op jit(solution)/shard_map/ppermute | solution.py:40
  235.9 14.7 %collective-permute-start.10 = (bf16[2,2,64,512]{3,2,1,0:T(8,128)(2,1)S(1)}, bf16[2,2,64,512]{3,2,1,0:T(8,128)(2,1)}, u32[]{:S(2)}, u32[]{:S(2)}) collective-permute-start(bf16[2,2,64,512]{3,2,1,0:T(8,128)(2,1)S(1)} %get-tuple-element.25), channel_id=1, source_target_pairs={{0,64},{32,96},{64,0},{96,32},{1,65},{33,97},{65,1},{97,33},{2,66}... | collective-permute-start | bytes 786440 | tf_op jit(solution)/shard_map/ppermute | solution.py:40
  240.2 45.1 %all-to-all-start.11 = ((bf16[16,16,1024]{2,1,0:T(8,128)(2,1)}), bf16[16,16,1024]{2,1,0:T(8,128)(2,1)S(1)}, u32[]{:S(2)}, u32[]{:S(2)}) async-start(bf16[16,16,1024]{2,1,0:T(8,128)(2,1)} %broadcast_in_dim.17), calls=%async_computation.11 | async-start | bytes 1048576 | tf_op jit(solution)/shard_map/all_to_all | solution.py:30
  246.6 6.5 %collective-permute-start.9 = (bf16[2,2,64,512]{3,2,1,0:T(8,128)(2,1)S(1)}, bf16[2,2,64,512]{3,2,1,0:T(8,128)(2,1)S(1)}, u32[]{:S(2)}, u32[]{:S(2)}) collective-permute-start(bf16[2,2,64,512]{3,2,1,0:T(8,128)(2,1)S(1)} %get-tuple-element.26), channel_id=1, source_target_pairs={{0,32},{32,64},{64,96},{96,0},{1,33},{33,65},{65,97},{97,1},{2,34}... | collective-permute-start | bytes 786440 | tf_op jit(solution)/shard_map/ppermute | solution.py:40
  255.0 42.0 %collective-permute-start.12 = (bf16[64,1280]{1,0:T(8,128)(2,1)}, bf16[64,1280]{1,0:T(8,128)(2,1)S(1)}, u32[]{:S(2)}, u32[]{:S(2)}) collective-permute-start(bf16[64,1280]{1,0:T(8,128)(2,1)} %get-tuple-element.29), channel_id=1, source_target_pairs={{0,16},{16,0},{128,144},{144,128},{1,17},{17,1},{129,145},{145,129... | collective-permute-start | bytes 491528 | tf_op jit(solution)/shard_map/ppermute | solution.py:64
  284.0 13.0 %collective-permute-start.14 = (bf16[64,1280]{1,0:T(8,128)(2,1)}, bf16[64,1280]{1,0:T(8,128)(2,1)S(1)}, u32[]{:S(2)}, u32[]{:S(2)}) collective-permute-start(bf16[64,1280]{1,0:T(8,128)(2,1)} %get-tuple-element.30), channel_id=1, source_target_pairs={{0,144},{16,128},{128,16},{144,0},{1,145},{17,129},{129,17},{145,1... | collective-permute-start | bytes 491528 | tf_op jit(solution)/shard_map/ppermute | solution.py:64
  284.0 13.1 %collective-permute-start.13 = (bf16[64,1280]{1,0:T(8,128)(2,1)S(1)}, bf16[64,1280]{1,0:T(8,128)(2,1)S(1)}, u32[]{:S(2)}, u32[]{:S(2)}) collective-permute-start(bf16[64,1280]{1,0:T(8,128)(2,1)S(1)} %get-tuple-element.31), channel_id=1, source_target_pairs={{0,128},{16,144},{128,0},{144,16},{1,129},{17,145},{129,1},{145,17... | collective-permute-start | bytes 491528 | tf_op jit(solution)/shard_map/ppermute | solution.py:64
  289.8 18.9 %all-to-all-start.12 = ((bf16[16,64,256]{2,1,0:T(8,128)(2,1)}), bf16[16,64,256]{2,1,0:T(8,128)(2,1)S(1)}, u32[]{:S(2)}, u32[]{:S(2)}) async-start(bf16[16,64,256]{2,1,0:T(8,128)(2,1)} %bitcast.53), calls=%async_computation.12 | async-start | bytes 1048576 | tf_op jit(solution)/shard_map/all_to_all | solution.py:23
  297.2 5.0 %collective-permute-start.5 = (bf16[256,256]{1,0:T(8,128)(2,1)S(1)}, bf16[256,256]{1,0:T(8,128)(2,1)S(1)}, u32[]{:S(2)}, u32[]{:S(2)}) collective-permute-start(bf16[256,256]{1,0:T(8,128)(2,1)S(1)} %bitcast.227), channel_id=1, source_target_pairs={{0,3},{1,0},{2,1},{3,2},{4,7},{5,4},{6,5},{7,6},{8,11},{9,8},{10,9... | collective-permute-start | bytes 393224 | tf_op jit(solution)/shard_map/ppermute | solution.py:40
  298.1 6.2 %collective-permute-start.4 = (bf16[256,256]{1,0:T(8,128)(2,1)S(1)}, bf16[256,256]{1,0:T(8,128)(2,1)S(1)}, u32[]{:S(2)}, u32[]{:S(2)}) collective-permute-start(bf16[256,256]{1,0:T(8,128)(2,1)S(1)} %bitcast.228), channel_id=1, source_target_pairs={{0,2},{1,3},{2,0},{3,1},{4,6},{5,7},{6,4},{7,5},{8,10},{9,11},{10,... | collective-permute-start | bytes 393224 | tf_op jit(solution)/shard_map/ppermute | solution.py:40
  299.3 8.4 %collective-permute-start.3 = (bf16[256,256]{1,0:T(8,128)(2,1)S(1)}, bf16[256,256]{1,0:T(8,128)(2,1)S(1)}, u32[]{:S(2)}, u32[]{:S(2)}) collective-permute-start(bf16[256,256]{1,0:T(8,128)(2,1)S(1)} %bitcast.229), channel_id=1, source_target_pairs={{0,1},{1,2},{2,3},{3,0},{4,5},{5,6},{6,7},{7,4},{8,9},{9,10},{10,1... | collective-permute-start | bytes 393224 | tf_op jit(solution)/shard_map/ppermute | solution.py:40
  (54 other events, 320.8 us)

commit v7 on v6

--- a/solution.py
+++ b/solution.py
@@ -11,6 +11,8 @@
 DP = ("z_lo", "y", "core")
 MP = ("z_hi", "x")
 
+
+STAGGER = 416
 
 epsilon = 1e-06
 bf16 = jnp.bfloat16
@@ -63,6 +65,11 @@
     return [pick(parts, here)] + [
         lax.ppermute(pick(parts, here ^ k), axes, [(i, i ^ k) for i in range(4)]) for k in range(1, 4)
     ]
+
+
+def later_start(tokens):
+    steps = lax.axis_index("core") * STAGGER
+    return lax.fori_loop(0, steps, lambda _, v: jnp.tanh(v) * 1.5, tokens[:8, :128].astype(f32))
 
 
 def normalize(stream):
@@ -131,6 +138,8 @@
         queries, key_rows, values = (qkv[:, k * HD : (k + 1) * HD] for k in range(3))
         probs, context = attend(queries, key_rows, values, live)
         partial_att = contract_cols(context, output_weight[l]).astype(bf16)
+        if l == 0:
+            partial_att = after(partial_att, later_start(tokens))
         mid_part = (stream_part.astype(f32) + share_rows(partial_att, MP)).astype(bf16)
         mid_stream = all_rows(mid_part, MP)
         normed_mid, scaled_mid, rscale_mid = normalize(mid_stream)

time: 312 us -> 312 us (level)
  no operation moved by 1% of the time
where the time goes in v7:
time: 312 us; the launch traced here: 310 us
  starting transfers between devices  97.3 us (31%)
  waiting for transfers between devices  79.7 us (26%)
  blocking collectives  77.7 us (25%)
  local copies, waits for them, and re-layouts  20.1 us (6%)
  other arithmetic  17.4 us (6%)
  matrix products  15.6 us (5%)
    all_to_all x2, blocking collectives, all_rows(): blocks = lax.all_to_all(copies, axis, 0, 0, tiled=True)  40.6 us
    all_to_all x2, blocking collectives, share_rows(): blocks = lax.all_to_all(blocks, axis, 0, 0, tiled=True)  37.1 us
    ppermute x3, starting transfers between devices, quad_stage(): lax.ppermute(pick(parts, here ^ k), axes, [(i, i ^ k) for i in range(4)])  30.3 us
    all_to_all x4, starting transfers between devices, share_rows(): blocks = lax.all_to_all(blocks, axis, 0, 0, tiled=True)  28.2 us
    all_to_all x3, waiting for transfers between devices, all_rows(): blocks = lax.all_to_all(copies, axis, 0, 0, tiled=True)  23.6 us
    all_to_all x4, waiting for transfers between devices, share_rows(): blocks = lax.all_to_all(blocks, axis, 0, 0, tiled=True)  18.2 us
    ppermute x12, waiting for transfers between devices, moved(): return lax.ppermute(x, axis, [(k, (k + step) % n) for k in range(n)])  15.8 us
    all_to_all x1, waiting for transfers between devices, step(): came = lax.all_to_all(after(sent, rscale_mid), MP, 0, 0, tiled=True)  15.2 us
  transfers between devices with their start and end apart: 24, of which 12 were waited for; matrix products, arithmetic and copies ran while one was open for 9% of the time, Pallas kernels for 0%

profile of v7, /device:TPU:1, one launch (start us, length us, event | category | flops | bytes accessed | tf_op | source)
XLA Modules:
  0.0 310.4 jit_solution(8485163615080279156)
XLA Ops:
  5.9 11.6 %all-to-all-start = ((bf16[16,16,1024]{2,1,0:T(8,128)(2,1)}), bf16[16,16,1024]{2,1,0:T(8,128)(2,1)S(1)}, u32[]{:S(2)}, u32[]{:S(2)}) async-start(bf16[16,16,1024]{2,1,0:T(8,128)(2,1)} %bitcast.3), calls=%async_computation | async-start | bytes 1048576 | tf_op jit(solution)/shard_map/all_to_all | solution.py:25
  17.5 14.8 %all-to-all-done = bf16[16,16,1024]{2,1,0:T(8,128)(2,1)S(1)} async-done(((bf16[16,16,1024]{2,1,0:T(8,128)(2,1)}), bf16[16,16,1024]{2,1,0:T(8,128)(2,1)S(1)}, u32[]{:S(2)}, u32[]{:S(2)}) %all-to-all-start) | async-done | bytes 524320 | tf_op jit(solution)/shard_map/all_to_all | solution.py:25
  32.5 22.6 %all_to_all.65 = bf16[16,16,1024]{2,1,0:T(8,128)(2,1)S(1)} all-to-all(bf16[16,16,1024]{2,1,0:T(8,128)(2,1)S(1)} %broadcast_in_dim.12), channel_id=1, replica_groups=mesh['z_lo'=2,'y'=4,'core'=2,'z_hi'=4,'x'=4] {'z_hi','x'}, dimensions={0} | all-to-all | bytes 1048576 | tf_op jit(solution)/shard_map/all_to_all | solution.py:32
  56.7 20.0 %all_to_all.66 = bf16[16,16,1024]{2,1,0:T(8,128)(2,1)S(1)} all-to-all(bf16[16,16,1024]{2,1,0:T(8,128)(2,1)S(1)} %bitcast.224), channel_id=1, replica_groups=mesh['z_lo'=2,'y'=4,'core'=2,'z_hi'=4,'x'=4] {'z_hi','x'}, dimensions={0} | all-to-all | bytes 1048576 | tf_op jit(solution)/shard_map/all_to_all | solution.py:25
  76.9 18.0 %all_to_all.67 = bf16[16,16,1024]{2,1,0:T(8,128)(2,1)S(1)} all-to-all(bf16[16,16,1024]{2,1,0:T(8,128)(2,1)S(1)} %broadcast_in_dim.13), channel_id=1, replica_groups=mesh['z_lo'=2,'y'=4,'core'=2,'z_hi'=4,'x'=4] {'z_hi','x'}, dimensions={0} | all-to-all | bytes 1048576 | tf_op jit(solution)/shard_map/all_to_all | solution.py:32
  97.1 17.0 %all_to_all.68 = bf16[16,16,1024]{2,1,0:T(8,128)(2,1)S(1)} all-to-all(bf16[16,16,1024]{2,1,0:T(8,128)(2,1)S(1)} %bitcast.221), channel_id=1, replica_groups=mesh['z_lo'=2,'y'=4,'core'=2,'z_hi'=4,'x'=4] {'z_hi','x'}, dimensions={0} | all-to-all | bytes 1048576 | tf_op jit(solution)/shard_map/all_to_all | solution.py:25
  115.1 4.4 %all-to-all-start.5 = ((bf16[16,16,1024]{2,1,0:T(8,128)(2,1)}), bf16[16,16,1024]{2,1,0:T(8,128)(2,1)S(1)}, u32[]{:S(2)}, u32[]{:S(2)}) async-start(bf16[16,16,1024]{2,1,0:T(8,128)(2,1)} %broadcast_in_dim.14), calls=%async_computation.5 | async-start | bytes 1048576 | tf_op jit(solution)/shard_map/all_to_all | solution.py:32
  119.5 11.3 %all-to-all-done.5 = bf16[16,16,1024]{2,1,0:T(8,128)(2,1)S(1)} async-done(((bf16[16,16,1024]{2,1,0:T(8,128)(2,1)}), bf16[16,16,1024]{2,1,0:T(8,128)(2,1)S(1)}, u32[]{:S(2)}, u32[]{:S(2)}) %all-to-all-start.5) | async-done | bytes 524320 | tf_op jit(solution)/shard_map/all_to_all | solution.py:32
  133.8 3.7 %all-to-all-start.6 = ((bf16[16,16,1024]{2,1,0:T(8,128)(2,1)}), bf16[16,16,1024]{2,1,0:T(8,128)(2,1)S(1)}, u32[]{:S(2)}, u32[]{:S(2)}) async-start(bf16[16,16,1024]{2,1,0:T(8,128)(2,1)} %bitcast.15), calls=%async_computation.6 | async-start | bytes 1048576 | tf_op jit(solution)/shard_map/all_to_all | solution.py:25
  144.0 3.2 %collective-permute-done = bf16[256,256]{1,0:T(8,128)(2,1)S(1)} collective-permute-done((bf16[256,256]{1,0:T(8,128)(2,1)}, bf16[256,256]{1,0:T(8,128)(2,1)S(1)}, u32[]{:S(2)}, u32[]{:S(2)}) %collective-permute-start) | collective-permute-done | bytes 131104 | tf_op jit(solution)/shard_map/ppermute | solution.py:42
  147.2 2.7 collective-permute-done.1
  152.0 5.7 %all-to-all-start.7 = ((bf16[16,16,1280]{2,1,0:T(8,128)(2,1)}), bf16[16,16,1280]{2,1,0:T(8,128)(2,1)S(1)}, u32[]{:S(2)}, u32[]{:S(2)}) async-start(bf16[16,16,1280]{2,1,0:T(8,128)(2,1)} %pad_maximum_fusion.2), calls=%async_computation.7 | async-start | bytes 1310720 | tf_op jit(solution)/shard_map/all_to_all | solution.py:174
  158.8 15.2 %all-to-all-done.7 = bf16[16,16,1280]{2,1,0:T(8,128)(2,1)S(1)} async-done(((bf16[16,16,1280]{2,1,0:T(8,128)(2,1)}), bf16[16,16,1280]{2,1,0:T(8,128)(2,1)S(1)}, u32[]{:S(2)}, u32[]{:S(2)}) %all-to-all-start.7) | async-done | bytes 655392 | tf_op jit(solution)/shard_map/all_to_all | solution.py:174
  180.0 3.9 %all-to-all-start.8 = ((bf16[16,16,1280]{2,1,0:T(8,128)(2,1)}), bf16[16,16,1280]{2,1,0:T(8,128)(2,1)S(1)}, u32[]{:S(2)}, u32[]{:S(2)}) async-start(bf16[16,16,1280]{2,1,0:T(8,128)(2,1)} %pad_maximum_fusion.3), calls=%async_computation.8 | async-start | bytes 1310720 | tf_op jit(solution)/shard_map/all_to_all | solution.py:185
  193.1 6.8 %all-to-all-done.8 = bf16[16,16,1280]{2,1,0:T(8,128)(2,1)S(1)} async-done(((bf16[16,16,1280]{2,1,0:T(8,128)(2,1)}), bf16[16,16,1280]{2,1,0:T(8,128)(2,1)S(1)}, u32[]{:S(2)}, u32[]{:S(2)}) %all-to-all-start.8) | async-done | bytes 655392 | tf_op jit(solution)/shard_map/all_to_all | solution.py:185
  200.9 4.3 %all-to-all-start.9 = ((bf16[16,16,1024]{2,1,0:T(8,128)(2,1)}), bf16[16,16,1024]{2,1,0:T(8,128)(2,1)S(1)}, u32[]{:S(2)}, u32[]{:S(2)}) async-start(bf16[16,16,1024]{2,1,0:T(8,128)(2,1)} %broadcast_in_dim.16), calls=%async_computation.9 | async-start | bytes 1048576 | tf_op jit(solution)/shard_map/all_to_all | solution.py:32
  205.4 12.3 %all-to-all-done.9 = bf16[16,16,1024]{2,1,0:T(8,128)(2,1)S(1)} async-done(((bf16[16,16,1024]{2,1,0:T(8,128)(2,1)}), bf16[16,16,1024]{2,1,0:T(8,128)(2,1)S(1)}, u32[]{:S(2)}, u32[]{:S(2)}) %all-to-all-start.9) | async-done | bytes 524320 | tf_op jit(solution)/shard_map/all_to_all | solution.py:32
  221.9 5.7 %all-to-all-start.10 = ((bf16[16,16,1024]{2,1,0:T(8,128)(2,1)}), bf16[16,16,1024]{2,1,0:T(8,128)(2,1)S(1)}, u32[]{:S(2)}, u32[]{:S(2)}) async-start(bf16[16,16,1024]{2,1,0:T(8,128)(2,1)} %bitcast.46), calls=%async_computation.10 | async-start | bytes 1048576 | tf_op jit(solution)/shard_map/all_to_all | solution.py:25
  233.2 2.7 collective-permute-start.11
  235.9 3.4 %all-to-all-done.10 = bf16[16,16,1024]{2,1,0:T(8,128)(2,1)S(1)} async-done(((bf16[16,16,1024]{2,1,0:T(8,128)(2,1)}), bf16[16,16,1024]{2,1,0:T(8,128)(2,1)S(1)}, u32[]{:S(2)}, u32[]{:S(2)}) %all-to-all-start.10) | async-done | bytes 524320 | tf_op jit(solution)/shard_map/all_to_all | solution.py:25
  240.2 6.3 %all-to-all-start.11 = ((bf16[16,16,1024]{2,1,0:T(8,128)(2,1)}), bf16[16,16,1024]{2,1,0:T(8,128)(2,1)S(1)}, u32[]{:S(2)}, u32[]{:S(2)}) async-start(bf16[16,16,1024]{2,1,0:T(8,128)(2,1)} %broadcast_in_dim.17), calls=%async_computation.11 | async-start | bytes 1048576 | tf_op jit(solution)/shard_map/all_to_all | solution.py:32
  255.0 29.0 %collective-permute-start.12 = (bf16[64,1280]{1,0:T(8,128)(2,1)}, bf16[64,1280]{1,0:T(8,128)(2,1)S(1)}, u32[]{:S(2)}, u32[]{:S(2)}) collective-permute-start(bf16[64,1280]{1,0:T(8,128)(2,1)} %get-tuple-element.35), channel_id=1, source_target_pairs={{0,16},{16,0},{128,144},{144,128},{1,17},{17,1},{129,145},{145,129... | collective-permute-start | bytes 491528 | tf_op jit(solution)/shard_map/ppermute | solution.py:66
  289.8 7.2 %all-to-all-start.12 = ((bf16[16,64,256]{2,1,0:T(8,128)(2,1)}), bf16[16,64,256]{2,1,0:T(8,128)(2,1)S(1)}, u32[]{:S(2)}, u32[]{:S(2)}) async-start(bf16[16,64,256]{2,1,0:T(8,128)(2,1)} %bitcast.53), calls=%async_computation.12 | async-start | bytes 1048576 | tf_op jit(solution)/shard_map/all_to_all | solution.py:25
  304.2 3.6 %collective-permute-done.3 = bf16[256,256]{1,0:T(8,128)(2,1)S(1)} collective-permute-done((bf16[256,256]{1,0:T(8,128)(2,1)S(1)}, bf16[256,256]{1,0:T(8,128)(2,1)S(1)}, u32[]{:S(2)}, u32[]{:S(2)}) %collective-permute-start.3) | collective-permute-done | bytes 131104 | tf_op jit(solution)/shard_map/ppermute | solution.py:42
  (259 shorter events, 72.3 us)
Async XLA Ops:
  5.9 26.4 %all-to-all-start = ((bf16[16,16,1024]{2,1,0:T(8,128)(2,1)}), bf16[16,16,1024]{2,1,0:T(8,128)(2,1)S(1)}, u32[]{:S(2)}, u32[]{:S(2)}) async-start(bf16[16,16,1024]{2,1,0:T(8,128)(2,1)} %bitcast.3), calls=%async_computation | async-start | bytes 1048576 | tf_op jit(solution)/shard_map/all_to_all | solution.py:25
  115.1 15.8 %all-to-all-start.5 = ((bf16[16,16,1024]{2,1,0:T(8,128)(2,1)}), bf16[16,16,1024]{2,1,0:T(8,128)(2,1)S(1)}, u32[]{:S(2)}, u32[]{:S(2)}) async-start(bf16[16,16,1024]{2,1,0:T(8,128)(2,1)} %broadcast_in_dim.14), calls=%async_computation.5 | async-start | bytes 1048576 | tf_op jit(solution)/shard_map/all_to_all | solution.py:32
  133.8 17.2 %all-to-all-start.6 = ((bf16[16,16,1024]{2,1,0:T(8,128)(2,1)}), bf16[16,16,1024]{2,1,0:T(8,128)(2,1)S(1)}, u32[]{:S(2)}, u32[]{:S(2)}) async-start(bf16[16,16,1024]{2,1,0:T(8,128)(2,1)} %bitcast.15), calls=%async_computation.6 | async-start | bytes 1048576 | tf_op jit(solution)/shard_map/all_to_all | solution.py:25
  139.7 7.5 %collective-permute-start = (bf16[256,256]{1,0:T(8,128)(2,1)}, bf16[256,256]{1,0:T(8,128)(2,1)S(1)}, u32[]{:S(2)}, u32[]{:S(2)}) collective-permute-start(bf16[256,256]{1,0:T(8,128)(2,1)} %get-tuple-element.44), channel_id=1, source_target_pairs={{0,1},{1,2},{2,3},{3,0},{4,5},{5,6},{6,7},{7,4},{8,9},{9,10},{10,1... | collective-permute-start | bytes 393224 | tf_op jit(solution)/shard_map/ppermute | solution.py:42
  141.1 6.2 %collective-permute-start.2 = (bf16[256,256]{1,0:T(8,128)(2,1)S(1)}, bf16[256,256]{1,0:T(8,128)(2,1)S(1)}, u32[]{:S(2)}, u32[]{:S(2)}) collective-permute-start(bf16[256,256]{1,0:T(8,128)(2,1)S(1)} %get-tuple-element.45), channel_id=1, source_target_pairs={{0,3},{1,0},{2,1},{3,2},{4,7},{5,4},{6,5},{7,6},{8,11},{9,8},{10,9... | collective-permute-start | bytes 393224 | tf_op jit(solution)/shard_map/ppermute | solution.py:42
  142.4 7.6 %collective-permute-start.1 = (bf16[256,256]{1,0:T(8,128)(2,1)S(1)}, bf16[256,256]{1,0:T(8,128)(2,1)}, u32[]{:S(2)}, u32[]{:S(2)}) collective-permute-start(bf16[256,256]{1,0:T(8,128)(2,1)S(1)} %get-tuple-element.46), channel_id=1, source_target_pairs={{0,2},{1,3},{2,0},{3,1},{4,6},{5,7},{6,4},{7,5},{8,10},{9,11},{10,... | collective-permute-start | bytes 393224 | tf_op jit(solution)/shard_map/ppermute | solution.py:42
  152.0 22.0 %all-to-all-start.7 = ((bf16[16,16,1280]{2,1,0:T(8,128)(2,1)}), bf16[16,16,1280]{2,1,0:T(8,128)(2,1)S(1)}, u32[]{:S(2)}, u32[]{:S(2)}) async-start(bf16[16,16,1280]{2,1,0:T(8,128)(2,1)} %pad_maximum_fusion.2), calls=%async_computation.7 | async-start | bytes 1310720 | tf_op jit(solution)/shard_map/all_to_all | solution.py:174
  180.0 19.9 %all-to-all-start.8 = ((bf16[16,16,1280]{2,1,0:T(8,128)(2,1)}), bf16[16,16,1280]{2,1,0:T(8,128)(2,1)S(1)}, u32[]{:S(2)}, u32[]{:S(2)}) async-start(bf16[16,16,1280]{2,1,0:T(8,128)(2,1)} %pad_maximum_fusion.3), calls=%async_computation.8 | async-start | bytes 1310720 | tf_op jit(solution)/shard_map/all_to_all | solution.py:185
  200.9 16.9 %all-to-all-start.9 = ((bf16[16,16,1024]{2,1,0:T(8,128)(2,1)}), bf16[16,16,1024]{2,1,0:T(8,128)(2,1)S(1)}, u32[]{:S(2)}, u32[]{:S(2)}) async-start(bf16[16,16,1024]{2,1,0:T(8,128)(2,1)} %broadcast_in_dim.16), calls=%async_computation.9 | async-start | bytes 1048576 | tf_op jit(solution)/shard_map/all_to_all | solution.py:32
  221.9 17.4 %all-to-all-start.10 = ((bf16[16,16,1024]{2,1,0:T(8,128)(2,1)}), bf16[16,16,1024]{2,1,0:T(8,128)(2,1)S(1)}, u32[]{:S(2)}, u32[]{:S(2)}) async-start(bf16[16,16,1024]{2,1,0:T(8,128)(2,1)} %bitcast.46), calls=%async_computation.10 | async-start | bytes 1048576 | tf_op jit(solution)/shard_map/all_to_all | solution.py:25
  227.8 18.7 %collective-permute-start.8 = (bf16[2,2,64,768]{3,2,1,0:T(8,128)(2,1)}, bf16[2,2,64,768]{3,2,1,0:T(8,128)(2,1)}, u32[]{:S(2)}, u32[]{:S(2)}) collective-permute-start(bf16[2,2,64,768]{3,2,1,0:T(8,128)(2,1)} %get-tuple-element.27), channel_id=1, source_target_pairs={{0,96},{32,0},{64,32},{96,64},{1,97},{33,1},{65,33},{97,65},{2,98}... | collective-permute-start | bytes 1179656 | tf_op jit(solution)/shard_map/ppermute | solution.py:42
  229.0 19.1 %collective-permute-start.7 = (bf16[2,2,64,768]{3,2,1,0:T(8,128)(2,1)}, bf16[2,2,64,768]{3,2,1,0:T(8,128)(2,1)}, u32[]{:S(2)}, u32[]{:S(2)}) collective-permute-start(bf16[2,2,64,768]{3,2,1,0:T(8,128)(2,1)} %get-tuple-element.28), channel_id=1, source_target_pairs={{0,64},{32,96},{64,0},{96,32},{1,65},{33,97},{65,1},{97,33},{2,66}... | collective-permute-start | bytes 1179656 | tf_op jit(solution)/shard_map/ppermute | solution.py:42
  231.1 17.0 %collective-permute-start.6 = (bf16[2,2,64,768]{3,2,1,0:T(8,128)(2,1)S(1)}, bf16[2,2,64,768]{3,2,1,0:T(8,128)(2,1)}, u32[]{:S(2)}, u32[]{:S(2)}) collective-permute-start(bf16[2,2,64,768]{3,2,1,0:T(8,128)(2,1)S(1)} %get-tuple-element.29), channel_id=1, source_target_pairs={{0,32},{32,64},{64,96},{96,0},{1,33},{33,65},{65,97},{97,1},{2,34}... | collective-permute-start | bytes 1179656 | tf_op jit(solution)/shard_map/ppermute | solution.py:42
  233.2 17.3 %collective-permute-start.11 = (bf16[2,2,64,512]{3,2,1,0:T(8,128)(2,1)}, bf16[2,2,64,512]{3,2,1,0:T(8,128)(2,1)S(1)}, u32[]{:S(2)}, u32[]{:S(2)}) collective-permute-start(bf16[2,2,64,512]{3,2,1,0:T(8,128)(2,1)} %get-tuple-element.30), channel_id=1, source_target_pairs={{0,96},{32,0},{64,32},{96,64},{1,97},{33,1},{65,33},{97,65},{2,98}... | collective-permute-start | bytes 786440 | tf_op jit(solution)/shard_map/ppermute | solution.py:42
  235.9 14.7 %collective-permute-start.10 = (bf16[2,2,64,512]{3,2,1,0:T(8,128)(2,1)S(1)}, bf16[2,2,64,512]{3,2,1,0:T(8,128)(2,1)}, u32[]{:S(2)}, u32[]{:S(2)}) collective-permute-start(bf16[2,2,64,512]{3,2,1,0:T(8,128)(2,1)S(1)} %get-tuple-element.31), channel_id=1, source_target_pairs={{0,64},{32,96},{64,0},{96,32},{1,65},{33,97},{65,1},{97,33},{2,66}... | collective-permute-start | bytes 786440 | tf_op jit(solution)/shard_map/ppermute | solution.py:42
  240.2 45.1 %all-to-all-start.11 = ((bf16[16,16,1024]{2,1,0:T(8,128)(2,1)}), bf16[16,16,1024]{2,1,0:T(8,128)(2,1)S(1)}, u32[]{:S(2)}, u32[]{:S(2)}) async-start(bf16[16,16,1024]{2,1,0:T(8,128)(2,1)} %broadcast_in_dim.17), calls=%async_computation.11 | async-start | bytes 1048576 | tf_op jit(solution)/shard_map/all_to_all | solution.py:32
  246.6 6.5 %collective-permute-start.9 = (bf16[2,2,64,512]{3,2,1,0:T(8,128)(2,1)S(1)}, bf16[2,2,64,512]{3,2,1,0:T(8,128)(2,1)S(1)}, u32[]{:S(2)}, u32[]{:S(2)}) collective-permute-start(bf16[2,2,64,512]{3,2,1,0:T(8,128)(2,1)S(1)} %get-tuple-element.32), channel_id=1, source_target_pairs={{0,32},{32,64},{64,96},{96,0},{1,33},{33,65},{65,97},{97,1},{2,34}... | collective-permute-start | bytes 786440 | tf_op jit(solution)/shard_map/ppermute | solution.py:42
  255.0 42.0 %collective-permute-start.12 = (bf16[64,1280]{1,0:T(8,128)(2,1)}, bf16[64,1280]{1,0:T(8,128)(2,1)S(1)}, u32[]{:S(2)}, u32[]{:S(2)}) collective-permute-start(bf16[64,1280]{1,0:T(8,128)(2,1)} %get-tuple-element.35), channel_id=1, source_target_pairs={{0,16},{16,0},{128,144},{144,128},{1,17},{17,1},{129,145},{145,129... | collective-permute-start | bytes 491528 | tf_op jit(solution)/shard_map/ppermute | solution.py:66
  284.0 13.0 %collective-permute-start.14 = (bf16[64,1280]{1,0:T(8,128)(2,1)}, bf16[64,1280]{1,0:T(8,128)(2,1)S(1)}, u32[]{:S(2)}, u32[]{:S(2)}) collective-permute-start(bf16[64,1280]{1,0:T(8,128)(2,1)} %get-tuple-element.36), channel_id=1, source_target_pairs={{0,144},{16,128},{128,16},{144,0},{1,145},{17,129},{129,17},{145,1... | collective-permute-start | bytes 491528 | tf_op jit(solution)/shard_map/ppermute | solution.py:66
  284.0 13.1 %collective-permute-start.13 = (bf16[64,1280]{1,0:T(8,128)(2,1)S(1)}, bf16[64,1280]{1,0:T(8,128)(2,1)S(1)}, u32[]{:S(2)}, u32[]{:S(2)}) collective-permute-start(bf16[64,1280]{1,0:T(8,128)(2,1)S(1)} %get-tuple-element.37), channel_id=1, source_target_pairs={{0,128},{16,144},{128,0},{144,16},{1,129},{17,145},{129,1},{145,17... | collective-permute-start | bytes 491528 | tf_op jit(solution)/shard_map/ppermute | solution.py:66
  289.8 18.9 %all-to-all-start.12 = ((bf16[16,64,256]{2,1,0:T(8,128)(2,1)}), bf16[16,64,256]{2,1,0:T(8,128)(2,1)S(1)}, u32[]{:S(2)}, u32[]{:S(2)}) async-start(bf16[16,64,256]{2,1,0:T(8,128)(2,1)} %bitcast.53), calls=%async_computation.12 | async-start | bytes 1048576 | tf_op jit(solution)/shard_map/all_to_all | solution.py:25
  297.2 5.0 %collective-permute-start.5 = (bf16[256,256]{1,0:T(8,128)(2,1)S(1)}, bf16[256,256]{1,0:T(8,128)(2,1)S(1)}, u32[]{:S(2)}, u32[]{:S(2)}) collective-permute-start(bf16[256,256]{1,0:T(8,128)(2,1)S(1)} %bitcast.227), channel_id=1, source_target_pairs={{0,3},{1,0},{2,1},{3,2},{4,7},{5,4},{6,5},{7,6},{8,11},{9,8},{10,9... | collective-permute-start | bytes 393224 | tf_op jit(solution)/shard_map/ppermute | solution.py:42
  298.1 6.2 %collective-permute-start.4 = (bf16[256,256]{1,0:T(8,128)(2,1)S(1)}, bf16[256,256]{1,0:T(8,128)(2,1)S(1)}, u32[]{:S(2)}, u32[]{:S(2)}) collective-permute-start(bf16[256,256]{1,0:T(8,128)(2,1)S(1)} %bitcast.228), channel_id=1, source_target_pairs={{0,2},{1,3},{2,0},{3,1},{4,6},{5,7},{6,4},{7,5},{8,10},{9,11},{10,... | collective-permute-start | bytes 393224 | tf_op jit(solution)/shard_map/ppermute | solution.py:42
  299.3 8.4 %collective-permute-start.3 = (bf16[256,256]{1,0:T(8,128)(2,1)S(1)}, bf16[256,256]{1,0:T(8,128)(2,1)S(1)}, u32[]{:S(2)}, u32[]{:S(2)}) collective-permute-start(bf16[256,256]{1,0:T(8,128)(2,1)S(1)} %bitcast.229), channel_id=1, source_target_pairs={{0,1},{1,2},{2,3},{3,0},{4,5},{5,6},{6,7},{7,4},{8,9},{9,10},{10,1... | collective-permute-start | bytes 393224 | tf_op jit(solution)/shard_map/ppermute | solution.py:42
  (54 other events, 320.8 us)

commit v8 on v6

--- a/solution.py
+++ b/solution.py
@@ -11,6 +11,8 @@
 DP = ("z_lo", "y", "core")
 MP = ("z_hi", "x")
 
+
+STAGGER = 520
 
 epsilon = 1e-06
 bf16 = jnp.bfloat16
@@ -63,6 +65,12 @@
     return [pick(parts, here)] + [
         lax.ppermute(pick(parts, here ^ k), axes, [(i, i ^ k) for i in range(4)]) for k in range(1, 4)
     ]
+
+
+def later_start(tokens):
+    steps = lax.axis_index("core") * STAGGER
+    state = lax.fori_loop(0, steps, lambda _, v: jnp.tanh(v) * 1.5, tokens[:8, :128].astype(f32) * 0.25)
+    return (state[0, 0] > 4.0).astype(jnp.int32)
 
 
 def normalize(stream):
@@ -120,6 +128,7 @@
     def part(x):
         return lax.dynamic_slice_in_dim(x, start, share, 0)
 
+    lengths = lengths + later_start(tokens)
     live = (jnp.arange(SLATE)[None, :] < lengths[:, None]).astype(f32)
     triple = [triple_weight[l].reshape(width, -1) for l in range(LAYERS)]
     saved = []

time: 312 us -> 301 us (0.965)
  starting transfers between devices: 97.3 us -> 78.5 us
  blocking collectives: 77.7 us -> 65.8 us
  loops' own time: 0 us -> 11.8 us
  other arithmetic: 17.4 us -> 20.9 us
    ppermute x3, starting transfers between devices: 30.3 us -> 6.1 us  [quad_stage(): lax.ppermute(pick(parts, here ^ k), axes, [(i, i ^ k) for i in range(4)])]
    another operation x0 -> x1, loops' own time: none -> 11.8 us  [later_start(): lax.fori_loop(0, steps, lambda _, v: jnp.tanh(v) * 1.5, tokens[:8, :128]....]
    all_to_all x2, blocking collectives: 40.6 us -> 33.6 us  [all_rows(): blocks = lax.all_to_all(copies, axis, 0, 0, tiled=True)]
    ppermute x12, waiting for transfers between devices: 15.8 us -> 21.8 us  [moved(): return lax.ppermute(x, axis, [(k, (k + step) % n) for k in range(n)])]
    all_to_all x2, blocking collectives: 37.1 us -> 32.2 us  [share_rows(): blocks = lax.all_to_all(blocks, axis, 0, 0, tiled=True)]
    all_to_all x4, waiting for transfers between devices: 18.2 us -> 14.3 us  [share_rows(): blocks = lax.all_to_all(blocks, axis, 0, 0, tiled=True)]
    all_to_all x3, starting transfers between devices: 15 us -> 18.5 us  [all_rows(): blocks = lax.all_to_all(copies, axis, 0, 0, tiled=True)]
    mul x0 -> x521, other arithmetic: none -> 3.42 us  [the longest x520 2.74 us: later_start(): jnp.tanh(v) * 1.5]
  transfers between devices with their start and end apart: 24 -> 24, of which waited for: 12 -> 13; matrix products, arithmetic and copies ran while one was open for 9% -> 9% of each run, Pallas kernels for 0% -> 0%
where the time goes in v8:
time: 301 us; the launch traced here: 299 us
  waiting for transfers between devices  82.7 us (27%)
  starting transfers between devices  78.5 us (26%)
  blocking collectives  65.8 us (22%)
  other arithmetic  20.9 us (7%)
  local copies, waits for them, and re-layouts  20.5 us (7%)
  matrix products  15.6 us (5%)
  loops' own time  11.8 us (4%)
  between operations  3.28 us (1%)
    all_to_all x2, blocking collectives, all_rows(): blocks = lax.all_to_all(copies, axis, 0, 0, tiled=True)  33.6 us
    all_to_all x2, blocking collectives, share_rows(): blocks = lax.all_to_all(blocks, axis, 0, 0, tiled=True)  32.2 us
    all_to_all x4, starting transfers between devices, share_rows(): blocks = lax.all_to_all(blocks, axis, 0, 0, tiled=True)  26.1 us
    all_to_all x3, waiting for transfers between devices, all_rows(): blocks = lax.all_to_all(copies, axis, 0, 0, tiled=True)  23.9 us
    ppermute x12, waiting for transfers between devices, moved(): return lax.ppermute(x, axis, [(k, (k + step) % n) for k in range(n)])  21.8 us
    all_to_all x3, starting transfers between devices, all_rows(): blocks = lax.all_to_all(copies, axis, 0, 0, tiled=True)  18.5 us
    ppermute x12, starting transfers between devices, moved(): return lax.ppermute(x, axis, [(k, (k + step) % n) for k in range(n)])  16.5 us
    all_to_all x1, waiting for transfers between devices, step(): came = lax.all_to_all(after(sent, rscale_mid), MP, 0, 0, tiled=True)  16.2 us
  transfers between devices with their start and end apart: 24, of which 13 were waited for; matrix products, arithmetic and copies ran while one was open for 9% of the time, Pallas kernels for 0%

profile of v8, /device:TPU:1, one launch (start us, length us, event | category | flops | bytes accessed | tf_op | source)
XLA Modules:
  0.0 299.1 jit_solution(369262202346280845)
XLA Ops:
  3.3 14.5 %while.10 = (s32[]{:T(128)}, f32[8,128]{1,0:T(8,128)S(1)}, s32[]{:T(128)}, s32[]{:T(128)}) while((s32[]{:T(128)}, f32[8,128]{1,0:T(8,128)S(1)}, s32[]{:T(128)}, s32[]{:T(128)}) %tuple.63), condition=%wide.region_2.0_spmd, body=%wide.region_1.0_spmd.sunk | while | flops 1026 | bytes 8245 | solution.py:72
  22.3 11.6 %all-to-all-start = ((bf16[16,16,1024]{2,1,0:T(8,128)(2,1)}), bf16[16,16,1024]{2,1,0:T(8,128)(2,1)S(1)}, u32[]{:S(2)}, u32[]{:S(2)}) async-start(bf16[16,16,1024]{2,1,0:T(8,128)(2,1)} %bitcast.4), calls=%async_computation | async-start | bytes 1048576 | tf_op jit(solution)/shard_map/all_to_all | solution.py:25
  33.9 12.2 %all-to-all-done = bf16[16,16,1024]{2,1,0:T(8,128)(2,1)S(1)} async-done(((bf16[16,16,1024]{2,1,0:T(8,128)(2,1)}), bf16[16,16,1024]{2,1,0:T(8,128)(2,1)S(1)}, u32[]{:S(2)}, u32[]{:S(2)}) %all-to-all-start) | async-done | bytes 524320 | tf_op jit(solution)/shard_map/all_to_all | solution.py:25
  46.2 17.4 %all_to_all.65 = bf16[16,16,1024]{2,1,0:T(8,128)(2,1)S(1)} all-to-all(bf16[16,16,1024]{2,1,0:T(8,128)(2,1)S(1)} %broadcast_in_dim.12), channel_id=1, replica_groups=mesh['z_lo'=2,'y'=4,'core'=2,'z_hi'=4,'x'=4] {'z_hi','x'}, dimensions={0} | all-to-all | bytes 1048576 | tf_op jit(solution)/shard_map/all_to_all | solution.py:32
  65.2 16.3 %all_to_all.66 = bf16[16,16,1024]{2,1,0:T(8,128)(2,1)S(1)} all-to-all(bf16[16,16,1024]{2,1,0:T(8,128)(2,1)S(1)} %bitcast.224), channel_id=1, replica_groups=mesh['z_lo'=2,'y'=4,'core'=2,'z_hi'=4,'x'=4] {'z_hi','x'}, dimensions={0} | all-to-all | bytes 1048576 | tf_op jit(solution)/shard_map/all_to_all | solution.py:25
  81.7 16.2 %all_to_all.67 = bf16[16,16,1024]{2,1,0:T(8,128)(2,1)S(1)} all-to-all(bf16[16,16,1024]{2,1,0:T(8,128)(2,1)S(1)} %broadcast_in_dim.13), channel_id=1, replica_groups=mesh['z_lo'=2,'y'=4,'core'=2,'z_hi'=4,'x'=4] {'z_hi','x'}, dimensions={0} | all-to-all | bytes 1048576 | tf_op jit(solution)/shard_map/all_to_all | solution.py:32
  100.0 15.9 %all_to_all.68 = bf16[16,16,1024]{2,1,0:T(8,128)(2,1)S(1)} all-to-all(bf16[16,16,1024]{2,1,0:T(8,128)(2,1)S(1)} %bitcast.221), channel_id=1, replica_groups=mesh['z_lo'=2,'y'=4,'core'=2,'z_hi'=4,'x'=4] {'z_hi','x'}, dimensions={0} | all-to-all | bytes 1048576 | tf_op jit(solution)/shard_map/all_to_all | solution.py:25
  116.9 4.9 %all-to-all-start.5 = ((bf16[16,16,1024]{2,1,0:T(8,128)(2,1)}), bf16[16,16,1024]{2,1,0:T(8,128)(2,1)S(1)}, u32[]{:S(2)}, u32[]{:S(2)}) async-start(bf16[16,16,1024]{2,1,0:T(8,128)(2,1)} %broadcast_in_dim.14), calls=%async_computation.5 | async-start | bytes 1048576 | tf_op jit(solution)/shard_map/all_to_all | solution.py:32
  121.8 11.5 %all-to-all-done.5 = bf16[16,16,1024]{2,1,0:T(8,128)(2,1)S(1)} async-done(((bf16[16,16,1024]{2,1,0:T(8,128)(2,1)}), bf16[16,16,1024]{2,1,0:T(8,128)(2,1)S(1)}, u32[]{:S(2)}, u32[]{:S(2)}) %all-to-all-start.5) | async-done | bytes 524320 | tf_op jit(solution)/shard_map/all_to_all | solution.py:32
  136.2 4.8 %all-to-all-start.6 = ((bf16[16,16,1024]{2,1,0:T(8,128)(2,1)}), bf16[16,16,1024]{2,1,0:T(8,128)(2,1)S(1)}, u32[]{:S(2)}, u32[]{:S(2)}) async-start(bf16[16,16,1024]{2,1,0:T(8,128)(2,1)} %bitcast.16), calls=%async_computation.6 | async-start | bytes 1048576 | tf_op jit(solution)/shard_map/all_to_all | solution.py:25
  147.6 3.7 %collective-permute-done = bf16[256,256]{1,0:T(8,128)(2,1)S(1)} collective-permute-done((bf16[256,256]{1,0:T(8,128)(2,1)}, bf16[256,256]{1,0:T(8,128)(2,1)S(1)}, u32[]{:S(2)}, u32[]{:S(2)}) %collective-permute-start) | collective-permute-done | bytes 131104 | tf_op jit(solution)/shard_map/ppermute | solution.py:42
  155.8 6.3 %all-to-all-start.7 = ((bf16[16,16,1280]{2,1,0:T(8,128)(2,1)}), bf16[16,16,1280]{2,1,0:T(8,128)(2,1)S(1)}, u32[]{:S(2)}, u32[]{:S(2)}) async-start(bf16[16,16,1280]{2,1,0:T(8,128)(2,1)} %pad_maximum_fusion.2), calls=%async_computation.7 | async-start | bytes 1310720 | tf_op jit(solution)/shard_map/all_to_all | solution.py:174
  163.3 16.2 %all-to-all-done.7 = bf16[16,16,1280]{2,1,0:T(8,128)(2,1)S(1)} async-done(((bf16[16,16,1280]{2,1,0:T(8,128)(2,1)}), bf16[16,16,1280]{2,1,0:T(8,128)(2,1)S(1)}, u32[]{:S(2)}, u32[]{:S(2)}) %all-to-all-start.7) | async-done | bytes 655392 | tf_op jit(solution)/shard_map/all_to_all | solution.py:174
  185.4 4.9 %all-to-all-start.8 = ((bf16[16,16,1280]{2,1,0:T(8,128)(2,1)}), bf16[16,16,1280]{2,1,0:T(8,128)(2,1)S(1)}, u32[]{:S(2)}, u32[]{:S(2)}) async-start(bf16[16,16,1280]{2,1,0:T(8,128)(2,1)} %pad_maximum_fusion.3), calls=%async_computation.8 | async-start | bytes 1310720 | tf_op jit(solution)/shard_map/all_to_all | solution.py:185
  199.5 6.4 %all-to-all-done.8 = bf16[16,16,1280]{2,1,0:T(8,128)(2,1)S(1)} async-done(((bf16[16,16,1280]{2,1,0:T(8,128)(2,1)}), bf16[16,16,1280]{2,1,0:T(8,128)(2,1)S(1)}, u32[]{:S(2)}, u32[]{:S(2)}) %all-to-all-start.8) | async-done | bytes 655392 | tf_op jit(solution)/shard_map/all_to_all | solution.py:185
  206.9 6.7 %all-to-all-start.9 = ((bf16[16,16,1024]{2,1,0:T(8,128)(2,1)}), bf16[16,16,1024]{2,1,0:T(8,128)(2,1)S(1)}, u32[]{:S(2)}, u32[]{:S(2)}) async-start(bf16[16,16,1024]{2,1,0:T(8,128)(2,1)} %broadcast_in_dim.16), calls=%async_computation.9 | async-start | bytes 1048576 | tf_op jit(solution)/shard_map/all_to_all | solution.py:32
  213.8 12.4 %all-to-all-done.9 = bf16[16,16,1024]{2,1,0:T(8,128)(2,1)S(1)} async-done(((bf16[16,16,1024]{2,1,0:T(8,128)(2,1)}), bf16[16,16,1024]{2,1,0:T(8,128)(2,1)S(1)}, u32[]{:S(2)}, u32[]{:S(2)}) %all-to-all-start.9) | async-done | bytes 524320 | tf_op jit(solution)/shard_map/all_to_all | solution.py:32
  230.4 5.6 %all-to-all-start.10 = ((bf16[16,16,1024]{2,1,0:T(8,128)(2,1)}), bf16[16,16,1024]{2,1,0:T(8,128)(2,1)S(1)}, u32[]{:S(2)}, u32[]{:S(2)}) async-start(bf16[16,16,1024]{2,1,0:T(8,128)(2,1)} %bitcast.47), calls=%async_computation.10 | async-start | bytes 1048576 | tf_op jit(solution)/shard_map/all_to_all | solution.py:25
  248.6 7.0 %all-to-all-start.11 = ((bf16[16,16,1024]{2,1,0:T(8,128)(2,1)}), bf16[16,16,1024]{2,1,0:T(8,128)(2,1)S(1)}, u32[]{:S(2)}, u32[]{:S(2)}) async-start(bf16[16,16,1024]{2,1,0:T(8,128)(2,1)} %broadcast_in_dim.17), calls=%async_computation.11 | async-start | bytes 1048576 | tf_op jit(solution)/shard_map/all_to_all | solution.py:32
  256.7 5.9 %collective-permute-done.6 = bf16[2,2,64,768]{3,2,1,0:T(8,128)(2,1)} collective-permute-done((bf16[2,2,64,768]{3,2,1,0:T(8,128)(2,1)S(1)}, bf16[2,2,64,768]{3,2,1,0:T(8,128)(2,1)}, u32[]{:S(2)}, u32[]{:S(2)}) %collective-permute-start.6) | collective-permute-done | bytes 393248 | tf_op jit(solution)/shard_map/ppermute | solution.py:42
  269.1 4.7 %collective-permute-start.12 = (bf16[64,1280]{1,0:T(8,128)(2,1)}, bf16[64,1280]{1,0:T(8,128)(2,1)S(1)}, u32[]{:S(2)}, u32[]{:S(2)}) collective-permute-start(bf16[64,1280]{1,0:T(8,128)(2,1)} %get-tuple-element.54), channel_id=1, source_target_pairs={{0,16},{16,0},{128,144},{144,128},{1,17},{17,1},{129,145},{145,129... | collective-permute-start | bytes 491528 | tf_op jit(solution)/shard_map/ppermute | solution.py:66
  279.7 4.1 %all-to-all-start.12 = ((bf16[16,64,256]{2,1,0:T(8,128)(2,1)}), bf16[16,64,256]{2,1,0:T(8,128)(2,1)S(1)}, u32[]{:S(2)}, u32[]{:S(2)}) async-start(bf16[16,64,256]{2,1,0:T(8,128)(2,1)} %bitcast.54), calls=%async_computation.12 | async-start | bytes 1048576 | tf_op jit(solution)/shard_map/all_to_all | solution.py:25
  288.7 3.2 %collective-permute-done.5 = bf16[256,256]{1,0:T(8,128)(2,1)S(1)} collective-permute-done((bf16[256,256]{1,0:T(8,128)(2,1)S(1)}, bf16[256,256]{1,0:T(8,128)(2,1)S(1)}, u32[]{:S(2)}, u32[]{:S(2)}) %collective-permute-start.5) | collective-permute-done | bytes 131104 | tf_op jit(solution)/shard_map/ppermute | solution.py:42
  292.7 3.7 %collective-permute-done.3 = bf16[256,256]{1,0:T(8,128)(2,1)S(1)} collective-permute-done((bf16[256,256]{1,0:T(8,128)(2,1)S(1)}, bf16[256,256]{1,0:T(8,128)(2,1)S(1)}, u32[]{:S(2)}, u32[]{:S(2)}) %collective-permute-start.3) | collective-permute-done | bytes 131104 | tf_op jit(solution)/shard_map/ppermute | solution.py:42
  (782 shorter events, 82.3 us)
Async XLA Ops:
  22.3 23.8 %all-to-all-start = ((bf16[16,16,1024]{2,1,0:T(8,128)(2,1)}), bf16[16,16,1024]{2,1,0:T(8,128)(2,1)S(1)}, u32[]{:S(2)}, u32[]{:S(2)}) async-start(bf16[16,16,1024]{2,1,0:T(8,128)(2,1)} %bitcast.4), calls=%async_computation | async-start | bytes 1048576 | tf_op jit(solution)/shard_map/all_to_all | solution.py:25
  116.9 16.5 %all-to-all-start.5 = ((bf16[16,16,1024]{2,1,0:T(8,128)(2,1)}), bf16[16,16,1024]{2,1,0:T(8,128)(2,1)S(1)}, u32[]{:S(2)}, u32[]{:S(2)}) async-start(bf16[16,16,1024]{2,1,0:T(8,128)(2,1)} %broadcast_in_dim.14), calls=%async_computation.5 | async-start | bytes 1048576 | tf_op jit(solution)/shard_map/all_to_all | solution.py:32
  136.2 18.5 %all-to-all-start.6 = ((bf16[16,16,1024]{2,1,0:T(8,128)(2,1)}), bf16[16,16,1024]{2,1,0:T(8,128)(2,1)S(1)}, u32[]{:S(2)}, u32[]{:S(2)}) async-start(bf16[16,16,1024]{2,1,0:T(8,128)(2,1)} %bitcast.16), calls=%async_computation.6 | async-start | bytes 1048576 | tf_op jit(solution)/shard_map/all_to_all | solution.py:25
  143.3 8.1 %collective-permute-start = (bf16[256,256]{1,0:T(8,128)(2,1)}, bf16[256,256]{1,0:T(8,128)(2,1)S(1)}, u32[]{:S(2)}, u32[]{:S(2)}) collective-permute-start(bf16[256,256]{1,0:T(8,128)(2,1)} %get-tuple-element.63), channel_id=1, source_target_pairs={{0,1},{1,2},{2,3},{3,0},{4,5},{5,6},{6,7},{7,4},{8,9},{9,10},{10,1... | collective-permute-start | bytes 393224 | tf_op jit(solution)/shard_map/ppermute | solution.py:42
  144.6 6.7 %collective-permute-start.2 = (bf16[256,256]{1,0:T(8,128)(2,1)S(1)}, bf16[256,256]{1,0:T(8,128)(2,1)S(1)}, u32[]{:S(2)}, u32[]{:S(2)}) collective-permute-start(bf16[256,256]{1,0:T(8,128)(2,1)S(1)} %get-tuple-element.64), channel_id=1, source_target_pairs={{0,3},{1,0},{2,1},{3,2},{4,7},{5,4},{6,5},{7,6},{8,11},{9,8},{10,9... | collective-permute-start | bytes 393224 | tf_op jit(solution)/shard_map/ppermute | solution.py:42
  145.9 7.8 %collective-permute-start.1 = (bf16[256,256]{1,0:T(8,128)(2,1)S(1)}, bf16[256,256]{1,0:T(8,128)(2,1)}, u32[]{:S(2)}, u32[]{:S(2)}) collective-permute-start(bf16[256,256]{1,0:T(8,128)(2,1)S(1)} %get-tuple-element.65), channel_id=1, source_target_pairs={{0,2},{1,3},{2,0},{3,1},{4,6},{5,7},{6,4},{7,5},{8,10},{9,11},{10,... | collective-permute-start | bytes 393224 | tf_op jit(solution)/shard_map/ppermute | solution.py:42
  155.8 23.7 %all-to-all-start.7 = ((bf16[16,16,1280]{2,1,0:T(8,128)(2,1)}), bf16[16,16,1280]{2,1,0:T(8,128)(2,1)S(1)}, u32[]{:S(2)}, u32[]{:S(2)}) async-start(bf16[16,16,1280]{2,1,0:T(8,128)(2,1)} %pad_maximum_fusion.2), calls=%async_computation.7 | async-start | bytes 1310720 | tf_op jit(solution)/shard_map/all_to_all | solution.py:174
  185.4 20.5 %all-to-all-start.8 = ((bf16[16,16,1280]{2,1,0:T(8,128)(2,1)}), bf16[16,16,1280]{2,1,0:T(8,128)(2,1)S(1)}, u32[]{:S(2)}, u32[]{:S(2)}) async-start(bf16[16,16,1280]{2,1,0:T(8,128)(2,1)} %pad_maximum_fusion.3), calls=%async_computation.8 | async-start | bytes 1310720 | tf_op jit(solution)/shard_map/all_to_all | solution.py:185
  206.9 19.3 %all-to-all-start.9 = ((bf16[16,16,1024]{2,1,0:T(8,128)(2,1)}), bf16[16,16,1024]{2,1,0:T(8,128)(2,1)S(1)}, u32[]{:S(2)}, u32[]{:S(2)}) async-start(bf16[16,16,1024]{2,1,0:T(8,128)(2,1)} %broadcast_in_dim.16), calls=%async_computation.9 | async-start | bytes 1048576 | tf_op jit(solution)/shard_map/all_to_all | solution.py:32
  230.4 17.2 %all-to-all-start.10 = ((bf16[16,16,1024]{2,1,0:T(8,128)(2,1)}), bf16[16,16,1024]{2,1,0:T(8,128)(2,1)S(1)}, u32[]{:S(2)}, u32[]{:S(2)}) async-start(bf16[16,16,1024]{2,1,0:T(8,128)(2,1)} %bitcast.47), calls=%async_computation.10 | async-start | bytes 1048576 | tf_op jit(solution)/shard_map/all_to_all | solution.py:25
  236.2 19.3 %collective-permute-start.8 = (bf16[2,2,64,768]{3,2,1,0:T(8,128)(2,1)}, bf16[2,2,64,768]{3,2,1,0:T(8,128)(2,1)}, u32[]{:S(2)}, u32[]{:S(2)}) collective-permute-start(bf16[2,2,64,768]{3,2,1,0:T(8,128)(2,1)} %get-tuple-element.46), channel_id=1, source_target_pairs={{0,96},{32,0},{64,32},{96,64},{1,97},{33,1},{65,33},{97,65},{2,98}... | collective-permute-start | bytes 1179656 | tf_op jit(solution)/shard_map/ppermute | solution.py:42
  239.0 17.7 %collective-permute-start.7 = (bf16[2,2,64,768]{3,2,1,0:T(8,128)(2,1)}, bf16[2,2,64,768]{3,2,1,0:T(8,128)(2,1)}, u32[]{:S(2)}, u32[]{:S(2)}) collective-permute-start(bf16[2,2,64,768]{3,2,1,0:T(8,128)(2,1)} %get-tuple-element.47), channel_id=1, source_target_pairs={{0,64},{32,96},{64,0},{96,32},{1,65},{33,97},{65,1},{97,33},{2,66}... | collective-permute-start | bytes 1179656 | tf_op jit(solution)/shard_map/ppermute | solution.py:42
  239.3 23.3 %collective-permute-start.6 = (bf16[2,2,64,768]{3,2,1,0:T(8,128)(2,1)S(1)}, bf16[2,2,64,768]{3,2,1,0:T(8,128)(2,1)}, u32[]{:S(2)}, u32[]{:S(2)}) collective-permute-start(bf16[2,2,64,768]{3,2,1,0:T(8,128)(2,1)S(1)} %get-tuple-element.48), channel_id=1, source_target_pairs={{0,32},{32,64},{64,96},{96,0},{1,33},{33,65},{65,97},{97,1},{2,34}... | collective-permute-start | bytes 1179656 | tf_op jit(solution)/shard_map/ppermute | solution.py:42
  242.1 23.0 %collective-permute-start.11 = (bf16[2,2,64,512]{3,2,1,0:T(8,128)(2,1)}, bf16[2,2,64,512]{3,2,1,0:T(8,128)(2,1)S(1)}, u32[]{:S(2)}, u32[]{:S(2)}) collective-permute-start(bf16[2,2,64,512]{3,2,1,0:T(8,128)(2,1)} %get-tuple-element.49), channel_id=1, source_target_pairs={{0,96},{32,0},{64,32},{96,64},{1,97},{33,1},{65,33},{97,65},{2,98}... | collective-permute-start | bytes 786440 | tf_op jit(solution)/shard_map/ppermute | solution.py:42
  244.1 21.0 %collective-permute-start.10 = (bf16[2,2,64,512]{3,2,1,0:T(8,128)(2,1)S(1)}, bf16[2,2,64,512]{3,2,1,0:T(8,128)(2,1)}, u32[]{:S(2)}, u32[]{:S(2)}) collective-permute-start(bf16[2,2,64,512]{3,2,1,0:T(8,128)(2,1)S(1)} %get-tuple-element.50), channel_id=1, source_target_pairs={{0,64},{32,96},{64,0},{96,32},{1,65},{33,97},{65,1},{97,33},{2,66}... | collective-permute-start | bytes 786440 | tf_op jit(solution)/shard_map/ppermute | solution.py:42
  248.6 26.6 %all-to-all-start.11 = ((bf16[16,16,1024]{2,1,0:T(8,128)(2,1)}), bf16[16,16,1024]{2,1,0:T(8,128)(2,1)S(1)}, u32[]{:S(2)}, u32[]{:S(2)}) async-start(bf16[16,16,1024]{2,1,0:T(8,128)(2,1)} %broadcast_in_dim.17), calls=%async_computation.11 | async-start | bytes 1048576 | tf_op jit(solution)/shard_map/all_to_all | solution.py:32
  255.5 11.6 %collective-permute-start.9 = (bf16[2,2,64,512]{3,2,1,0:T(8,128)(2,1)S(1)}, bf16[2,2,64,512]{3,2,1,0:T(8,128)(2,1)S(1)}, u32[]{:S(2)}, u32[]{:S(2)}) collective-permute-start(bf16[2,2,64,512]{3,2,1,0:T(8,128)(2,1)S(1)} %get-tuple-element.51), channel_id=1, source_target_pairs={{0,32},{32,64},{64,96},{96,0},{1,33},{33,65},{65,97},{97,1},{2,34}... | collective-permute-start | bytes 786440 | tf_op jit(solution)/shard_map/ppermute | solution.py:42
  269.1 14.8 %collective-permute-start.12 = (bf16[64,1280]{1,0:T(8,128)(2,1)}, bf16[64,1280]{1,0:T(8,128)(2,1)S(1)}, u32[]{:S(2)}, u32[]{:S(2)}) collective-permute-start(bf16[64,1280]{1,0:T(8,128)(2,1)} %get-tuple-element.54), channel_id=1, source_target_pairs={{0,16},{16,0},{128,144},{144,128},{1,17},{17,1},{129,145},{145,129... | collective-permute-start | bytes 491528 | tf_op jit(solution)/shard_map/ppermute | solution.py:66
  273.8 10.1 %collective-permute-start.14 = (bf16[64,1280]{1,0:T(8,128)(2,1)}, bf16[64,1280]{1,0:T(8,128)(2,1)S(1)}, u32[]{:S(2)}, u32[]{:S(2)}) collective-permute-start(bf16[64,1280]{1,0:T(8,128)(2,1)} %get-tuple-element.55), channel_id=1, source_target_pairs={{0,144},{16,128},{128,16},{144,0},{1,145},{17,129},{129,17},{145,1... | collective-permute-start | bytes 491528 | tf_op jit(solution)/shard_map/ppermute | solution.py:66
  273.9 10.1 %collective-permute-start.13 = (bf16[64,1280]{1,0:T(8,128)(2,1)S(1)}, bf16[64,1280]{1,0:T(8,128)(2,1)S(1)}, u32[]{:S(2)}, u32[]{:S(2)}) collective-permute-start(bf16[64,1280]{1,0:T(8,128)(2,1)S(1)} %get-tuple-element.56), channel_id=1, source_target_pairs={{0,128},{16,144},{128,0},{144,16},{1,129},{17,145},{129,1},{145,17... | collective-permute-start | bytes 491528 | tf_op jit(solution)/shard_map/ppermute | solution.py:66
  279.7 17.6 %all-to-all-start.12 = ((bf16[16,64,256]{2,1,0:T(8,128)(2,1)}), bf16[16,64,256]{2,1,0:T(8,128)(2,1)S(1)}, u32[]{:S(2)}, u32[]{:S(2)}) async-start(bf16[16,64,256]{2,1,0:T(8,128)(2,1)} %bitcast.54), calls=%async_computation.12 | async-start | bytes 1048576 | tf_op jit(solution)/shard_map/all_to_all | solution.py:25
  284.0 7.9 %collective-permute-start.5 = (bf16[256,256]{1,0:T(8,128)(2,1)S(1)}, bf16[256,256]{1,0:T(8,128)(2,1)S(1)}, u32[]{:S(2)}, u32[]{:S(2)}) collective-permute-start(bf16[256,256]{1,0:T(8,128)(2,1)S(1)} %bitcast.227), channel_id=1, source_target_pairs={{0,3},{1,0},{2,1},{3,2},{4,7},{5,4},{6,5},{7,6},{8,11},{9,8},{10,9... | collective-permute-start | bytes 393224 | tf_op jit(solution)/shard_map/ppermute | solution.py:42
  286.7 6.1 %collective-permute-start.4 = (bf16[256,256]{1,0:T(8,128)(2,1)S(1)}, bf16[256,256]{1,0:T(8,128)(2,1)S(1)}, u32[]{:S(2)}, u32[]{:S(2)}) collective-permute-start(bf16[256,256]{1,0:T(8,128)(2,1)S(1)} %bitcast.228), channel_id=1, source_target_pairs={{0,2},{1,3},{2,0},{3,1},{4,6},{5,7},{6,4},{7,5},{8,10},{9,11},{10,... | collective-permute-start | bytes 393224 | tf_op jit(solution)/shard_map/ppermute | solution.py:42
  287.3 9.2 %collective-permute-start.3 = (bf16[256,256]{1,0:T(8,128)(2,1)S(1)}, bf16[256,256]{1,0:T(8,128)(2,1)S(1)}, u32[]{:S(2)}, u32[]{:S(2)}) collective-permute-start(bf16[256,256]{1,0:T(8,128)(2,1)S(1)} %bitcast.229), channel_id=1, source_target_pairs={{0,1},{1,2},{2,3},{3,0},{4,5},{5,6},{6,7},{7,4},{8,9},{9,10},{10,1... | collective-permute-start | bytes 393224 | tf_op jit(solution)/shard_map/ppermute | solution.py:42
  (54 other events, 302.7 us)
